TPU v7x, 32 devices: a whole 2x2x4 slice. The times are simulated.
32 devices in a mesh: rows: 2 (over core), cols: 4 (over y, x), slabs: 4 (over z).
Axes of the slice: x: 2, y: 2, z: 4, core: 2. Of those that a mesh axis runs over, the one named last changes fastest.
Arguments:
- tracer: float32 [8, 256, 384, 128], P('rows', 'cols', 'slabs'), may hold values from 0.2 to 1.8
- crowding: float32 [8, 256, 384, 128], P('rows', 'cols', 'slabs'), may hold values from 0.5 to 2
Outputs:
- tracer_end: float32 [8, 256, 384, 128], P('rows', 'cols', 'slabs')
All inputs are finite; a program needn't handle non-finite values.
Results may differ from a plain program's by a relative error of at most 0.00002.
Values sent between devices are 32-bit elements.
No kernel may reach another device: no remote copies, remote signals or barrier semaphores. Data moves between devices by JAX's collectives and lax.ppermute only.
A program may use at most 448 MiB of HBM per device.

v0:
```python
import jax
import jax.numpy as jnp
from jax import lax
from jax.sharding import PartitionSpec as P

STEPS = 4


def with_halo(block, sides, width):
    for axis, dim in sides:
        count = lax.axis_size(axis)
        forward = [(i, i + 1) for i in range(count - 1)]
        backward = [(target, source) for source, target in forward]
        low = lax.ppermute(
            lax.slice_in_dim(block, block.shape[dim] - width, None, axis=dim), axis, forward
        )
        high = lax.ppermute(lax.slice_in_dim(block, 0, width, axis=dim), axis, backward)
        block = jnp.concatenate([low, block, high], axis=dim)
    return block


def inner_cells(values, dims):
    for dim in dims:
        values = lax.slice_in_dim(values, 1, values.shape[dim] - 1, axis=dim)
    return values


def side_cells(values, dim, start, dims):
    others = [other for other in dims if other != dim]
    values = inner_cells(values, others)
    return lax.slice_in_dim(values, start, start + values.shape[dim] - 2, axis=dim)


def advance(padded, crowding):
    middle = inner_cells(padded, (0, 1, 2))
    lower = [side_cells(padded, dim, 0, (0, 1, 2)) for dim in (0, 1, 2)]
    upper = [side_cells(padded, dim, 2, (0, 1, 2)) for dim in (0, 1, 2)]
    spread = lower[0] + upper[0] + lower[1] + upper[1] + lower[2] + upper[2] - 6.0 * middle
    return middle + 0.1 * spread + 0.2 * middle * (1.0 - middle * crowding)


def on_device(tracer, crowding):
    for step in range(STEPS):
        padded = with_halo(tracer, (("rows", 0), ("cols", 1), ("slabs", 2)), 1)
        tracer = advance(padded, crowding)
    return tracer


def solution(mesh):
    placed = (P("rows", "cols", "slabs", None), P("rows", "cols", "slabs", None))
    return jax.shard_map(
        on_device,
        mesh=mesh,
        in_specs=placed,
        out_specs=P("rows", "cols", "slabs", None),
        check_vma=False,
    )
```

profile of v0, /device:TPU:13, one launch (start us, length us, event | category | flops | bytes accessed | tf_op | source)
XLA Modules:
  0.0 355.6 jit_solution(10264535121621644159)
XLA Ops:
  0.0 5.0 %fusion.40 = (f32[1,64,96,128]{3,2,1,0:T(8,128)}, f32[1,64,96,128]{3,2,1,0:T(8,128)S(1)}) fusion(f32[4,64,96,128]{3,2,1,0:T(8,128)} %param.2), kind=kLoop, calls=%fused_computation.134 | loop fusion | bytes 12582912 | tf_op jit(solution)/shard_map/slice | solution.py:17
  6.2 3.4 collective-permute-start.1
  9.7 2.8 collective-permute-done
  14.3 10.3 %constant_dynamic-update-slice_fusion.1 = f32[6,64,96,128]{3,2,1,0:T(8,128)} fusion(f32[6,64,96,128]{3,2,1,0:T(8,128)} %constant_dynamic-update-slice_fusion.2, f32[4,64,96,128]{3,2,1,0:T(8,128)} %param.2), kind=kLoop, calls=%fused_computation.128 | loop fusion | bytes 25165824
  27.8 3.1 collective-permute-start.2
  31.0 3.1 collective-permute-start.3
  34.0 5.0 %collective-permute-done.2 = f32[6,1,96,128]{3,2,1,0:T(8,128)S(1)} collective-permute-done((f32[6,1,96,128]{3,2,1,0:T(8,128)S(1)}, f32[6,1,96,128]{3,2,1,0:T(8,128)S(1)}, u32[]{:S(2)}, u32[]{:S(2)}) %collective-permute-start.2) | collective-permute-done | bytes 294944 | tf_op jit(solution)/shard_map/ppermute | solution.py:14
  39.1 4.4 %collective-permute-done.3 = f32[6,1,96,128]{3,2,1,0:T(8,128)S(1)} collective-permute-done((f32[6,1,96,128]{3,2,1,0:T(8,128)S(1)}, f32[6,1,96,128]{3,2,1,0:T(8,128)S(1)}, u32[]{:S(2)}, u32[]{:S(2)}) %collective-permute-start.3) | collective-permute-done | bytes 294944 | tf_op jit(solution)/shard_map/ppermute | solution.py:17
  48.0 3.2 collective-permute-start.4
  56.5 42.2 %fusion.31 = f32[4,64,96,128]{3,2,1,0:T(8,128)} fusion(f32[4,64,96,128]{3,2,1,0:T(8,128)} %param.2, f32[6,66,1,128]{3,2,1,0:T(1,128)} %copy.20, f32[6,1,96,128]{3,2,1,0:T(8,128)} %copy-done.7, f32[6,64,96,128]{3,2,1,0:T(8,128)} %constant_dynamic-update-slice_fusion, f32[6,1,96,128]{3,2,1,0:T(8,128)S(1)} %collective-permute-done.2, ...), kind=kLoop, calls=%fused_computation.86 | loop fusion | flops 75497472 | bytes 63909888 | tf_op jit(solution)/shard_map/add | solution.py:39
  98.7 3.4 fusion.39
  103.7 4.6 %collective-permute-start.7 = (f32[1,64,96,128]{3,2,1,0:T(8,128)S(1)}, f32[1,64,96,128]{3,2,1,0:T(8,128)S(1)}, u32[]{:S(2)}, u32[]{:S(2)}) collective-permute-start(f32[1,64,96,128]{3,2,1,0:T(8,128)S(1)} %get-tuple-element.26), channel_id=1, source_target_pairs={{16,0},{17,1},{18,2},{19,3},{20,4},{21,5},{22,6},{23,7},{24,8},{25... | collective-permute-start | bytes 9437192 | tf_op jit(solution)/shard_map/ppermute | solution.py:17
  108.3 2.7 collective-permute-done.6
  115.4 5.0 %collective-permute-start.9 = (f32[6,1,96,128]{3,2,1,0:T(8,128)S(1)}, f32[6,1,96,128]{3,2,1,0:T(8,128)S(1)}, u32[]{:S(2)}, u32[]{:S(2)}) collective-permute-start(f32[6,1,96,128]{3,2,1,0:T(8,128)S(1)} %get-tuple-element.18), channel_id=1, source_target_pairs={{4,0},{8,4},{12,8},{5,1},{9,5},{13,9},{6,2},{10,6},{14,10},{7,3},{... | collective-permute-start | bytes 884744 | tf_op jit(solution)/shard_map/ppermute | solution.py:17
  120.4 5.1 %collective-permute-done.8 = f32[6,1,96,128]{3,2,1,0:T(8,128)S(1)} collective-permute-done((f32[6,1,96,128]{3,2,1,0:T(8,128)S(1)}, f32[6,1,96,128]{3,2,1,0:T(8,128)S(1)}, u32[]{:S(2)}, u32[]{:S(2)}) %collective-permute-start.8) | collective-permute-done | bytes 294944 | tf_op jit(solution)/shard_map/ppermute | solution.py:14
  130.6 3.5 collective-permute-start.10
  139.4 45.2 %fusion.22 = f32[4,64,96,128]{3,2,1,0:T(8,128)} fusion(f32[4,64,96,128]{3,2,1,0:T(8,128)} %fusion.31, f32[6,66,1,128]{3,2,1,0:T(1,128)} %copy.24, f32[6,1,96,128]{3,2,1,0:T(8,128)} %copy-done.8, f32[6,1,96,128]{3,2,1,0:T(8,128)S(1)} %collective-permute-done.8, f32[1,64,96,128]{3,2,1,0:T(8,128)} %copy-done.3, ...), kind=kLoop, calls=%fused_computation.59 | loop fusion | flops 100663296 | bytes 45035520 | tf_op jit(solution)/shard_map/add | solution.py:39
  184.6 3.4 fusion.38
  189.7 4.2 %collective-permute-start.13 = (f32[1,64,96,128]{3,2,1,0:T(8,128)S(1)}, f32[1,64,96,128]{3,2,1,0:T(8,128)S(1)}, u32[]{:S(2)}, u32[]{:S(2)}) collective-permute-start(f32[1,64,96,128]{3,2,1,0:T(8,128)S(1)} %get-tuple-element.24), channel_id=1, source_target_pairs={{16,0},{17,1},{18,2},{19,3},{20,4},{21,5},{22,6},{23,7},{24,8},{25... | collective-permute-start | bytes 9437192 | tf_op jit(solution)/shard_map/ppermute | solution.py:17
  193.9 2.7 collective-permute-done.12
  201.0 5.0 %collective-permute-start.15 = (f32[6,1,96,128]{3,2,1,0:T(8,128)S(1)}, f32[6,1,96,128]{3,2,1,0:T(8,128)S(1)}, u32[]{:S(2)}, u32[]{:S(2)}) collective-permute-start(f32[6,1,96,128]{3,2,1,0:T(8,128)S(1)} %get-tuple-element.16), channel_id=1, source_target_pairs={{4,0},{8,4},{12,8},{5,1},{9,5},{13,9},{6,2},{10,6},{14,10},{7,3},{... | collective-permute-start | bytes 884744 | tf_op jit(solution)/shard_map/ppermute | solution.py:17
  206.0 5.1 %collective-permute-done.14 = f32[6,1,96,128]{3,2,1,0:T(8,128)S(1)} collective-permute-done((f32[6,1,96,128]{3,2,1,0:T(8,128)S(1)}, f32[6,1,96,128]{3,2,1,0:T(8,128)S(1)}, u32[]{:S(2)}, u32[]{:S(2)}) %collective-permute-start.14) | collective-permute-done | bytes 294944 | tf_op jit(solution)/shard_map/ppermute | solution.py:14
  216.2 3.4 collective-permute-start.16
  219.6 2.6 collective-permute-done.17
  225.1 44.5 %fusion.13 = f32[4,64,96,128]{3,2,1,0:T(8,128)} fusion(f32[4,64,96,128]{3,2,1,0:T(8,128)} %fusion.22, f32[6,66,1,128]{3,2,1,0:T(1,128)} %copy.28, f32[6,1,96,128]{3,2,1,0:T(8,128)} %copy-done.9, f32[6,1,96,128]{3,2,1,0:T(8,128)S(1)} %collective-permute-done.14, f32[1,64,96,128]{3,2,1,0:T(8,128)} %copy-done.4, ...), kind=kLoop, calls=%fused_computation.32 | loop fusion | flops 100663296 | bytes 45035520 | tf_op jit(solution)/shard_map/add | solution.py:39
  269.6 3.4 fusion.37
  274.6 4.5 %collective-permute-start.19 = (f32[1,64,96,128]{3,2,1,0:T(8,128)S(1)}, f32[1,64,96,128]{3,2,1,0:T(8,128)S(1)}, u32[]{:S(2)}, u32[]{:S(2)}) collective-permute-start(f32[1,64,96,128]{3,2,1,0:T(8,128)S(1)} %get-tuple-element.22), channel_id=1, source_target_pairs={{16,0},{17,1},{18,2},{19,3},{20,4},{21,5},{22,6},{23,7},{24,8},{25... | collective-permute-start | bytes 9437192 | tf_op jit(solution)/shard_map/ppermute | solution.py:17
  285.9 5.0 %collective-permute-start.21 = (f32[6,1,96,128]{3,2,1,0:T(8,128)S(1)}, f32[6,1,96,128]{3,2,1,0:T(8,128)S(1)}, u32[]{:S(2)}, u32[]{:S(2)}) collective-permute-start(f32[6,1,96,128]{3,2,1,0:T(8,128)S(1)} %get-tuple-element.14), channel_id=1, source_target_pairs={{4,0},{8,4},{12,8},{5,1},{9,5},{13,9},{6,2},{10,6},{14,10},{7,3},{... | collective-permute-start | bytes 884744 | tf_op jit(solution)/shard_map/ppermute | solution.py:17
  290.9 5.1 %collective-permute-done.20 = f32[6,1,96,128]{3,2,1,0:T(8,128)S(1)} collective-permute-done((f32[6,1,96,128]{3,2,1,0:T(8,128)S(1)}, f32[6,1,96,128]{3,2,1,0:T(8,128)S(1)}, u32[]{:S(2)}, u32[]{:S(2)}) %collective-permute-start.20) | collective-permute-done | bytes 294944 | tf_op jit(solution)/shard_map/ppermute | solution.py:14
  301.2 3.4 collective-permute-start.22
  304.5 2.6 collective-permute-done.23
  310.0 45.4 %fusion.4 = f32[4,64,96,128]{3,2,1,0:T(8,128)} fusion(f32[4,64,96,128]{3,2,1,0:T(8,128)} %fusion.13, f32[6,66,1,128]{3,2,1,0:T(1,128)} %copy.32, f32[6,1,96,128]{3,2,1,0:T(8,128)} %copy-done.10, f32[6,1,96,128]{3,2,1,0:T(8,128)S(1)} %collective-permute-done.20, f32[1,64,96,128]{3,2,1,0:T(8,128)} %copy-done.5, ...), kind=kLoop, calls=%fused_computation.5 | loop fusion | flops 100663296 | bytes 45035520 | tf_op jit(solution)/shard_map/add | solution.py:39
  (73 shorter events, 62.6 us)
Async XLA Ops:
  5.0 7.5 %collective-permute-start = (f32[1,64,96,128]{3,2,1,0:T(8,128)S(1)}, f32[1,64,96,128]{3,2,1,0:T(8,128)S(1)}, u32[]{:S(2)}, u32[]{:S(2)}) collective-permute-start(f32[1,64,96,128]{3,2,1,0:T(8,128)S(1)} %get-tuple-element.28), channel_id=1, source_target_pairs={{0,16},{1,17},{2,18},{3,19},{4,20},{5,21},{6,22},{7,23},{8,24},{9,... | collective-permute-start | bytes 9437192 | tf_op jit(solution)/shard_map/ppermute | solution.py:14
  6.2 18.4 %collective-permute-start.1 = (f32[1,64,96,128]{3,2,1,0:T(8,128)}, f32[1,64,96,128]{3,2,1,0:T(8,128)S(1)}, u32[]{:S(2)}, u32[]{:S(2)}) collective-permute-start(f32[1,64,96,128]{3,2,1,0:T(8,128)} %get-tuple-element.27), channel_id=1, source_target_pairs={{16,0},{17,1},{18,2},{19,3},{20,4},{21,5},{22,6},{23,7},{24,8},{25... | collective-permute-start | bytes 9437192 | tf_op jit(solution)/shard_map/ppermute | solution.py:17
  24.6 21.2 %copy-start.6 = (f32[1,64,96,128]{3,2,1,0:T(8,128)}, f32[1,64,96,128]{3,2,1,0:T(8,128)S(1)}, u32[]{:S(2)}) copy-start(f32[1,64,96,128]{3,2,1,0:T(8,128)S(1)} %collective-permute-done.1) | copy-start | bytes 9437188
  27.8 11.2 %collective-permute-start.2 = (f32[6,1,96,128]{3,2,1,0:T(8,128)S(1)}, f32[6,1,96,128]{3,2,1,0:T(8,128)S(1)}, u32[]{:S(2)}, u32[]{:S(2)}) collective-permute-start(f32[6,1,96,128]{3,2,1,0:T(8,128)S(1)} %get-tuple-element.19), channel_id=1, source_target_pairs={{0,4},{4,8},{8,12},{1,5},{5,9},{9,13},{2,6},{6,10},{10,14},{3,7},{... | collective-permute-start | bytes 884744 | tf_op jit(solution)/shard_map/ppermute | solution.py:14
  31.0 12.5 %collective-permute-start.3 = (f32[6,1,96,128]{3,2,1,0:T(8,128)S(1)}, f32[6,1,96,128]{3,2,1,0:T(8,128)S(1)}, u32[]{:S(2)}, u32[]{:S(2)}) collective-permute-start(f32[6,1,96,128]{3,2,1,0:T(8,128)S(1)} %get-tuple-element.20), channel_id=1, source_target_pairs={{4,0},{8,4},{12,8},{5,1},{9,5},{13,9},{6,2},{10,6},{14,10},{7,3},{... | collective-permute-start | bytes 884744 | tf_op jit(solution)/shard_map/ppermute | solution.py:17
  43.5 2.3 copy-start.7
  45.9 7.9 %collective-permute-start.5 = (f32[6,66,1,128]{3,1,2,0:T(8,128)S(1)}, f32[6,66,1,128]{3,1,2,0:T(8,128)S(1)}, u32[]{:S(2)}, u32[]{:S(2)}) collective-permute-start(f32[6,66,1,128]{3,1,2,0:T(8,128)S(1)} %copy.19), channel_id=1, source_target_pairs={{1,0},{2,1},{3,2},{5,4},{6,5},{7,6},{9,8},{10,9},{11,10},{13,12},{... | collective-permute-start | bytes 608264 | tf_op jit(solution)/shard_map/ppermute | solution.py:17
  48.0 7.6 %collective-permute-start.4 = (f32[6,66,1,128]{3,1,2,0:T(8,128)S(1)}, f32[6,66,1,128]{3,1,2,0:T(8,128)S(1)}, u32[]{:S(2)}, u32[]{:S(2)}) collective-permute-start(f32[6,66,1,128]{3,1,2,0:T(8,128)S(1)} %copy.17), channel_id=1, source_target_pairs={{0,1},{1,2},{2,3},{4,5},{5,6},{6,7},{8,9},{9,10},{10,11},{12,13},{... | collective-permute-start | bytes 608264 | tf_op jit(solution)/shard_map/ppermute | solution.py:14
  98.7 14.7 %copy-start = (f32[4,64,96,128]{3,2,1,0:T(8,128)S(1)}, f32[4,64,96,128]{3,2,1,0:T(8,128)}, u32[]{:S(2)}) copy-start(f32[4,64,96,128]{3,2,1,0:T(8,128)} %fusion.31) | copy-start | bytes 37748740
  102.2 8.8 %collective-permute-start.6 = (f32[1,64,96,128]{3,2,1,0:T(8,128)S(1)}, f32[1,64,96,128]{3,2,1,0:T(8,128)S(1)}, u32[]{:S(2)}, u32[]{:S(2)}) collective-permute-start(f32[1,64,96,128]{3,2,1,0:T(8,128)S(1)} %get-tuple-element.25), channel_id=1, source_target_pairs={{0,16},{1,17},{2,18},{3,19},{4,20},{5,21},{6,22},{7,23},{8,24},{9,... | collective-permute-start | bytes 9437192 | tf_op jit(solution)/shard_map/ppermute | solution.py:14
  103.7 9.6 %collective-permute-start.7 = (f32[1,64,96,128]{3,2,1,0:T(8,128)S(1)}, f32[1,64,96,128]{3,2,1,0:T(8,128)S(1)}, u32[]{:S(2)}, u32[]{:S(2)}) collective-permute-start(f32[1,64,96,128]{3,2,1,0:T(8,128)S(1)} %get-tuple-element.26), channel_id=1, source_target_pairs={{16,0},{17,1},{18,2},{19,3},{20,4},{21,5},{22,6},{23,7},{24,8},{25... | collective-permute-start | bytes 9437192 | tf_op jit(solution)/shard_map/ppermute | solution.py:17
  113.4 14.8 %copy-start.3 = (f32[1,64,96,128]{3,2,1,0:T(8,128)}, f32[1,64,96,128]{3,2,1,0:T(8,128)S(1)}, u32[]{:S(2)}) copy-start(f32[1,64,96,128]{3,2,1,0:T(8,128)S(1)} %collective-permute-done.7) | copy-start | bytes 9437188
  113.4 12.0 %collective-permute-start.8 = (f32[6,1,96,128]{3,2,1,0:T(8,128)S(1)}, f32[6,1,96,128]{3,2,1,0:T(8,128)S(1)}, u32[]{:S(2)}, u32[]{:S(2)}) collective-permute-start(f32[6,1,96,128]{3,2,1,0:T(8,128)S(1)} %get-tuple-element.17), channel_id=1, source_target_pairs={{0,4},{4,8},{8,12},{1,5},{5,9},{9,13},{2,6},{6,10},{10,14},{3,7},{... | collective-permute-start | bytes 884744 | tf_op jit(solution)/shard_map/ppermute | solution.py:14
  115.4 12.6 %collective-permute-start.9 = (f32[6,1,96,128]{3,2,1,0:T(8,128)S(1)}, f32[6,1,96,128]{3,2,1,0:T(8,128)S(1)}, u32[]{:S(2)}, u32[]{:S(2)}) collective-permute-start(f32[6,1,96,128]{3,2,1,0:T(8,128)S(1)} %get-tuple-element.18), channel_id=1, source_target_pairs={{4,0},{8,4},{12,8},{5,1},{9,5},{13,9},{6,2},{10,6},{14,10},{7,3},{... | collective-permute-start | bytes 884744 | tf_op jit(solution)/shard_map/ppermute | solution.py:17
  128.7 7.9 %collective-permute-start.11 = (f32[6,66,1,128]{3,1,2,0:T(8,128)S(1)}, f32[6,66,1,128]{3,1,2,0:T(8,128)S(1)}, u32[]{:S(2)}, u32[]{:S(2)}) collective-permute-start(f32[6,66,1,128]{3,1,2,0:T(8,128)S(1)} %copy.23), channel_id=1, source_target_pairs={{1,0},{2,1},{3,2},{5,4},{6,5},{7,6},{9,8},{10,9},{11,10},{13,12},{... | collective-permute-start | bytes 608264 | tf_op jit(solution)/shard_map/ppermute | solution.py:17
  130.6 7.9 %collective-permute-start.10 = (f32[6,66,1,128]{3,1,2,0:T(8,128)S(1)}, f32[6,66,1,128]{3,1,2,0:T(8,128)S(1)}, u32[]{:S(2)}, u32[]{:S(2)}) collective-permute-start(f32[6,66,1,128]{3,1,2,0:T(8,128)S(1)} %copy.21), channel_id=1, source_target_pairs={{0,1},{1,2},{2,3},{4,5},{5,6},{6,7},{8,9},{9,10},{10,11},{12,13},{... | collective-permute-start | bytes 608264 | tf_op jit(solution)/shard_map/ppermute | solution.py:14
  184.6 14.3 %copy-start.1 = (f32[4,64,96,128]{3,2,1,0:T(8,128)S(1)}, f32[4,64,96,128]{3,2,1,0:T(8,128)}, u32[]{:S(2)}) copy-start(f32[4,64,96,128]{3,2,1,0:T(8,128)} %fusion.22) | copy-start | bytes 37748740
  188.1 8.5 %collective-permute-start.12 = (f32[1,64,96,128]{3,2,1,0:T(8,128)S(1)}, f32[1,64,96,128]{3,2,1,0:T(8,128)S(1)}, u32[]{:S(2)}, u32[]{:S(2)}) collective-permute-start(f32[1,64,96,128]{3,2,1,0:T(8,128)S(1)} %get-tuple-element.23), channel_id=1, source_target_pairs={{0,16},{1,17},{2,18},{3,19},{4,20},{5,21},{6,22},{7,23},{8,24},{9,... | collective-permute-start | bytes 9437192 | tf_op jit(solution)/shard_map/ppermute | solution.py:14
  189.7 9.3 %collective-permute-start.13 = (f32[1,64,96,128]{3,2,1,0:T(8,128)S(1)}, f32[1,64,96,128]{3,2,1,0:T(8,128)S(1)}, u32[]{:S(2)}, u32[]{:S(2)}) collective-permute-start(f32[1,64,96,128]{3,2,1,0:T(8,128)S(1)} %get-tuple-element.24), channel_id=1, source_target_pairs={{16,0},{17,1},{18,2},{19,3},{20,4},{21,5},{22,6},{23,7},{24,8},{25... | collective-permute-start | bytes 9437192 | tf_op jit(solution)/shard_map/ppermute | solution.py:17
  199.0 14.8 %copy-start.4 = (f32[1,64,96,128]{3,2,1,0:T(8,128)}, f32[1,64,96,128]{3,2,1,0:T(8,128)S(1)}, u32[]{:S(2)}) copy-start(f32[1,64,96,128]{3,2,1,0:T(8,128)S(1)} %collective-permute-done.13) | copy-start | bytes 9437188
  199.0 12.0 %collective-permute-start.14 = (f32[6,1,96,128]{3,2,1,0:T(8,128)S(1)}, f32[6,1,96,128]{3,2,1,0:T(8,128)S(1)}, u32[]{:S(2)}, u32[]{:S(2)}) collective-permute-start(f32[6,1,96,128]{3,2,1,0:T(8,128)S(1)} %get-tuple-element.15), channel_id=1, source_target_pairs={{0,4},{4,8},{8,12},{1,5},{5,9},{9,13},{2,6},{6,10},{10,14},{3,7},{... | collective-permute-start | bytes 884744 | tf_op jit(solution)/shard_map/ppermute | solution.py:14
  201.0 12.6 %collective-permute-start.15 = (f32[6,1,96,128]{3,2,1,0:T(8,128)S(1)}, f32[6,1,96,128]{3,2,1,0:T(8,128)S(1)}, u32[]{:S(2)}, u32[]{:S(2)}) collective-permute-start(f32[6,1,96,128]{3,2,1,0:T(8,128)S(1)} %get-tuple-element.16), channel_id=1, source_target_pairs={{4,0},{8,4},{12,8},{5,1},{9,5},{13,9},{6,2},{10,6},{14,10},{7,3},{... | collective-permute-start | bytes 884744 | tf_op jit(solution)/shard_map/ppermute | solution.py:17
  214.3 7.9 %collective-permute-start.17 = (f32[6,66,1,128]{3,1,2,0:T(8,128)S(1)}, f32[6,66,1,128]{3,1,2,0:T(8,128)S(1)}, u32[]{:S(2)}, u32[]{:S(2)}) collective-permute-start(f32[6,66,1,128]{3,1,2,0:T(8,128)S(1)} %copy.27), channel_id=1, source_target_pairs={{1,0},{2,1},{3,2},{5,4},{6,5},{7,6},{9,8},{10,9},{11,10},{13,12},{... | collective-permute-start | bytes 608264 | tf_op jit(solution)/shard_map/ppermute | solution.py:17
  216.2 7.9 %collective-permute-start.16 = (f32[6,66,1,128]{3,1,2,0:T(8,128)S(1)}, f32[6,66,1,128]{3,1,2,0:T(8,128)S(1)}, u32[]{:S(2)}, u32[]{:S(2)}) collective-permute-start(f32[6,66,1,128]{3,1,2,0:T(8,128)S(1)} %copy.25), channel_id=1, source_target_pairs={{0,1},{1,2},{2,3},{4,5},{5,6},{6,7},{8,9},{9,10},{10,11},{12,13},{... | collective-permute-start | bytes 608264 | tf_op jit(solution)/shard_map/ppermute | solution.py:14
  269.6 14.3 %copy-start.2 = (f32[4,64,96,128]{3,2,1,0:T(8,128)S(1)}, f32[4,64,96,128]{3,2,1,0:T(8,128)}, u32[]{:S(2)}) copy-start(f32[4,64,96,128]{3,2,1,0:T(8,128)} %fusion.13) | copy-start | bytes 37748740
  273.0 8.5 %collective-permute-start.18 = (f32[1,64,96,128]{3,2,1,0:T(8,128)S(1)}, f32[1,64,96,128]{3,2,1,0:T(8,128)S(1)}, u32[]{:S(2)}, u32[]{:S(2)}) collective-permute-start(f32[1,64,96,128]{3,2,1,0:T(8,128)S(1)} %get-tuple-element.21), channel_id=1, source_target_pairs={{0,16},{1,17},{2,18},{3,19},{4,20},{5,21},{6,22},{7,23},{8,24},{9,... | collective-permute-start | bytes 9437192 | tf_op jit(solution)/shard_map/ppermute | solution.py:14
  274.6 9.3 %collective-permute-start.19 = (f32[1,64,96,128]{3,2,1,0:T(8,128)S(1)}, f32[1,64,96,128]{3,2,1,0:T(8,128)S(1)}, u32[]{:S(2)}, u32[]{:S(2)}) collective-permute-start(f32[1,64,96,128]{3,2,1,0:T(8,128)S(1)} %get-tuple-element.22), channel_id=1, source_target_pairs={{16,0},{17,1},{18,2},{19,3},{20,4},{21,5},{22,6},{23,7},{24,8},{25... | collective-permute-start | bytes 9437192 | tf_op jit(solution)/shard_map/ppermute | solution.py:17
  283.9 14.8 %copy-start.5 = (f32[1,64,96,128]{3,2,1,0:T(8,128)}, f32[1,64,96,128]{3,2,1,0:T(8,128)S(1)}, u32[]{:S(2)}) copy-start(f32[1,64,96,128]{3,2,1,0:T(8,128)S(1)} %collective-permute-done.19) | copy-start | bytes 9437188
  283.9 12.0 %collective-permute-start.20 = (f32[6,1,96,128]{3,2,1,0:T(8,128)S(1)}, f32[6,1,96,128]{3,2,1,0:T(8,128)S(1)}, u32[]{:S(2)}, u32[]{:S(2)}) collective-permute-start(f32[6,1,96,128]{3,2,1,0:T(8,128)S(1)} %get-tuple-element.13), channel_id=1, source_target_pairs={{0,4},{4,8},{8,12},{1,5},{5,9},{9,13},{2,6},{6,10},{10,14},{3,7},{... | collective-permute-start | bytes 884744 | tf_op jit(solution)/shard_map/ppermute | solution.py:14
  285.9 12.6 %collective-permute-start.21 = (f32[6,1,96,128]{3,2,1,0:T(8,128)S(1)}, f32[6,1,96,128]{3,2,1,0:T(8,128)S(1)}, u32[]{:S(2)}, u32[]{:S(2)}) collective-permute-start(f32[6,1,96,128]{3,2,1,0:T(8,128)S(1)} %get-tuple-element.14), channel_id=1, source_target_pairs={{4,0},{8,4},{12,8},{5,1},{9,5},{13,9},{6,2},{10,6},{14,10},{7,3},{... | collective-permute-start | bytes 884744 | tf_op jit(solution)/shard_map/ppermute | solution.py:17
  299.2 7.9 %collective-permute-start.23 = (f32[6,66,1,128]{3,1,2,0:T(8,128)S(1)}, f32[6,66,1,128]{3,1,2,0:T(8,128)S(1)}, u32[]{:S(2)}, u32[]{:S(2)}) collective-permute-start(f32[6,66,1,128]{3,1,2,0:T(8,128)S(1)} %copy.31), channel_id=1, source_target_pairs={{1,0},{2,1},{3,2},{5,4},{6,5},{7,6},{9,8},{10,9},{11,10},{13,12},{... | collective-permute-start | bytes 608264 | tf_op jit(solution)/shard_map/ppermute | solution.py:17
  301.2 7.9 %collective-permute-start.22 = (f32[6,66,1,128]{3,1,2,0:T(8,128)S(1)}, f32[6,66,1,128]{3,1,2,0:T(8,128)S(1)}, u32[]{:S(2)}, u32[]{:S(2)}) collective-permute-start(f32[6,66,1,128]{3,1,2,0:T(8,128)S(1)} %copy.29), channel_id=1, source_target_pairs={{0,1},{1,2},{2,3},{4,5},{5,6},{6,7},{8,9},{9,10},{10,11},{12,13},{... | collective-permute-start | bytes 608264 | tf_op jit(solution)/shard_map/ppermute | solution.py:14
  (3 other events, 2.2 us)
where the time goes:
time: 362 us; the launch traced here: 356 us
  other arithmetic  181 us (50%)
  starting transfers between devices  70.9 us (20%)
  waiting for transfers between devices  64.3 us (18%)
  local copies, waits for them, and re-layouts  39.2 us (11%)
    add x4, other arithmetic, advance(): return middle + 0.1 * spread + 0.2 * middle * (1.0 - middle * crowding)  177 us
    ppermute x12, starting transfers between devices, with_halo(): lax.ppermute(lax.slice_in_dim(block, 0, width, axis=dim), axis, backward)  42.6 us
    ppermute x12, waiting for transfers between devices, with_halo(): lax.ppermute(lax.slice_in_dim(block, block.shape[dim] - width, None, axis...  35 us
    ppermute x12, waiting for transfers between devices, with_halo(): lax.ppermute(lax.slice_in_dim(block, 0, width, axis=dim), axis, backward)  29.2 us
    ppermute x12, starting transfers between devices, with_halo(): lax.ppermute(lax.slice_in_dim(block, block.shape[dim] - width, None, axis...  28.3 us
    unnamed x24, local copies, waits for them, and re-layouts  13.5 us
    slice x8, local copies, waits for them, and re-layouts, with_halo(): lax.slice_in_dim(block, block.shape[dim] - width, None, axis=dim)  11.6 us
  transfers between devices with their start and end apart: 24, of which 23 were waited for; matrix products, arithmetic and copies ran while one was open for 4% of the time, Pallas kernels for 0%

commit v1 on v0

v1 whole, which is shorter than its diff:
```python
import functools

import jax
import jax.numpy as jnp
from jax import lax
from jax.experimental import pallas as pl
from jax.experimental.pallas import tpu as pltpu
from jax.sharding import PartitionSpec as P

STEPS = 4
SUB = 8
VMEM_SPEC = pl.BlockSpec(memory_space=pltpu.VMEM)
HBM_SPEC = pl.BlockSpec(memory_space=pltpu.HBM)


def matchings(count):
    swaps = []
    for first in (0, 1):
        pairs = [(i, i + 1) for i in range(first, count - 1, 2)]
        if pairs:
            swaps.append(pairs + [(b, a) for a, b in pairs])
    return swaps


def swap(face, axis, which, count):
    with jax.named_scope(f"swap_{axis}_{which}"):
        return lax.ppermute(face, axis, matchings(count)[which])


def near(which, parity, size):
    high = parity == which
    return jnp.where(high, size - 1, 0)


def mirrored(j, parity, rows):
    return jnp.where(parity == 0, j, rows - 1 - j)


def pack_kernel(dims, counts, tracer, *refs):
    rows, nx, nz = dims
    n_y, n_x, n_z = counts
    faces, (groups, sems) = refs[: sum(counts)], refs[sum(counts) :]
    y_faces, x_faces, z_faces = faces[:n_y], faces[n_y : n_y + n_x], faces[n_y + n_x :]
    py = lax.rem(lax.axis_index("rows"), 2)
    px = lax.rem(lax.axis_index("cols"), 2)
    pz = lax.rem(lax.axis_index("slabs"), 2)
    order = [mirrored(j, py, rows) for j in range(rows)]
    z_copies, copies = [], []
    for which in range(n_z):
        z = pl.multiple_of(near(which, pz, nz // SUB) * SUB, SUB)
        for j in range(rows):
            z_copies.append((tracer.at[order[j], :, pl.ds(z, SUB), :], groups.at[which, j]))
    for which in range(n_x):
        for j in range(rows):
            copies.append((tracer.at[order[j], near(which, px, nx)], x_faces[which].at[j]))
    for which in range(n_y):
        copies.append((tracer.at[order[rows - 1 if which == 0 else 0]], y_faces[which]))
    started = []
    for k, (src, dst) in enumerate(z_copies + copies):
        copy = pltpu.make_async_copy(src, dst, sems.at[k])
        copy.start()
        started.append(copy)
    for copy in started[: len(z_copies)]:
        copy.wait()
    for which in range(n_z):
        z = near(which, pz, SUB)
        for j in range(rows):
            cells = groups.at[which, j].reshape(nx * SUB, 128)
            for x in range(0, nx, SUB):
                face = cells[pl.ds(x * SUB + z, SUB, stride=SUB), :]
                z_faces[which][j, pl.ds(x, SUB), :] = face
    for copy in started[len(z_copies) :]:
        copy.wait()


def bulk_kernel(dims, counts, step, pitches, *refs):
    rows, nx, nz = dims
    first, last = step == 0, step == STEPS - 1
    src, refs = (refs[:1], refs[1:]) if first else (refs[:rows], refs[rows:])
    halos, refs = refs[: counts[0]], refs[counts[0] :]
    crowding, outs = refs[0], refs[1:]
    py = lax.rem(lax.axis_index("rows"), 2)
    order = [mirrored(j, py, rows) for j in range(rows)]
    pitch = nz + 1

    if not last:
        zero = jnp.zeros((SUB, 128), jnp.float32)
        for out in outs:
            for x in range(0, nx, SUB):
                out[pl.ds(x * pitch, SUB, stride=pitch), :] = zero
            out[pl.ds(nx * pitch, SUB), :] = zero

    scale = 2.0 * 10.0**-step

    def column(z, edge):
        def load(j, x, shift):
            if first:
                ref = src[0].at[order[j]]
                if shift == 0:
                    return ref[x, pl.ds(z, SUB), :]
                if edge == shift:
                    own = ref[x, pl.ds(z, SUB), :]
                    rolled = pltpu.roll(own, (-shift) % SUB, 0)
                    row = lax.broadcasted_iota(jnp.int32, (SUB, 128), 0)
                    return jnp.where(row == (0 if shift < 0 else SUB - 1), 0.0, rolled)
                return ref[x, pl.ds(z + shift, SUB), :]
            return src[j][pl.ds(x * pitch + 1 + z + shift, SUB), :]

        def load_halo(which, x):
            if first:
                return halos[which][x, pl.ds(z, SUB), :]
            return halos[which][pl.ds(x * pitch + 1 + z, SUB), :]

        def plane(x):
            cells = [load(j, x, 0) for j in range(rows)]
            cells.append(load_halo(0, x))
            below = load_halo(1, x) if counts[0] > 1 else None
            return cells, below

        def advance(x, carry, final):
            diag, here, below = carry
            if final:
                after, after_below = None, None
            else:
                after, after_below = plane(x + 1)
            forward = []
            for j in range(-1, rows):
                own = below if j < 0 else here[j]
                if final:
                    forward.append(own)
                elif own is None:
                    forward.append(after[j + 1])
                else:
                    forward.append(own + after[j + 1])
            for j in range(rows):
                total = load(j, x, -1) + load(j, x, 1)
                total = total + diag[j]
                if forward[j] is not None:
                    total = total + forward[j]
                cell = here[j]
                c = crowding[order[j], x, pl.ds(z, SUB), :]
                value = total + cell * (6.0 - (c * scale) * cell)
                if last:
                    outs[0][order[j], x, pl.ds(z, SUB), :] = value * 10.0**-STEPS
                else:
                    outs[j][pl.ds(x * pitch + 1 + z, SUB), :] = value
            return forward[1:], after[:rows] if after else None, after_below

        start, start_below = plane(0)
        carry = (start[1:], start[:rows], start_below)
        unroll = 3 if (nx - 1) % 3 == 0 else 1

        def body(i, carry):
            for k in range(unroll):
                carry = advance(i * unroll + k, carry, False)
            return carry

        carry = lax.fori_loop(0, (nx - 1) // unroll, body, carry)
        advance(nx - 1, carry, True)

    groups = nz // SUB
    if first:
        column(0, -1)
        pl.loop(1, groups - 1)(lambda g: column(pl.multiple_of(g * SUB, SUB), 0))
        column(nz - SUB, 1)
    else:
        pl.loop(0, groups)(lambda g: column(pl.multiple_of(g * SUB, SUB), 0))


def patch_kernel(dims, counts, step, *refs):
    rows, nx, nz = dims
    last = step == STEPS - 1
    n_state = 1 if last else rows
    state, refs = refs[:n_state], refs[n_state:]
    n_x, n_z = counts[1], counts[2]
    halo_x, halo_z, refs = refs[:n_x], refs[n_x : n_x + n_z], refs[n_x + n_z :]
    out, refs = refs[:n_state], refs[n_state:]
    face_x, face_z = (None, None) if last else (refs[:n_x], refs[n_x : n_x + n_z])
    py = lax.rem(lax.axis_index("rows"), 2)
    px = lax.rem(lax.axis_index("cols"), 2)
    pz = lax.rem(lax.axis_index("slabs"), 2)
    pitch = nz if last else nz + 1
    offset = 0 if last else 1

    def view(refs, j):
        return refs[0].at[mirrored(j, py, rows)] if last else refs[j]

    def scaled(values):
        return values * 10.0**-STEPS if last else values

    for which in range(n_z):
        z = near(which, pz, nz)
        for j in range(rows):
            for x in range(0, nx, SUB):
                at = (pl.ds(x * pitch + offset + z, SUB, stride=pitch), slice(None))
                view(out, j)[at] = view(out, j)[at] + scaled(halo_z[which][j, pl.ds(x, SUB), :])
    for which in range(n_x):
        x = near(which, px, nx)
        for j in range(rows):
            for z in range(0, nz, SUB):
                at = (pl.ds(x * pitch + offset + z, SUB), slice(None))
                value = view(out, j)[at] + scaled(halo_x[which][j, pl.ds(z, SUB), :])
                view(out, j)[at] = value
                if not last:
                    face_x[which][j, pl.ds(z, SUB), :] = value
    if not last:
        for which in range(n_z):
            z = near(which, pz, nz)
            for j in range(rows):
                for x in range(0, nx, SUB):
                    at = (pl.ds(x * pitch + offset + z, SUB, stride=pitch), slice(None))
                    face_z[which][j, pl.ds(x, SUB), :] = out[j][at]


def call(kernel, name, out_shape, args, out_specs=None, in_specs=None, aliases=None, scratch=(), vmem=1):
    return pl.pallas_call(
        kernel,
        name=name,
        out_shape=out_shape,
        in_specs=in_specs or [VMEM_SPEC] * len(args),
        out_specs=out_specs or [VMEM_SPEC] * len(out_shape),
        input_output_aliases=aliases or {},
        scratch_shapes=list(scratch),
        compiler_params=pltpu.CompilerParams(vmem_limit_bytes=vmem * 1024 * 1024),
    )(*args)


def on_device(tracer, crowding):
    rows, nx, nz, species = tracer.shape
    dims = (rows, nx, nz)
    sizes = [lax.axis_size(axis) for axis in ("rows", "cols", "slabs")]
    counts = [len(matchings(size)) for size in sizes]
    pitch_rows = -(-(nx * (nz + 1) + SUB) // SUB) * SUB
    f32 = jnp.float32
    full_row = pltpu.VMEM((nx, nz, species), f32)
    state_row = pltpu.VMEM((pitch_rows, species), f32)
    x_face = pltpu.VMEM((rows, nz, species), f32)
    z_face = pltpu.VMEM((rows, nx, species), f32)

    out_shape = [full_row] * counts[0] + [x_face] * counts[1] + [z_face] * counts[2]
    packed = call(
        functools.partial(pack_kernel, dims, counts),
        "pack",
        out_shape,
        (pltpu.with_memory_space_constraint(tracer, pltpu.HBM),),
        in_specs=[HBM_SPEC],
        scratch=[
            pltpu.VMEM((counts[2], rows, nx, SUB, species), f32),
            pltpu.SemaphoreType.DMA((counts[0] + rows * (counts[1] + counts[2]),)),
        ],
        vmem=4,
    )
    y_faces, packed = packed[: counts[0]], packed[counts[0] :]
    x_faces, z_faces = packed[: counts[1]], packed[counts[1] :]
    state = [tracer]
    for step in range(STEPS):
        last = step == STEPS - 1
        y_halos = [swap(face, "rows", k, sizes[0]) for k, face in enumerate(y_faces)]
        x_halos = [swap(face, "cols", k, sizes[1]) for k, face in enumerate(x_faces)]
        z_halos = [swap(face, "slabs", k, sizes[2]) for k, face in enumerate(z_faces)]
        if last:
            out_shape = [pltpu.VMEM(tracer.shape, f32)]
        else:
            out_shape = [state_row] * rows
        state = call(
            functools.partial(bulk_kernel, dims, counts, step, None),
            f"bulk{step}",
            out_shape,
            (*state, *y_halos, crowding),
        )
        args = (*state, *x_halos, *z_halos)
        if last:
            out_shape = [pltpu.VMEM((rows, nx * nz, species), f32)]
            args = (state[0].reshape(rows, nx * nz, species), *args[1:])
        else:
            out_shape = [state_row] * rows + [x_face] * counts[1] + [z_face] * counts[2]
        patched = call(
            functools.partial(patch_kernel, dims, counts, step),
            f"patch{step}",
            out_shape,
            args,
            aliases={k: k for k in range(len(state))},
        )
        if not last:
            state = patched[:rows]
            y_faces = [state[rows - 1 if k == 0 else 0] for k in range(counts[0])]
            x_faces = patched[rows : rows + counts[1]]
            z_faces = patched[rows + counts[1] :]
    return patched[0].reshape(rows, nx, nz, species)


def solution(mesh):
    placed = (P("rows", "cols", "slabs", None), P("rows", "cols", "slabs", None))
    return jax.shard_map(
        on_device,
        mesh=mesh,
        in_specs=placed,
        out_specs=P("rows", "cols", "slabs", None),
        check_vma=False,
    )
```

time: 362 us -> 80.5 us (0.22); the launches traced: 356 us -> 80.2 us
  other arithmetic: 181 us -> 0 us
  waiting for transfers between devices: 64.3 us -> 0.05 us
  starting transfers between devices: 70.9 us -> 29.5 us
  Pallas kernels: 0 us -> 40.9 us
  local copies, waits for them, and re-layouts: 39.2 us -> 9.35 us
    add x4 -> x0, other arithmetic: 177 us -> none  [advance(): return middle + 0.1 * spread + 0.2 * middle * (1.0 - middle * crowding)]
    ppermute x24 -> x20, waiting for transfers between devices: 64.3 us -> 0.05 us  [swap(): return lax.ppermute(face, axis, matchings(count)[which])]
    ppermute x24 -> x20, starting transfers between devices: 70.9 us -> 29.5 us  [swap(): return lax.ppermute(face, axis, matchings(count)[which])]
    pallas_call x0 -> x9, Pallas kernels: none -> 40.9 us  [call(): pl.pallas_call(kernel, name=name, out_shape=out_shape, in_specs=in_specs...]
    slice x13 -> x0, local copies, waits for them, and re-layouts: 16.6 us -> none  [the longest x8 11.6 us: with_halo(): lax.slice_in_dim(block, block.shape[dim] - width, None, axis=dim)]
    ppermute x8 -> x0, local copies, waits for them, and re-layouts: 7.09 us -> none  [the longest x4 3.55 us: with_halo(): lax.ppermute(lax.slice_in_dim(block, 0, width, axis=dim), axis, backward)]
    unnamed x24 -> x5, local copies, waits for them, and re-layouts: 13.5 us -> 9.35 us
  transfers between devices with their start and end apart: 24 -> 20, of which waited for: 23 -> 0; matrix products, arithmetic and copies ran while one was open for 4% -> 0% of each run, Pallas kernels for 0% -> 46%
where the time goes in v1:
time: 80.5 us; the launch traced here: 80.2 us
  Pallas kernels  40.9 us (51%)
  starting transfers between devices  29.5 us (37%)
  local copies, waits for them, and re-layouts  9.35 us (12%)
    pallas_call x9, Pallas kernels, call(): pl.pallas_call(kernel, name=name, out_shape=out_shape, in_specs=in_specs...  40.9 us
    ppermute x20, starting transfers between devices, swap(): return lax.ppermute(face, axis, matchings(count)[which])  29.5 us
    unnamed x5, local copies, waits for them, and re-layouts  9.35 us
  transfers between devices with their start and end apart: 20, of which 0 were waited for; matrix products, arithmetic and copies ran while one was open for 0% of the time, Pallas kernels for 46%

profile of v1, /device:TPU:13, one launch (start us, length us, event | category | flops | bytes accessed | tf_op | source)
XLA Modules:
  0.0 80.2 jit_solution(731740034830745865)
XLA Ops:
  0.0 3.0 %pack.1 = (f32[64,96,128]{2,1,0:T(8,128)S(1)}, f32[4,96,128]{2,1,0:T(8,128)S(1)}, f32[4,96,128]{2,1,0:T(8,128)S(1)}, f32[4,64,128]{2,1,0:T(8,128)S(1)}, f32[4,64,128]{2,1,0:T(8,128)S(1)}) custom-call(f32[4,64,96,128]{3,2,1,0:T(8,128)} %refs_0_.1), custom_call_target="tpu_custom_call" | custom-call | tf_op jit(solution)/shard_map/pack/pallas_call | solution.py:216
  3.0 0.7 collective-permute-start
  3.7 1.2 %collective-permute-start.1 = (f32[4,96,128]{2,1,0:T(8,128)S(1)}, f32[4,96,128]{2,1,0:T(8,128)S(1)}, u32[]{:S(2)}, u32[]{:S(2)}) collective-permute-start(f32[4,96,128]{2,1,0:T(8,128)S(1)} %get-tuple-element.51), channel_id=1, source_target_pairs={{0,4},{8,12},{4,0},{12,8},{1,5},{9,13},{5,1},{13,9},{2,6},{10,14},... | collective-permute-start | bytes 589832 | tf_op jit(solution)/shard_map/swap_cols_0/ppermute | solution.py:27
  4.9 2.4 %collective-permute-start.2 = (f32[4,96,128]{2,1,0:T(8,128)S(1)}, f32[4,96,128]{2,1,0:T(8,128)S(1)}, u32[]{:S(2)}, u32[]{:S(2)}) collective-permute-start(f32[4,96,128]{2,1,0:T(8,128)S(1)} %get-tuple-element.52), channel_id=1, source_target_pairs={{4,8},{8,4},{5,9},{9,5},{6,10},{10,6},{7,11},{11,7},{20,24},{24,20... | collective-permute-start | bytes 589832 | tf_op jit(solution)/shard_map/swap_cols_1/ppermute | solution.py:27
  7.3 0.1 collective-permute-start.3
  7.4 4.5 %collective-permute-start.4 = (f32[4,64,128]{2,1,0:T(8,128)S(1)}, f32[4,64,128]{2,1,0:T(8,128)S(1)}, u32[]{:S(2)}, u32[]{:S(2)}) collective-permute-start(f32[4,64,128]{2,1,0:T(8,128)S(1)} %get-tuple-element.54), channel_id=1, source_target_pairs={{1,2},{2,1},{5,6},{6,5},{9,10},{10,9},{13,14},{14,13},{17,18},{18,... | collective-permute-start | bytes 393224 | tf_op jit(solution)/shard_map/swap_slabs_1/ppermute | solution.py:27
  11.9 0.0 collective-permute-done.refs_1_
  11.9 0.0 copy-start.1
  11.9 4.6 %copy-done.1 = f32[4,64,96,128]{3,2,1,0:T(8,128)S(1)} copy-done((f32[4,64,96,128]{3,2,1,0:T(8,128)S(1)}, f32[4,64,96,128]{3,2,1,0:T(8,128)}, u32[]{:S(2)}) %copy-start.1) | copy-done | bytes 12582936
  16.5 9.0 %bulk0.1 = (f32[6216,128]{1,0:T(8,128)S(1)}, f32[6216,128]{1,0:T(8,128)S(1)}, f32[6216,128]{1,0:T(8,128)S(1)}, f32[6216,128]{1,0:T(8,128)S(1)}) custom-call(f32[4,64,96,128]{3,2,1,0:T(8,128)S(1)} %copy-done.1, f32[64,96,128]{2,1,0:T(8,128)S(1)} %collective-permute-done.refs_1_, f32[4,64,96,128]{3,2,1,0:T(8,128)S(1)} %copy-done), custom_call_target="tpu_custom_call" | custom-call | tf_op jit(solution)/shard_map/bulk0/pallas_call | solution.py:216
  25.5 0.0 collective-permute-done.4.refs_7_
  25.5 0.0 collective-permute-done.1.refs_4_
  25.5 0.1 patch0.1
  25.6 1.3 %collective-permute-start.5 = (f32[6216,128]{1,0:T(8,128)S(1)}, f32[6216,128]{1,0:T(8,128)S(1)}, u32[]{:S(2)}, u32[]{:S(2)}) collective-permute-start(f32[6216,128]{1,0:T(8,128)S(1)} %get-tuple-element.58.refs_3_), channel_id=1, source_target_pairs={{0,16},{16,0},{1,17},{17,1},{2,18},{18,2},{3,19},{19,3},{4,20},{20... | collective-permute-start | bytes 9547784 | tf_op jit(solution)/shard_map/swap_rows_0/ppermute | solution.py:27
  26.9 3.9 %collective-permute-start.7 = (f32[4,96,128]{2,1,0:T(8,128)S(1)}, f32[4,96,128]{2,1,0:T(8,128)S(1)}, u32[]{:S(2)}, u32[]{:S(2)}) collective-permute-start(f32[4,96,128]{2,1,0:T(8,128)S(1)} %get-tuple-element.64), channel_id=1, source_target_pairs={{4,8},{8,4},{5,9},{9,5},{6,10},{10,6},{7,11},{11,7},{20,24},{24,20... | collective-permute-start | bytes 589832 | tf_op jit(solution)/shard_map/swap_cols_1/ppermute | solution.py:27
  30.8 0.1 collective-permute-start.8
  30.9 1.9 %collective-permute-start.9 = (f32[4,64,128]{2,1,0:T(8,128)S(1)}, f32[4,64,128]{2,1,0:T(8,128)S(1)}, u32[]{:S(2)}, u32[]{:S(2)}) collective-permute-start(f32[4,64,128]{2,1,0:T(8,128)S(1)} %get-tuple-element.66), channel_id=1, source_target_pairs={{1,2},{2,1},{5,6},{6,5},{9,10},{10,9},{13,14},{14,13},{17,18},{18,... | collective-permute-start | bytes 393224 | tf_op jit(solution)/shard_map/swap_slabs_1/ppermute | solution.py:27
  32.9 9.2 %bulk1.1 = (f32[6216,128]{1,0:T(8,128)S(1)}, f32[6216,128]{1,0:T(8,128)S(1)}, f32[6216,128]{1,0:T(8,128)S(1)}, f32[6216,128]{1,0:T(8,128)S(1)}) custom-call(f32[6216,128]{1,0:T(8,128)S(1)} %get-tuple-element.55.refs_0_, f32[6216,128]{1,0:T(8,128)S(1)} %get-tuple-element.56.refs_1_, f32[6216,128]{1,0:T(8,128)S(1)} %get-tuple-element.57.refs_2_, ...), custom_call_target="tpu_custom_call" | custom-call | tf_op jit(solution)/shard_map/bulk1/pallas_call | solution.py:216
  42.1 0.1 patch1.1
  42.2 0.4 collective-permute-start.10
  42.7 3.3 %collective-permute-start.12 = (f32[4,96,128]{2,1,0:T(8,128)S(1)}, f32[4,96,128]{2,1,0:T(8,128)S(1)}, u32[]{:S(2)}, u32[]{:S(2)}) collective-permute-start(f32[4,96,128]{2,1,0:T(8,128)S(1)} %get-tuple-element.76), channel_id=1, source_target_pairs={{4,8},{8,4},{5,9},{9,5},{6,10},{10,6},{7,11},{11,7},{20,24},{24,20... | collective-permute-start | bytes 589832 | tf_op jit(solution)/shard_map/swap_cols_1/ppermute | solution.py:27
  46.0 0.1 collective-permute-start.13
  46.1 2.6 %collective-permute-start.14 = (f32[4,64,128]{2,1,0:T(8,128)S(1)}, f32[4,64,128]{2,1,0:T(8,128)S(1)}, u32[]{:S(2)}, u32[]{:S(2)}) collective-permute-start(f32[4,64,128]{2,1,0:T(8,128)S(1)} %get-tuple-element.78), channel_id=1, source_target_pairs={{1,2},{2,1},{5,6},{6,5},{9,10},{10,9},{13,14},{14,13},{17,18},{18,... | collective-permute-start | bytes 393224 | tf_op jit(solution)/shard_map/swap_slabs_1/ppermute | solution.py:27
  48.7 9.2 %bulk2.1 = (f32[6216,128]{1,0:T(8,128)S(1)}, f32[6216,128]{1,0:T(8,128)S(1)}, f32[6216,128]{1,0:T(8,128)S(1)}, f32[6216,128]{1,0:T(8,128)S(1)}) custom-call(f32[6216,128]{1,0:T(8,128)S(1)} %get-tuple-element.67.refs_0_, f32[6216,128]{1,0:T(8,128)S(1)} %get-tuple-element.68.refs_1_, f32[6216,128]{1,0:T(8,128)S(1)} %get-tuple-element.69.refs_2_, ...), custom_call_target="tpu_custom_call" | custom-call | tf_op jit(solution)/shard_map/bulk2/pallas_call | solution.py:216
  57.9 0.1 patch2.1
  58.1 0.9 %collective-permute-start.15 = (f32[6216,128]{1,0:T(8,128)S(1)}, f32[6216,128]{1,0:T(8,128)S(1)}, u32[]{:S(2)}, u32[]{:S(2)}) collective-permute-start(f32[6216,128]{1,0:T(8,128)S(1)} %get-tuple-element.82.refs_3_), channel_id=1, source_target_pairs={{0,16},{16,0},{1,17},{17,1},{2,18},{18,2},{3,19},{19,3},{4,20},{20... | collective-permute-start | bytes 9547784 | tf_op jit(solution)/shard_map/swap_rows_0/ppermute | solution.py:27
  58.9 3.8 %collective-permute-start.17 = (f32[4,96,128]{2,1,0:T(8,128)S(1)}, f32[4,96,128]{2,1,0:T(8,128)S(1)}, u32[]{:S(2)}, u32[]{:S(2)}) collective-permute-start(f32[4,96,128]{2,1,0:T(8,128)S(1)} %get-tuple-element.84), channel_id=1, source_target_pairs={{4,8},{8,4},{5,9},{9,5},{6,10},{10,6},{7,11},{11,7},{20,24},{24,20... | collective-permute-start | bytes 589832 | tf_op jit(solution)/shard_map/swap_cols_1/ppermute | solution.py:27
  62.7 0.1 collective-permute-start.18
  62.8 2.4 %collective-permute-start.19 = (f32[4,64,128]{2,1,0:T(8,128)S(1)}, f32[4,64,128]{2,1,0:T(8,128)S(1)}, u32[]{:S(2)}, u32[]{:S(2)}) collective-permute-start(f32[4,64,128]{2,1,0:T(8,128)S(1)} %get-tuple-element.86), channel_id=1, source_target_pairs={{1,2},{2,1},{5,6},{6,5},{9,10},{10,9},{13,14},{14,13},{17,18},{18,... | collective-permute-start | bytes 393224 | tf_op jit(solution)/shard_map/swap_slabs_1/ppermute | solution.py:27
  65.2 9.7 %bulk3.1 = f32[4,64,96,128]{3,2,1,0:T(8,128)S(1)} custom-call(f32[6216,128]{1,0:T(8,128)S(1)} %get-tuple-element.79.refs_0_, f32[6216,128]{1,0:T(8,128)S(1)} %get-tuple-element.80.refs_1_, f32[6216,128]{1,0:T(8,128)S(1)} %get-tuple-element.81.refs_2_, f32[6216,128]{1,0:T(8,128)S(1)} %get-tuple-element.82.refs_3_, ...), custom_call_target="tpu_custom_call" | custom-call | tf_op jit(solution)/shard_map/bulk3/pallas_call | solution.py:216
  74.9 0.5 patch3.1
  75.4 4.8 %copy.29 = f32[4,64,96,128]{3,2,1,0:T(8,128)} copy(f32[4,64,96,128]{3,2,1,0:T(8,128)S(1)} %bitcast.3) | data formatting | bytes 25165824
  (22 shorter events, 0.1 us)
Async XLA Ops:
  0.0 11.9 %copy-start = (f32[4,64,96,128]{3,2,1,0:T(8,128)S(1)}, f32[4,64,96,128]{3,2,1,0:T(8,128)}, u32[]{:S(2)}) copy-start(f32[4,64,96,128]{3,2,1,0:T(8,128)} %refs_5_.5) | copy-start | bytes 37748740
  3.0 8.9 %collective-permute-start = (f32[64,96,128]{2,1,0:T(8,128)S(1)}, f32[64,96,128]{2,1,0:T(8,128)S(1)}, u32[]{:S(2)}, u32[]{:S(2)}) collective-permute-start(f32[64,96,128]{2,1,0:T(8,128)S(1)} %get-tuple-element.46), channel_id=1, source_target_pairs={{0,16},{16,0},{1,17},{17,1},{2,18},{18,2},{3,19},{19,3},{4,20},{20... | collective-permute-start | bytes 9437192 | tf_op jit(solution)/shard_map/swap_rows_0/ppermute | solution.py:27
  3.7 21.8 %collective-permute-start.1 = (f32[4,96,128]{2,1,0:T(8,128)S(1)}, f32[4,96,128]{2,1,0:T(8,128)S(1)}, u32[]{:S(2)}, u32[]{:S(2)}) collective-permute-start(f32[4,96,128]{2,1,0:T(8,128)S(1)} %get-tuple-element.51), channel_id=1, source_target_pairs={{0,4},{8,12},{4,0},{12,8},{1,5},{9,13},{5,1},{13,9},{2,6},{10,14},... | collective-permute-start | bytes 589832 | tf_op jit(solution)/shard_map/swap_cols_0/ppermute | solution.py:27
  4.9 20.6 %collective-permute-start.2 = (f32[4,96,128]{2,1,0:T(8,128)S(1)}, f32[4,96,128]{2,1,0:T(8,128)S(1)}, u32[]{:S(2)}, u32[]{:S(2)}) collective-permute-start(f32[4,96,128]{2,1,0:T(8,128)S(1)} %get-tuple-element.52), channel_id=1, source_target_pairs={{4,8},{8,4},{5,9},{9,5},{6,10},{10,6},{7,11},{11,7},{20,24},{24,20... | collective-permute-start | bytes 589832 | tf_op jit(solution)/shard_map/swap_cols_1/ppermute | solution.py:27
  7.3 18.2 %collective-permute-start.3 = (f32[4,64,128]{2,1,0:T(8,128)S(1)}, f32[4,64,128]{2,1,0:T(8,128)S(1)}, u32[]{:S(2)}, u32[]{:S(2)}) collective-permute-start(f32[4,64,128]{2,1,0:T(8,128)S(1)} %get-tuple-element.53), channel_id=1, source_target_pairs={{0,1},{2,3},{1,0},{3,2},{4,5},{6,7},{5,4},{7,6},{8,9},{10,11},{9,8... | collective-permute-start | bytes 393224 | tf_op jit(solution)/shard_map/swap_slabs_0/ppermute | solution.py:27
  7.4 18.1 %collective-permute-start.4 = (f32[4,64,128]{2,1,0:T(8,128)S(1)}, f32[4,64,128]{2,1,0:T(8,128)S(1)}, u32[]{:S(2)}, u32[]{:S(2)}) collective-permute-start(f32[4,64,128]{2,1,0:T(8,128)S(1)} %get-tuple-element.54), channel_id=1, source_target_pairs={{1,2},{2,1},{5,6},{6,5},{9,10},{10,9},{13,14},{14,13},{17,18},{18,... | collective-permute-start | bytes 393224 | tf_op jit(solution)/shard_map/swap_slabs_1/ppermute | solution.py:27
  11.9 4.6 %copy-start.1 = (f32[4,64,96,128]{3,2,1,0:T(8,128)S(1)}, f32[4,64,96,128]{3,2,1,0:T(8,128)}, u32[]{:S(2)}) copy-start(f32[4,64,96,128]{3,2,1,0:T(8,128)} %refs_0_.1) | copy-start | bytes 37748740
  25.6 7.2 %collective-permute-start.5 = (f32[6216,128]{1,0:T(8,128)S(1)}, f32[6216,128]{1,0:T(8,128)S(1)}, u32[]{:S(2)}, u32[]{:S(2)}) collective-permute-start(f32[6216,128]{1,0:T(8,128)S(1)} %get-tuple-element.58.refs_3_), channel_id=1, source_target_pairs={{0,16},{16,0},{1,17},{17,1},{2,18},{18,2},{3,19},{19,3},{4,20},{20... | collective-permute-start | bytes 9547784 | tf_op jit(solution)/shard_map/swap_rows_0/ppermute | solution.py:27
  26.9 15.2 %collective-permute-start.6 = (f32[4,96,128]{2,1,0:T(8,128)S(1)}, f32[4,96,128]{2,1,0:T(8,128)S(1)}, u32[]{:S(2)}, u32[]{:S(2)}) collective-permute-start(f32[4,96,128]{2,1,0:T(8,128)S(1)} %get-tuple-element.63), channel_id=1, source_target_pairs={{0,4},{8,12},{4,0},{12,8},{1,5},{9,13},{5,1},{13,9},{2,6},{10,14},... | collective-permute-start | bytes 589832 | tf_op jit(solution)/shard_map/swap_cols_0/ppermute | solution.py:27
  26.9 15.2 %collective-permute-start.7 = (f32[4,96,128]{2,1,0:T(8,128)S(1)}, f32[4,96,128]{2,1,0:T(8,128)S(1)}, u32[]{:S(2)}, u32[]{:S(2)}) collective-permute-start(f32[4,96,128]{2,1,0:T(8,128)S(1)} %get-tuple-element.64), channel_id=1, source_target_pairs={{4,8},{8,4},{5,9},{9,5},{6,10},{10,6},{7,11},{11,7},{20,24},{24,20... | collective-permute-start | bytes 589832 | tf_op jit(solution)/shard_map/swap_cols_1/ppermute | solution.py:27
  30.8 11.2 %collective-permute-start.8 = (f32[4,64,128]{2,1,0:T(8,128)S(1)}, f32[4,64,128]{2,1,0:T(8,128)S(1)}, u32[]{:S(2)}, u32[]{:S(2)}) collective-permute-start(f32[4,64,128]{2,1,0:T(8,128)S(1)} %get-tuple-element.65), channel_id=1, source_target_pairs={{0,1},{2,3},{1,0},{3,2},{4,5},{6,7},{5,4},{7,6},{8,9},{10,11},{9,8... | collective-permute-start | bytes 393224 | tf_op jit(solution)/shard_map/swap_slabs_0/ppermute | solution.py:27
  30.9 11.2 %collective-permute-start.9 = (f32[4,64,128]{2,1,0:T(8,128)S(1)}, f32[4,64,128]{2,1,0:T(8,128)S(1)}, u32[]{:S(2)}, u32[]{:S(2)}) collective-permute-start(f32[4,64,128]{2,1,0:T(8,128)S(1)} %get-tuple-element.66), channel_id=1, source_target_pairs={{1,2},{2,1},{5,6},{6,5},{9,10},{10,9},{13,14},{14,13},{17,18},{18,... | collective-permute-start | bytes 393224 | tf_op jit(solution)/shard_map/swap_slabs_1/ppermute | solution.py:27
  42.2 6.4 %collective-permute-start.10 = (f32[6216,128]{1,0:T(8,128)S(1)}, f32[6216,128]{1,0:T(8,128)S(1)}, u32[]{:S(2)}, u32[]{:S(2)}) collective-permute-start(f32[6216,128]{1,0:T(8,128)S(1)} %get-tuple-element.70.refs_3_), channel_id=1, source_target_pairs={{0,16},{16,0},{1,17},{17,1},{2,18},{18,2},{3,19},{19,3},{4,20},{20... | collective-permute-start | bytes 9547784 | tf_op jit(solution)/shard_map/swap_rows_0/ppermute | solution.py:27
  42.7 15.2 %collective-permute-start.11 = (f32[4,96,128]{2,1,0:T(8,128)S(1)}, f32[4,96,128]{2,1,0:T(8,128)S(1)}, u32[]{:S(2)}, u32[]{:S(2)}) collective-permute-start(f32[4,96,128]{2,1,0:T(8,128)S(1)} %get-tuple-element.75), channel_id=1, source_target_pairs={{0,4},{8,12},{4,0},{12,8},{1,5},{9,13},{5,1},{13,9},{2,6},{10,14},... | collective-permute-start | bytes 589832 | tf_op jit(solution)/shard_map/swap_cols_0/ppermute | solution.py:27
  42.7 15.2 %collective-permute-start.12 = (f32[4,96,128]{2,1,0:T(8,128)S(1)}, f32[4,96,128]{2,1,0:T(8,128)S(1)}, u32[]{:S(2)}, u32[]{:S(2)}) collective-permute-start(f32[4,96,128]{2,1,0:T(8,128)S(1)} %get-tuple-element.76), channel_id=1, source_target_pairs={{4,8},{8,4},{5,9},{9,5},{6,10},{10,6},{7,11},{11,7},{20,24},{24,20... | collective-permute-start | bytes 589832 | tf_op jit(solution)/shard_map/swap_cols_1/ppermute | solution.py:27
  46.0 11.9 %collective-permute-start.13 = (f32[4,64,128]{2,1,0:T(8,128)S(1)}, f32[4,64,128]{2,1,0:T(8,128)S(1)}, u32[]{:S(2)}, u32[]{:S(2)}) collective-permute-start(f32[4,64,128]{2,1,0:T(8,128)S(1)} %get-tuple-element.77), channel_id=1, source_target_pairs={{0,1},{2,3},{1,0},{3,2},{4,5},{6,7},{5,4},{7,6},{8,9},{10,11},{9,8... | collective-permute-start | bytes 393224 | tf_op jit(solution)/shard_map/swap_slabs_0/ppermute | solution.py:27
  46.1 11.8 %collective-permute-start.14 = (f32[4,64,128]{2,1,0:T(8,128)S(1)}, f32[4,64,128]{2,1,0:T(8,128)S(1)}, u32[]{:S(2)}, u32[]{:S(2)}) collective-permute-start(f32[4,64,128]{2,1,0:T(8,128)S(1)} %get-tuple-element.78), channel_id=1, source_target_pairs={{1,2},{2,1},{5,6},{6,5},{9,10},{10,9},{13,14},{14,13},{17,18},{18,... | collective-permute-start | bytes 393224 | tf_op jit(solution)/shard_map/swap_slabs_1/ppermute | solution.py:27
  58.1 7.1 %collective-permute-start.15 = (f32[6216,128]{1,0:T(8,128)S(1)}, f32[6216,128]{1,0:T(8,128)S(1)}, u32[]{:S(2)}, u32[]{:S(2)}) collective-permute-start(f32[6216,128]{1,0:T(8,128)S(1)} %get-tuple-element.82.refs_3_), channel_id=1, source_target_pairs={{0,16},{16,0},{1,17},{17,1},{2,18},{18,2},{3,19},{19,3},{4,20},{20... | collective-permute-start | bytes 9547784 | tf_op jit(solution)/shard_map/swap_rows_0/ppermute | solution.py:27
  58.9 16.0 %collective-permute-start.16 = (f32[4,96,128]{2,1,0:T(8,128)S(1)}, f32[4,96,128]{2,1,0:T(8,128)S(1)}, u32[]{:S(2)}, u32[]{:S(2)}) collective-permute-start(f32[4,96,128]{2,1,0:T(8,128)S(1)} %get-tuple-element.83), channel_id=1, source_target_pairs={{0,4},{8,12},{4,0},{12,8},{1,5},{9,13},{5,1},{13,9},{2,6},{10,14},... | collective-permute-start | bytes 589832 | tf_op jit(solution)/shard_map/swap_cols_0/ppermute | solution.py:27
  58.9 16.0 %collective-permute-start.17 = (f32[4,96,128]{2,1,0:T(8,128)S(1)}, f32[4,96,128]{2,1,0:T(8,128)S(1)}, u32[]{:S(2)}, u32[]{:S(2)}) collective-permute-start(f32[4,96,128]{2,1,0:T(8,128)S(1)} %get-tuple-element.84), channel_id=1, source_target_pairs={{4,8},{8,4},{5,9},{9,5},{6,10},{10,6},{7,11},{11,7},{20,24},{24,20... | collective-permute-start | bytes 589832 | tf_op jit(solution)/shard_map/swap_cols_1/ppermute | solution.py:27
  62.7 12.1 %collective-permute-start.18 = (f32[4,64,128]{2,1,0:T(8,128)S(1)}, f32[4,64,128]{2,1,0:T(8,128)S(1)}, u32[]{:S(2)}, u32[]{:S(2)}) collective-permute-start(f32[4,64,128]{2,1,0:T(8,128)S(1)} %get-tuple-element.85), channel_id=1, source_target_pairs={{0,1},{2,3},{1,0},{3,2},{4,5},{6,7},{5,4},{7,6},{8,9},{10,11},{9,8... | collective-permute-start | bytes 393224 | tf_op jit(solution)/shard_map/swap_slabs_0/ppermute | solution.py:27
  62.8 12.1 %collective-permute-start.19 = (f32[4,64,128]{2,1,0:T(8,128)S(1)}, f32[4,64,128]{2,1,0:T(8,128)S(1)}, u32[]{:S(2)}, u32[]{:S(2)}) collective-permute-start(f32[4,64,128]{2,1,0:T(8,128)S(1)} %get-tuple-element.86), channel_id=1, source_target_pairs={{1,2},{2,1},{5,6},{6,5},{9,10},{10,9},{13,14},{14,13},{17,18},{18,... | collective-permute-start | bytes 393224 | tf_op jit(solution)/shard_map/swap_slabs_1/ppermute | solution.py:27

commit v2 on v1

v2 whole, which is shorter than its diff:
```python
import functools

import jax
import jax.numpy as jnp
from jax import lax
from jax.experimental import pallas as pl
from jax.experimental.pallas import tpu as pltpu
from jax.sharding import PartitionSpec as P

STEPS = 4
SUB = 8
VMEM_SPEC = pl.BlockSpec(memory_space=pltpu.VMEM)
HBM_SPEC = pl.BlockSpec(memory_space=pltpu.HBM)


def matchings(count):
    swaps = []
    for first in (0, 1):
        pairs = [(i, i + 1) for i in range(first, count - 1, 2)]
        if pairs:
            swaps.append(pairs + [(b, a) for a, b in pairs])
    return swaps


def swap(face, axis, which, count):
    with jax.named_scope(f"swap_{axis}_{which}"):
        return lax.ppermute(face, axis, matchings(count)[which])


def near(which, parity, size):
    high = parity == which
    return jnp.where(high, size - 1, 0)


def mirrored(j, parity, rows):
    return jnp.where(parity == 0, j, rows - 1 - j)


def pack_kernel(dims, counts, tracer, *refs):
    rows, nx, nz = dims
    n_y, n_x, n_z = counts
    faces, (groups, sems) = refs[: sum(counts)], refs[sum(counts) :]
    y_faces, x_faces, z_faces = faces[:n_y], faces[n_y : n_y + n_x], faces[n_y + n_x :]
    py = lax.rem(lax.axis_index("rows"), 2)
    px = lax.rem(lax.axis_index("cols"), 2)
    pz = lax.rem(lax.axis_index("slabs"), 2)
    order = [mirrored(j, py, rows) for j in range(rows)]
    z_copies, copies = [], []
    for which in range(n_z):
        z = pl.multiple_of(near(which, pz, nz // SUB) * SUB, SUB)
        for j in range(rows):
            z_copies.append((tracer.at[order[j], :, pl.ds(z, SUB), :], groups.at[which, j]))
    for which in range(n_x):
        for j in range(rows):
            copies.append((tracer.at[order[j], near(which, px, nx)], x_faces[which].at[j]))
    for which in range(n_y):
        copies.append((tracer.at[order[rows - 1 if which == 0 else 0]], y_faces[which]))
    started = []
    for k, (src, dst) in enumerate(z_copies + copies):
        copy = pltpu.make_async_copy(src, dst, sems.at[k])
        copy.start()
        started.append(copy)
    for copy in started[: len(z_copies)]:
        copy.wait()
    for which in range(n_z):
        z = near(which, pz, SUB)
        for j in range(rows):
            cells = groups.at[which, j].reshape(nx * SUB, 128)
            for x in range(0, nx, SUB):
                face = cells[pl.ds(x * SUB + z, SUB, stride=SUB), :]
                z_faces[which][j, pl.ds(x, SUB), :] = face
    for copy in started[len(z_copies) :]:
        copy.wait()


def bulk_kernel(dims, counts, step, *refs):
    rows, nx, nz = dims
    first, last = step == 0, step == STEPS - 1
    src, refs = (refs[:1], refs[1:]) if first else (refs[:rows], refs[rows:])
    halos, refs = refs[: counts[0]], refs[counts[0] :]
    crowding, refs = refs[0], refs[1:]
    py = lax.rem(lax.axis_index("rows"), 2)
    order = [mirrored(j, py, rows) for j in range(rows)]
    pitch = nz + 1
    groups = nz // SUB
    together = 2 if groups % 4 == 0 else 1
    span = together * together * SUB
    piece = together * SUB
    blocks = nz // span
    copies = []
    if first:
        outs, (cells, sems) = refs[:rows], refs[rows:]
        for k in range(nz // piece):
            at = (slice(None), slice(None), pl.ds(k * piece, piece), slice(None))
            copies.append(pltpu.make_async_copy(src[0].at[at], cells.at[at], sems.at[k]))
            copies[-1].start()
    elif last:
        done, outs, sems = refs[0], refs[1 : 1 + rows], refs[1 + rows]
    else:
        outs = refs

    if not last:
        zero = jnp.zeros((SUB, 128), jnp.float32)
        for out in outs:
            for x in range(0, nx, SUB):
                out[pl.ds(x * pitch, SUB, stride=pitch), :] = zero
            out[pl.ds(nx * pitch, SUB), :] = zero

    scale = 2.0 * 10.0**-step

    def columns(z, edges):
        shifts = [z + k * together * SUB for k in range(together)]

        def load(k, j, x, shift):
            z = shifts[k]
            if first:
                ref = cells.at[order[j]]
                if shift == 0:
                    return ref[x, pl.ds(z, SUB), :]
                if edges[k] == shift:
                    own = ref[x, pl.ds(z, SUB), :]
                    rolled = pltpu.roll(own, (-shift) % SUB, 0)
                    row = lax.broadcasted_iota(jnp.int32, (SUB, 128), 0)
                    return jnp.where(row == (0 if shift < 0 else SUB - 1), 0.0, rolled)
                return ref[x, pl.ds(z + shift, SUB), :]
            return src[j][pl.ds(x * pitch + 1 + z + shift, SUB), :]

        def load_halo(k, which, x):
            if first:
                return halos[which][x, pl.ds(shifts[k], SUB), :]
            return halos[which][pl.ds(x * pitch + 1 + shifts[k], SUB), :]

        def plane(x):
            planes = [[load(k, j, x, 0) for j in range(rows)] for k in range(together)]
            above = [load_halo(k, 0, x) for k in range(together)]
            below = [load_halo(k, 1, x) if counts[0] > 1 else None for k in range(together)]
            return planes, above, below

        def advance(x, carry, final):
            diag, here, below = carry
            after = None if final else plane(x + 1)
            diags = []
            for k in range(together):
                forward = []
                for j in range(-1, rows):
                    own = below[k] if j < 0 else here[k][j]
                    if final:
                        forward.append(own)
                        continue
                    ahead = after[0][k][j + 1] if j + 1 < rows else after[1][k]
                    forward.append(ahead if own is None else own + ahead)
                for j in range(rows):
                    total = load(k, j, x, -1) + load(k, j, x, 1)
                    total = total + diag[k][j]
                    if forward[j] is not None:
                        total = total + forward[j]
                    cell = here[k][j]
                    c = crowding[order[j], x, pl.ds(shifts[k], SUB), :]
                    value = total + cell * (6.0 - (c * scale) * cell)
                    if last:
                        outs[j][x, pl.ds(shifts[k], SUB), :] = value * 10.0**-STEPS
                    else:
                        outs[j][pl.ds(x * pitch + 1 + shifts[k], SUB), :] = value
                diags.append(forward[1:])
            return None if final else (diags, after[0], after[2])

        planes, above, below = plane(0)
        carry = ([planes[k][1:] + [above[k]] for k in range(together)], planes, below)
        unroll = max(k for k in range(1, 10) if (nx - 1) % k == 0)

        def body(i, carry):
            for k in range(unroll):
                carry = advance(i * unroll + k, carry, False)
            return carry

        carry = lax.fori_loop(0, (nx - 1) // unroll, body, carry)
        advance(nx - 1, carry, True)

    def block(base, part, edges):
        columns(base + part * SUB, edges)

    parts = [(k, part) for k in range(blocks) for part in range(together)]
    if first:
        landed = 0
        for k, part in parts:
            base = k * span + part * SUB
            top = base + (together - 1) * piece + SUB
            edges = [0] * together
            if base == 0:
                edges[0] = -1
            if top == nz:
                edges[-1] = 1
            while landed * piece < min(top + 1, nz):
                copies[landed].wait()
                landed += 1
            block(k * span, part, edges)
    elif last:

        def send(group, j):
            at = (slice(None), pl.ds(pl.multiple_of(group * SUB, SUB), SUB), slice(None))
            return pltpu.make_async_copy(outs[j].at[at], done.at[order[j]].at[at], sems.at[group, j])

        @pl.loop(0, blocks)
        def _(k):
            for part in range(together):
                block(pl.multiple_of(k * span, SUB), part, None)
                for g in range(together):
                    for j in range(rows):
                        send(k * together * together + part + g * together, j).start()

        for group in range(groups):
            for j in range(rows):
                send(group, j).wait()
    else:

        @pl.loop(0, blocks)
        def _(k):
            for part in range(together):
                block(pl.multiple_of(k * span, SUB), part, None)


def patch_kernel(dims, counts, step, *refs):
    rows, nx, nz = dims
    last = step == STEPS - 1
    n_state = rows + 1 if last else rows
    n_x, n_z = counts[1], counts[2]
    refs = refs[n_state:]
    halo_x, halo_z, refs = refs[:n_x], refs[n_x : n_x + n_z], refs[n_x + n_z :]
    state, refs = refs[:n_state], refs[n_state:]
    if last:
        done, cells, sems = state[0], state[1:], refs[0]
    else:
        face_x, face_z = refs[:n_x], refs[n_x:]
    py = lax.rem(lax.axis_index("rows"), 2)
    px = lax.rem(lax.axis_index("cols"), 2)
    pz = lax.rem(lax.axis_index("slabs"), 2)
    pitch = nz if last else nz + 1
    offset = 0 if last else 1

    if last:
        order = [mirrored(j, py, rows) for j in range(rows)]
        views = [cells[j].reshape(nx * nz, 128) for j in range(rows)]
    else:
        views = state

    def scaled(values):
        return values * 10.0**-STEPS if last else values

    copies = []

    def send(j, at):
        sem = sems.at[len(copies)]
        copies.append(pltpu.make_async_copy(cells[j].at[at], done.at[order[j]].at[at], sem))
        copies[-1].start()

    for which in range(n_z):
        z = near(which, pz, nz)
        for j in range(rows):
            for x in range(0, nx, SUB):
                at = (pl.ds(x * pitch + offset + z, SUB, stride=pitch), slice(None))
                views[j][at] = views[j][at] + scaled(halo_z[which][j, pl.ds(x, SUB), :])
    for which in range(n_x):
        x = near(which, px, nx)
        for j in range(rows):
            for z in range(0, nz, SUB):
                at = (pl.ds(x * pitch + offset + z, SUB), slice(None))
                value = views[j][at] + scaled(halo_x[which][j, pl.ds(z, SUB), :])
                views[j][at] = value
                if not last:
                    face_x[which][j, pl.ds(z, SUB), :] = value
    if last:
        inner = pl.ds(SUB, nz - 2 * SUB)
        for j in range(rows):
            for z in (0, nz - SUB):
                send(j, (slice(None), pl.ds(z, SUB), slice(None)))
            for x in (0, nx - 1):
                send(j, (x, inner, slice(None)))
        for copy in copies:
            copy.wait()
        return
    for which in range(n_z):
        z = near(which, pz, nz)
        for j in range(rows):
            for x in range(0, nx, SUB):
                at = (pl.ds(x * pitch + offset + z, SUB, stride=pitch), slice(None))
                face_z[which][j, pl.ds(x, SUB), :] = views[j][at]


def call(kernel, name, out_shape, args, out_specs=None, in_specs=None, aliases=None, scratch=(), vmem=1):
    return pl.pallas_call(
        kernel,
        name=name,
        out_shape=out_shape,
        in_specs=in_specs or [VMEM_SPEC] * len(args),
        out_specs=out_specs or [VMEM_SPEC] * len(out_shape),
        input_output_aliases=aliases or {},
        scratch_shapes=list(scratch),
        compiler_params=pltpu.CompilerParams(vmem_limit_bytes=vmem * 1024 * 1024),
    )(*args)


def on_device(tracer, crowding):
    rows, nx, nz, species = tracer.shape
    dims = (rows, nx, nz)
    sizes = [lax.axis_size(axis) for axis in ("rows", "cols", "slabs")]
    counts = [len(matchings(size)) for size in sizes]
    pitch_rows = -(-(nx * (nz + 1) + SUB) // 32) * 32
    f32 = jnp.float32
    full_row = pltpu.VMEM((nx, nz, species), f32)
    state_row = pltpu.VMEM((pitch_rows, species), f32)
    x_face = pltpu.VMEM((rows, nz, species), f32)
    z_face = pltpu.VMEM((rows, nx, species), f32)

    out_shape = [full_row] * counts[0] + [x_face] * counts[1] + [z_face] * counts[2]
    packed = call(
        functools.partial(pack_kernel, dims, counts),
        "pack",
        out_shape,
        (pltpu.with_memory_space_constraint(tracer, pltpu.HBM),),
        in_specs=[HBM_SPEC],
        scratch=[
            pltpu.VMEM((counts[2], rows, nx, SUB, species), f32),
            pltpu.SemaphoreType.DMA((counts[0] + rows * (counts[1] + counts[2]),)),
        ],
        vmem=4,
    )
    y_faces, packed = packed[: counts[0]], packed[counts[0] :]
    x_faces, z_faces = packed[: counts[1]], packed[counts[1] :]
    state = [tracer]
    for step in range(STEPS):
        last = step == STEPS - 1
        y_halos = [swap(face, "rows", k, sizes[0]) for k, face in enumerate(y_faces)]
        x_halos = [swap(face, "cols", k, sizes[1]) for k, face in enumerate(x_faces)]
        z_halos = [swap(face, "slabs", k, sizes[2]) for k, face in enumerate(z_faces)]
        stage_sems = pltpu.SemaphoreType.DMA((nz // SUB,))
        kernel = functools.partial(bulk_kernel, dims, counts, step)
        args = (*state, *y_halos, crowding)
        if step == 0:
            args = (pltpu.with_memory_space_constraint(tracer, pltpu.HBM), *args[1:])
            state = call(
                kernel,
                "bulk0",
                [state_row] * rows,
                args,
                in_specs=[HBM_SPEC] + [VMEM_SPEC] * (len(args) - 1),
                scratch=[pltpu.VMEM(tracer.shape, f32), stage_sems],
                vmem=tracer.size * 4 // 2**20 + 1,
            )
        elif last:
            state = call(
                kernel,
                "bulk_last",
                [pltpu.HBM(tracer.shape, f32)] + [full_row] * rows,
                args,
                out_specs=[HBM_SPEC] + [VMEM_SPEC] * rows,
                scratch=[pltpu.SemaphoreType.DMA((nz // SUB, rows))],
            )
        else:
            state = call(kernel, f"bulk{step}", [state_row] * rows, args)
        kernel = functools.partial(patch_kernel, dims, counts, step)
        args = (*state, *x_halos, *z_halos)
        aliases = {k: k for k in range(len(state))}
        if last:
            specs = [HBM_SPEC] + [VMEM_SPEC] * rows
            return call(
                kernel,
                "patch_last",
                [pltpu.HBM(tracer.shape, f32)] + [full_row] * rows,
                args,
                in_specs=specs + [VMEM_SPEC] * (len(args) - len(specs)),
                out_specs=specs,
                aliases=aliases,
                scratch=[pltpu.SemaphoreType.DMA((4 * rows,))],
            )[0]
        out_shape = [state_row] * rows + [x_face] * counts[1] + [z_face] * counts[2]
        patched = call(kernel, f"patch{step}", out_shape, args, aliases=aliases)
        state = patched[:rows]
        y_faces = [state[rows - 1 if k == 0 else 0] for k in range(counts[0])]
        x_faces = patched[rows : rows + counts[1]]
        z_faces = patched[rows + counts[1] :]


def solution(mesh):
    placed = (P("rows", "cols", "slabs", None), P("rows", "cols", "slabs", None))
    return jax.shard_map(
        on_device,
        mesh=mesh,
        in_specs=placed,
        out_specs=P("rows", "cols", "slabs", None),
        check_vma=False,
    )
```

time: 80.5 us -> 58.7 us (0.73)
  Pallas kernels: 40.9 us -> 28.2 us
  local copies, waits for them, and re-layouts: 9.35 us -> 0.01 us
  waiting for transfers between devices: 0.05 us -> 1.19 us
    pallas_call x9, Pallas kernels: 40.9 us -> 28.2 us  [call(): pl.pallas_call(kernel, name=name, out_shape=out_shape, in_specs=in_specs...]
    unnamed x5 -> x2, local copies, waits for them, and re-layouts: 9.35 us -> 0.01 us
    ppermute x20, waiting for transfers between devices: 0.05 us -> 1.19 us  [swap(): return lax.ppermute(face, axis, matchings(count)[which])]
    ppermute x20, starting transfers between devices: 29.5 us -> 28.7 us  [swap(): return lax.ppermute(face, axis, matchings(count)[which])]
  transfers between devices with their start and end apart: 20 -> 20, of which waited for: 0 -> 2; matrix products, arithmetic and copies ran while one was open for 0% -> 0% of each run, Pallas kernels for 46% -> 39%
where the time goes in v2:
time: 58.7 us; the launch traced here: 58.4 us
  starting transfers between devices  28.7 us (49%)
  Pallas kernels  28.2 us (48%)
  waiting for transfers between devices  1.19 us (2%)
    ppermute x20, starting transfers between devices, swap(): return lax.ppermute(face, axis, matchings(count)[which])  28.7 us
    pallas_call x9, Pallas kernels, call(): pl.pallas_call(kernel, name=name, out_shape=out_shape, in_specs=in_specs...  28.2 us
    ppermute x20, waiting for transfers between devices, swap(): return lax.ppermute(face, axis, matchings(count)[which])  1.19 us
  transfers between devices with their start and end apart: 20, of which 2 were waited for; matrix products, arithmetic and copies ran while one was open for 0% of the time, Pallas kernels for 39%

profile of v2, /device:TPU:13, one launch (start us, length us, event | category | flops | bytes accessed | tf_op | source)
XLA Modules:
  0.0 58.4 jit_solution(15388121580675872936)
XLA Ops:
  0.0 3.0 %pack.1 = (f32[64,96,128]{2,1,0:T(8,128)S(1)}, f32[4,96,128]{2,1,0:T(8,128)S(1)}, f32[4,96,128]{2,1,0:T(8,128)S(1)}, f32[4,64,128]{2,1,0:T(8,128)S(1)}, f32[4,64,128]{2,1,0:T(8,128)S(1)}) custom-call(f32[4,64,96,128]{3,2,1,0:T(8,128)} %refs_0_.1), custom_call_target="tpu_custom_call" | custom-call | tf_op jit(solution)/shard_map/pack/pallas_call | solution.py:290
  3.0 0.7 %collective-permute-start = (f32[64,96,128]{2,1,0:T(8,128)S(1)}, f32[64,96,128]{2,1,0:T(8,128)S(1)}, u32[]{:S(2)}, u32[]{:S(2)}) collective-permute-start(f32[64,96,128]{2,1,0:T(8,128)S(1)} %get-tuple-element.52), channel_id=1, source_target_pairs={{0,16},{16,0},{1,17},{17,1},{2,18},{18,2},{3,19},{19,3},{4,20},{20... | collective-permute-start | bytes 9437192 | tf_op jit(solution)/shard_map/swap_rows_0/ppermute | solution.py:27
  3.7 1.2 %collective-permute-start.1 = (f32[4,96,128]{2,1,0:T(8,128)S(1)}, f32[4,96,128]{2,1,0:T(8,128)S(1)}, u32[]{:S(2)}, u32[]{:S(2)}) collective-permute-start(f32[4,96,128]{2,1,0:T(8,128)S(1)} %get-tuple-element.57), channel_id=1, source_target_pairs={{0,4},{8,12},{4,0},{12,8},{1,5},{9,13},{5,1},{13,9},{2,6},{10,14},... | collective-permute-start | bytes 589832 | tf_op jit(solution)/shard_map/swap_cols_0/ppermute | solution.py:27
  4.9 2.4 %collective-permute-start.2 = (f32[4,96,128]{2,1,0:T(8,128)S(1)}, f32[4,96,128]{2,1,0:T(8,128)S(1)}, u32[]{:S(2)}, u32[]{:S(2)}) collective-permute-start(f32[4,96,128]{2,1,0:T(8,128)S(1)} %get-tuple-element.58), channel_id=1, source_target_pairs={{4,8},{8,4},{5,9},{9,5},{6,10},{10,6},{7,11},{11,7},{20,24},{24,20... | collective-permute-start | bytes 589832 | tf_op jit(solution)/shard_map/swap_cols_1/ppermute | solution.py:27
  7.3 0.1 collective-permute-start.3
  7.4 4.5 %collective-permute-start.4 = (f32[4,64,128]{2,1,0:T(8,128)S(1)}, f32[4,64,128]{2,1,0:T(8,128)S(1)}, u32[]{:S(2)}, u32[]{:S(2)}) collective-permute-start(f32[4,64,128]{2,1,0:T(8,128)S(1)} %get-tuple-element.60), channel_id=1, source_target_pairs={{1,2},{2,1},{5,6},{6,5},{9,10},{10,9},{13,14},{14,13},{17,18},{18,... | collective-permute-start | bytes 393224 | tf_op jit(solution)/shard_map/swap_slabs_1/ppermute | solution.py:27
  11.9 0.0 collective-permute-done.refs_1_
  11.9 6.6 %bulk0.1 = (f32[6240,128]{1,0:T(8,128)S(1)}, f32[6240,128]{1,0:T(8,128)S(1)}, f32[6240,128]{1,0:T(8,128)S(1)}, f32[6240,128]{1,0:T(8,128)S(1)}) custom-call(f32[4,64,96,128]{3,2,1,0:T(8,128)} %refs_0_.1, f32[64,96,128]{2,1,0:T(8,128)S(1)} %collective-permute-done.refs_1_, f32[4,64,96,128]{3,2,1,0:T(8,128)S(1)} %copy-done), custom_call_target="tpu_custom_call" | custom-call | tf_op jit(solution)/shard_map/bulk0/pallas_call | solution.py:290
  18.5 0.0 collective-permute-done.3.refs_6_
  18.6 0.0 collective-permute-done.1.refs_4_
  18.6 0.0 collective-permute-done.2.refs_5_
  18.6 0.1 patch0.1
  18.7 1.3 %collective-permute-start.5 = (f32[6240,128]{1,0:T(8,128)S(1)}, f32[6240,128]{1,0:T(8,128)S(1)}, u32[]{:S(2)}, u32[]{:S(2)}) collective-permute-start(f32[6240,128]{1,0:T(8,128)S(1)} %get-tuple-element.64.refs_3_), channel_id=1, source_target_pairs={{0,16},{16,0},{1,17},{17,1},{2,18},{18,2},{3,19},{19,3},{4,20},{20... | collective-permute-start | bytes 9584648 | tf_op jit(solution)/shard_map/swap_rows_0/ppermute | solution.py:27
  20.0 3.9 %collective-permute-start.7 = (f32[4,96,128]{2,1,0:T(8,128)S(1)}, f32[4,96,128]{2,1,0:T(8,128)S(1)}, u32[]{:S(2)}, u32[]{:S(2)}) collective-permute-start(f32[4,96,128]{2,1,0:T(8,128)S(1)} %get-tuple-element.70), channel_id=1, source_target_pairs={{4,8},{8,4},{5,9},{9,5},{6,10},{10,6},{7,11},{11,7},{20,24},{24,20... | collective-permute-start | bytes 589832 | tf_op jit(solution)/shard_map/swap_cols_1/ppermute | solution.py:27
  23.9 0.1 collective-permute-start.8
  24.0 1.9 %collective-permute-start.9 = (f32[4,64,128]{2,1,0:T(8,128)S(1)}, f32[4,64,128]{2,1,0:T(8,128)S(1)}, u32[]{:S(2)}, u32[]{:S(2)}) collective-permute-start(f32[4,64,128]{2,1,0:T(8,128)S(1)} %get-tuple-element.72), channel_id=1, source_target_pairs={{1,2},{2,1},{5,6},{6,5},{9,10},{10,9},{13,14},{14,13},{17,18},{18,... | collective-permute-start | bytes 393224 | tf_op jit(solution)/shard_map/swap_slabs_1/ppermute | solution.py:27
  25.9 4.7 %bulk1.1 = (f32[6240,128]{1,0:T(8,128)S(1)}, f32[6240,128]{1,0:T(8,128)S(1)}, f32[6240,128]{1,0:T(8,128)S(1)}, f32[6240,128]{1,0:T(8,128)S(1)}) custom-call(f32[6240,128]{1,0:T(8,128)S(1)} %get-tuple-element.61.refs_0_, f32[6240,128]{1,0:T(8,128)S(1)} %get-tuple-element.62.refs_1_, f32[6240,128]{1,0:T(8,128)S(1)} %get-tuple-element.63.refs_2_, ...), custom_call_target="tpu_custom_call" | custom-call | tf_op jit(solution)/shard_map/bulk1/pallas_call | solution.py:290
  30.7 0.8 %collective-permute-done.7.refs_5_ = f32[4,96,128]{2,1,0:T(8,128)S(1)} collective-permute-done((f32[4,96,128]{2,1,0:T(8,128)S(1)}, f32[4,96,128]{2,1,0:T(8,128)S(1)}, u32[]{:S(2)}, u32[]{:S(2)}) %collective-permute-start.7) | collective-permute-done | bytes 196640 | tf_op jit(solution)/shard_map/swap_cols_1/ppermute | solution.py:27
  31.4 0.1 patch1.1
  31.5 0.7 %collective-permute-start.10 = (f32[6240,128]{1,0:T(8,128)S(1)}, f32[6240,128]{1,0:T(8,128)S(1)}, u32[]{:S(2)}, u32[]{:S(2)}) collective-permute-start(f32[6240,128]{1,0:T(8,128)S(1)} %get-tuple-element.76.refs_3_), channel_id=1, source_target_pairs={{0,16},{16,0},{1,17},{17,1},{2,18},{18,2},{3,19},{19,3},{4,20},{20... | collective-permute-start | bytes 9584648 | tf_op jit(solution)/shard_map/swap_rows_0/ppermute | solution.py:27
  32.2 2.3 %collective-permute-start.12 = (f32[4,96,128]{2,1,0:T(8,128)S(1)}, f32[4,96,128]{2,1,0:T(8,128)S(1)}, u32[]{:S(2)}, u32[]{:S(2)}) collective-permute-start(f32[4,96,128]{2,1,0:T(8,128)S(1)} %get-tuple-element.82), channel_id=1, source_target_pairs={{4,8},{8,4},{5,9},{9,5},{6,10},{10,6},{7,11},{11,7},{20,24},{24,20... | collective-permute-start | bytes 589832 | tf_op jit(solution)/shard_map/swap_cols_1/ppermute | solution.py:27
  34.6 0.1 collective-permute-start.13
  34.6 2.6 %collective-permute-start.14 = (f32[4,64,128]{2,1,0:T(8,128)S(1)}, f32[4,64,128]{2,1,0:T(8,128)S(1)}, u32[]{:S(2)}, u32[]{:S(2)}) collective-permute-start(f32[4,64,128]{2,1,0:T(8,128)S(1)} %get-tuple-element.84), channel_id=1, source_target_pairs={{1,2},{2,1},{5,6},{6,5},{9,10},{10,9},{13,14},{14,13},{17,18},{18,... | collective-permute-start | bytes 393224 | tf_op jit(solution)/shard_map/swap_slabs_1/ppermute | solution.py:27
  37.2 0.4 collective-permute-done.10.refs_4_
  37.6 4.7 %bulk2.1 = (f32[6240,128]{1,0:T(8,128)S(1)}, f32[6240,128]{1,0:T(8,128)S(1)}, f32[6240,128]{1,0:T(8,128)S(1)}, f32[6240,128]{1,0:T(8,128)S(1)}) custom-call(f32[6240,128]{1,0:T(8,128)S(1)} %get-tuple-element.73.refs_0_, f32[6240,128]{1,0:T(8,128)S(1)} %get-tuple-element.74.refs_1_, f32[6240,128]{1,0:T(8,128)S(1)} %get-tuple-element.75.refs_2_, ...), custom_call_target="tpu_custom_call" | custom-call | tf_op jit(solution)/shard_map/bulk2/pallas_call | solution.py:290
  42.3 0.1 patch2.1
  42.5 0.5 collective-permute-start.15
  42.9 3.8 %collective-permute-start.17 = (f32[4,96,128]{2,1,0:T(8,128)S(1)}, f32[4,96,128]{2,1,0:T(8,128)S(1)}, u32[]{:S(2)}, u32[]{:S(2)}) collective-permute-start(f32[4,96,128]{2,1,0:T(8,128)S(1)} %get-tuple-element.95), channel_id=1, source_target_pairs={{4,8},{8,4},{5,9},{9,5},{6,10},{10,6},{7,11},{11,7},{20,24},{24,20... | collective-permute-start | bytes 589832 | tf_op jit(solution)/shard_map/swap_cols_1/ppermute | solution.py:27
  46.7 0.1 collective-permute-start.18
  46.8 2.6 %collective-permute-start.19 = (f32[4,64,128]{2,1,0:T(8,128)S(1)}, f32[4,64,128]{2,1,0:T(8,128)S(1)}, u32[]{:S(2)}, u32[]{:S(2)}) collective-permute-start(f32[4,64,128]{2,1,0:T(8,128)S(1)} %get-tuple-element.97), channel_id=1, source_target_pairs={{1,2},{2,1},{5,6},{6,5},{9,10},{10,9},{13,14},{14,13},{17,18},{18,... | collective-permute-start | bytes 393224 | tf_op jit(solution)/shard_map/swap_slabs_1/ppermute | solution.py:27
  49.5 6.9 %bulk_last.1 = (f32[4,64,96,128]{3,2,1,0:T(8,128)}, f32[64,96,128]{2,1,0:T(8,128)S(1)}, f32[64,96,128]{2,1,0:T(8,128)S(1)}, f32[64,96,128]{2,1,0:T(8,128)S(1)}, f32[64,96,128]{2,1,0:T(8,128)S(1)}) custom-call(f32[6240,128]{1,0:T(8,128)S(1)} %get-tuple-element.85.refs_0_, f32[6240,128]{1,0:T(8,128)S(1)} %get-tuple-element.86.refs_1_, ...), custom_call_target="tpu_custom_call" | custom-call | tf_op jit(solution)/shard_map/bulk_last/pallas_call | solution.py:290
  56.4 2.0 %patch_last.1 = (f32[4,64,96,128]{3,2,1,0:T(8,128)}, f32[64,96,128]{2,1,0:T(8,128)S(1)}, f32[64,96,128]{2,1,0:T(8,128)S(1)}, f32[64,96,128]{2,1,0:T(8,128)S(1)}, f32[64,96,128]{2,1,0:T(8,128)S(1)}) custom-call(f32[4,64,96,128]{3,2,1,0:T(8,128)} %get-tuple-element.89.refs_0_, ...), custom_call_target="tpu_custom_call", output_to_operand_aliasing={{0}: (0, {}), {1}: (1, {}), {2}: (2, {}), {3}: (3, {}), {4}... | custom-call | tf_op jit(solution)/shard_map/patch_last/pallas_call | solution.py:290
  (19 shorter events, 0.0 us)
Async XLA Ops:
  0.0 11.9 %copy-start = (f32[4,64,96,128]{3,2,1,0:T(8,128)S(1)}, f32[4,64,96,128]{3,2,1,0:T(8,128)}, u32[]{:S(2)}) copy-start(f32[4,64,96,128]{3,2,1,0:T(8,128)} %refs_5_.5) | copy-start | bytes 37748740
  3.0 8.9 %collective-permute-start = (f32[64,96,128]{2,1,0:T(8,128)S(1)}, f32[64,96,128]{2,1,0:T(8,128)S(1)}, u32[]{:S(2)}, u32[]{:S(2)}) collective-permute-start(f32[64,96,128]{2,1,0:T(8,128)S(1)} %get-tuple-element.52), channel_id=1, source_target_pairs={{0,16},{16,0},{1,17},{17,1},{2,18},{18,2},{3,19},{19,3},{4,20},{20... | collective-permute-start | bytes 9437192 | tf_op jit(solution)/shard_map/swap_rows_0/ppermute | solution.py:27
  3.7 14.8 %collective-permute-start.1 = (f32[4,96,128]{2,1,0:T(8,128)S(1)}, f32[4,96,128]{2,1,0:T(8,128)S(1)}, u32[]{:S(2)}, u32[]{:S(2)}) collective-permute-start(f32[4,96,128]{2,1,0:T(8,128)S(1)} %get-tuple-element.57), channel_id=1, source_target_pairs={{0,4},{8,12},{4,0},{12,8},{1,5},{9,13},{5,1},{13,9},{2,6},{10,14},... | collective-permute-start | bytes 589832 | tf_op jit(solution)/shard_map/swap_cols_0/ppermute | solution.py:27
  4.9 13.6 %collective-permute-start.2 = (f32[4,96,128]{2,1,0:T(8,128)S(1)}, f32[4,96,128]{2,1,0:T(8,128)S(1)}, u32[]{:S(2)}, u32[]{:S(2)}) collective-permute-start(f32[4,96,128]{2,1,0:T(8,128)S(1)} %get-tuple-element.58), channel_id=1, source_target_pairs={{4,8},{8,4},{5,9},{9,5},{6,10},{10,6},{7,11},{11,7},{20,24},{24,20... | collective-permute-start | bytes 589832 | tf_op jit(solution)/shard_map/swap_cols_1/ppermute | solution.py:27
  7.3 11.2 %collective-permute-start.3 = (f32[4,64,128]{2,1,0:T(8,128)S(1)}, f32[4,64,128]{2,1,0:T(8,128)S(1)}, u32[]{:S(2)}, u32[]{:S(2)}) collective-permute-start(f32[4,64,128]{2,1,0:T(8,128)S(1)} %get-tuple-element.59), channel_id=1, source_target_pairs={{0,1},{2,3},{1,0},{3,2},{4,5},{6,7},{5,4},{7,6},{8,9},{10,11},{9,8... | collective-permute-start | bytes 393224 | tf_op jit(solution)/shard_map/swap_slabs_0/ppermute | solution.py:27
  7.4 11.2 %collective-permute-start.4 = (f32[4,64,128]{2,1,0:T(8,128)S(1)}, f32[4,64,128]{2,1,0:T(8,128)S(1)}, u32[]{:S(2)}, u32[]{:S(2)}) collective-permute-start(f32[4,64,128]{2,1,0:T(8,128)S(1)} %get-tuple-element.60), channel_id=1, source_target_pairs={{1,2},{2,1},{5,6},{6,5},{9,10},{10,9},{13,14},{14,13},{17,18},{18,... | collective-permute-start | bytes 393224 | tf_op jit(solution)/shard_map/swap_slabs_1/ppermute | solution.py:27
  18.7 7.2 %collective-permute-start.5 = (f32[6240,128]{1,0:T(8,128)S(1)}, f32[6240,128]{1,0:T(8,128)S(1)}, u32[]{:S(2)}, u32[]{:S(2)}) collective-permute-start(f32[6240,128]{1,0:T(8,128)S(1)} %get-tuple-element.64.refs_3_), channel_id=1, source_target_pairs={{0,16},{16,0},{1,17},{17,1},{2,18},{18,2},{3,19},{19,3},{4,20},{20... | collective-permute-start | bytes 9584648 | tf_op jit(solution)/shard_map/swap_rows_0/ppermute | solution.py:27
  20.0 10.7 %collective-permute-start.6 = (f32[4,96,128]{2,1,0:T(8,128)S(1)}, f32[4,96,128]{2,1,0:T(8,128)S(1)}, u32[]{:S(2)}, u32[]{:S(2)}) collective-permute-start(f32[4,96,128]{2,1,0:T(8,128)S(1)} %get-tuple-element.69), channel_id=1, source_target_pairs={{0,4},{8,12},{4,0},{12,8},{1,5},{9,13},{5,1},{13,9},{2,6},{10,14},... | collective-permute-start | bytes 589832 | tf_op jit(solution)/shard_map/swap_cols_0/ppermute | solution.py:27
  20.0 11.4 %collective-permute-start.7 = (f32[4,96,128]{2,1,0:T(8,128)S(1)}, f32[4,96,128]{2,1,0:T(8,128)S(1)}, u32[]{:S(2)}, u32[]{:S(2)}) collective-permute-start(f32[4,96,128]{2,1,0:T(8,128)S(1)} %get-tuple-element.70), channel_id=1, source_target_pairs={{4,8},{8,4},{5,9},{9,5},{6,10},{10,6},{7,11},{11,7},{20,24},{24,20... | collective-permute-start | bytes 589832 | tf_op jit(solution)/shard_map/swap_cols_1/ppermute | solution.py:27
  23.9 6.7 %collective-permute-start.8 = (f32[4,64,128]{2,1,0:T(8,128)S(1)}, f32[4,64,128]{2,1,0:T(8,128)S(1)}, u32[]{:S(2)}, u32[]{:S(2)}) collective-permute-start(f32[4,64,128]{2,1,0:T(8,128)S(1)} %get-tuple-element.71), channel_id=1, source_target_pairs={{0,1},{2,3},{1,0},{3,2},{4,5},{6,7},{5,4},{7,6},{8,9},{10,11},{9,8... | collective-permute-start | bytes 393224 | tf_op jit(solution)/shard_map/swap_slabs_0/ppermute | solution.py:27
  24.0 6.7 %collective-permute-start.9 = (f32[4,64,128]{2,1,0:T(8,128)S(1)}, f32[4,64,128]{2,1,0:T(8,128)S(1)}, u32[]{:S(2)}, u32[]{:S(2)}) collective-permute-start(f32[4,64,128]{2,1,0:T(8,128)S(1)} %get-tuple-element.72), channel_id=1, source_target_pairs={{1,2},{2,1},{5,6},{6,5},{9,10},{10,9},{13,14},{14,13},{17,18},{18,... | collective-permute-start | bytes 393224 | tf_op jit(solution)/shard_map/swap_slabs_1/ppermute | solution.py:27
  31.5 6.1 %collective-permute-start.10 = (f32[6240,128]{1,0:T(8,128)S(1)}, f32[6240,128]{1,0:T(8,128)S(1)}, u32[]{:S(2)}, u32[]{:S(2)}) collective-permute-start(f32[6240,128]{1,0:T(8,128)S(1)} %get-tuple-element.76.refs_3_), channel_id=1, source_target_pairs={{0,16},{16,0},{1,17},{17,1},{2,18},{18,2},{3,19},{19,3},{4,20},{20... | collective-permute-start | bytes 9584648 | tf_op jit(solution)/shard_map/swap_rows_0/ppermute | solution.py:27
  32.2 10.1 %collective-permute-start.11 = (f32[4,96,128]{2,1,0:T(8,128)S(1)}, f32[4,96,128]{2,1,0:T(8,128)S(1)}, u32[]{:S(2)}, u32[]{:S(2)}) collective-permute-start(f32[4,96,128]{2,1,0:T(8,128)S(1)} %get-tuple-element.81), channel_id=1, source_target_pairs={{0,4},{8,12},{4,0},{12,8},{1,5},{9,13},{5,1},{13,9},{2,6},{10,14},... | collective-permute-start | bytes 589832 | tf_op jit(solution)/shard_map/swap_cols_0/ppermute | solution.py:27
  32.2 10.1 %collective-permute-start.12 = (f32[4,96,128]{2,1,0:T(8,128)S(1)}, f32[4,96,128]{2,1,0:T(8,128)S(1)}, u32[]{:S(2)}, u32[]{:S(2)}) collective-permute-start(f32[4,96,128]{2,1,0:T(8,128)S(1)} %get-tuple-element.82), channel_id=1, source_target_pairs={{4,8},{8,4},{5,9},{9,5},{6,10},{10,6},{7,11},{11,7},{20,24},{24,20... | collective-permute-start | bytes 589832 | tf_op jit(solution)/shard_map/swap_cols_1/ppermute | solution.py:27
  34.6 7.7 %collective-permute-start.13 = (f32[4,64,128]{2,1,0:T(8,128)S(1)}, f32[4,64,128]{2,1,0:T(8,128)S(1)}, u32[]{:S(2)}, u32[]{:S(2)}) collective-permute-start(f32[4,64,128]{2,1,0:T(8,128)S(1)} %get-tuple-element.83), channel_id=1, source_target_pairs={{0,1},{2,3},{1,0},{3,2},{4,5},{6,7},{5,4},{7,6},{8,9},{10,11},{9,8... | collective-permute-start | bytes 393224 | tf_op jit(solution)/shard_map/swap_slabs_0/ppermute | solution.py:27
  34.6 7.7 %collective-permute-start.14 = (f32[4,64,128]{2,1,0:T(8,128)S(1)}, f32[4,64,128]{2,1,0:T(8,128)S(1)}, u32[]{:S(2)}, u32[]{:S(2)}) collective-permute-start(f32[4,64,128]{2,1,0:T(8,128)S(1)} %get-tuple-element.84), channel_id=1, source_target_pairs={{1,2},{2,1},{5,6},{6,5},{9,10},{10,9},{13,14},{14,13},{17,18},{18,... | collective-permute-start | bytes 393224 | tf_op jit(solution)/shard_map/swap_slabs_1/ppermute | solution.py:27
  42.5 7.0 %collective-permute-start.15 = (f32[6240,128]{1,0:T(8,128)S(1)}, f32[6240,128]{1,0:T(8,128)S(1)}, u32[]{:S(2)}, u32[]{:S(2)}) collective-permute-start(f32[6240,128]{1,0:T(8,128)S(1)} %get-tuple-element.88.refs_3_), channel_id=1, source_target_pairs={{0,16},{16,0},{1,17},{17,1},{2,18},{18,2},{3,19},{19,3},{4,20},{20... | collective-permute-start | bytes 9584648 | tf_op jit(solution)/shard_map/swap_rows_0/ppermute | solution.py:27
  42.9 13.5 %collective-permute-start.16 = (f32[4,96,128]{2,1,0:T(8,128)S(1)}, f32[4,96,128]{2,1,0:T(8,128)S(1)}, u32[]{:S(2)}, u32[]{:S(2)}) collective-permute-start(f32[4,96,128]{2,1,0:T(8,128)S(1)} %get-tuple-element.94), channel_id=1, source_target_pairs={{0,4},{8,12},{4,0},{12,8},{1,5},{9,13},{5,1},{13,9},{2,6},{10,14},... | collective-permute-start | bytes 589832 | tf_op jit(solution)/shard_map/swap_cols_0/ppermute | solution.py:27
  42.9 13.5 %collective-permute-start.17 = (f32[4,96,128]{2,1,0:T(8,128)S(1)}, f32[4,96,128]{2,1,0:T(8,128)S(1)}, u32[]{:S(2)}, u32[]{:S(2)}) collective-permute-start(f32[4,96,128]{2,1,0:T(8,128)S(1)} %get-tuple-element.95), channel_id=1, source_target_pairs={{4,8},{8,4},{5,9},{9,5},{6,10},{10,6},{7,11},{11,7},{20,24},{24,20... | collective-permute-start | bytes 589832 | tf_op jit(solution)/shard_map/swap_cols_1/ppermute | solution.py:27
  46.7 9.6 %collective-permute-start.18 = (f32[4,64,128]{2,1,0:T(8,128)S(1)}, f32[4,64,128]{2,1,0:T(8,128)S(1)}, u32[]{:S(2)}, u32[]{:S(2)}) collective-permute-start(f32[4,64,128]{2,1,0:T(8,128)S(1)} %get-tuple-element.96), channel_id=1, source_target_pairs={{0,1},{2,3},{1,0},{3,2},{4,5},{6,7},{5,4},{7,6},{8,9},{10,11},{9,8... | collective-permute-start | bytes 393224 | tf_op jit(solution)/shard_map/swap_slabs_0/ppermute | solution.py:27
  46.8 9.5 %collective-permute-start.19 = (f32[4,64,128]{2,1,0:T(8,128)S(1)}, f32[4,64,128]{2,1,0:T(8,128)S(1)}, u32[]{:S(2)}, u32[]{:S(2)}) collective-permute-start(f32[4,64,128]{2,1,0:T(8,128)S(1)} %get-tuple-element.97), channel_id=1, source_target_pairs={{1,2},{2,1},{5,6},{6,5},{9,10},{10,9},{13,14},{14,13},{17,18},{18,... | collective-permute-start | bytes 393224 | tf_op jit(solution)/shard_map/swap_slabs_1/ppermute | solution.py:27

commit v3 on v2

--- a/solution.py
+++ b/solution.py
@@ -34,6 +34,10 @@
 
 def mirrored(j, parity, rows):
     return jnp.where(parity == 0, j, rows - 1 - j)
+
+
+def face_rows(n_y, rows):
+    return {rows - 1 if which == 0 else 0: which for which in range(n_y)}
 
 
 def pack_kernel(dims, counts, tracer, *refs):
@@ -73,27 +77,42 @@
         copy.wait()
 
 
+def together_of(nz):
+    return 2 if nz // SUB % 4 == 0 else 1
+
+
+def late_groups(nz):
+    groups, together = nz // SUB, together_of(nz)
+    return {0, *range(groups - 1 - together * (together - 1), groups, together)}
+
+
 def bulk_kernel(dims, counts, step, *refs):
     rows, nx, nz = dims
     first, last = step == 0, step == STEPS - 1
-    src, refs = (refs[:1], refs[1:]) if first else (refs[:rows], refs[rows:])
+    n_src = 1 + counts[0] if first else rows
+    src, refs = refs[:n_src], refs[n_src:]
     halos, refs = refs[: counts[0]], refs[counts[0] :]
     crowding, refs = refs[0], refs[1:]
     py = lax.rem(lax.axis_index("rows"), 2)
     order = [mirrored(j, py, rows) for j in range(rows)]
     pitch = nz + 1
     groups = nz // SUB
-    together = 2 if groups % 4 == 0 else 1
+    together = together_of(nz)
     span = together * together * SUB
     piece = together * SUB
     blocks = nz // span
     copies = []
     if first:
         outs, (cells, sems) = refs[:rows], refs[rows:]
+        held = face_rows(counts[0], rows)
+        fetched = [j for j in range(rows) if j not in held]
+        planes_of = [src[1 + held[j]] if j in held else cells.at[fetched.index(j)] for j in range(rows)]
         for k in range(nz // piece):
-            at = (slice(None), slice(None), pl.ds(k * piece, piece), slice(None))
-            copies.append(pltpu.make_async_copy(src[0].at[at], cells.at[at], sems.at[k]))
-            copies[-1].start()
+            for n, j in enumerate(fetched):
+                at = (slice(None), pl.ds(k * piece, piece), slice(None))
+                dst = cells.at[n].at[at]
+                copies.append(pltpu.make_async_copy(src[0].at[order[j]].at[at], dst, sems.at[k, n]))
+                copies[-1].start()
     elif last:
         done, outs, sems = refs[0], refs[1 : 1 + rows], refs[1 + rows]
     else:
@@ -114,7 +133,7 @@
         def load(k, j, x, shift):
             z = shifts[k]
             if first:
-                ref = cells.at[order[j]]
+                ref = planes_of[j]
                 if shift == 0:
                     return ref[x, pl.ds(z, SUB), :]
                 if edges[k] == shift:
@@ -191,7 +210,8 @@
             if top == nz:
                 edges[-1] = 1
             while landed * piece < min(top + 1, nz):
-                copies[landed].wait()
+                for n in range(len(fetched)):
+                    copies[landed * len(fetched) + n].wait()
                 landed += 1
             block(k * span, part, edges)
     elif last:
@@ -205,12 +225,18 @@
             for part in range(together):
                 block(pl.multiple_of(k * span, SUB), part, None)
                 for g in range(together):
-                    for j in range(rows):
-                        send(k * together * together + part + g * together, j).start()
+                    group = k * together * together + part + g * together
+                    early = [group != left for left in late_groups(nz)]
+
+                    @pl.when(functools.reduce(jnp.logical_and, early))
+                    def _():
+                        for j in range(rows):
+                            send(group, j).start()
 
         for group in range(groups):
-            for j in range(rows):
-                send(group, j).wait()
+            if group not in late_groups(nz):
+                for j in range(rows):
+                    send(group, j).wait()
     else:
 
         @pl.loop(0, blocks)
@@ -253,13 +279,14 @@
         copies.append(pltpu.make_async_copy(cells[j].at[at], done.at[order[j]].at[at], sem))
         copies[-1].start()
 
-    for which in range(n_z):
+    def patch_z(which):
         z = near(which, pz, nz)
         for j in range(rows):
             for x in range(0, nx, SUB):
                 at = (pl.ds(x * pitch + offset + z, SUB, stride=pitch), slice(None))
                 views[j][at] = views[j][at] + scaled(halo_z[which][j, pl.ds(x, SUB), :])
-    for which in range(n_x):
+
+    def patch_x(which):
         x = near(which, px, nx)
         for j in range(rows):
             for z in range(0, nz, SUB):
@@ -268,16 +295,29 @@
                 views[j][at] = value
                 if not last:
                     face_x[which][j, pl.ds(z, SUB), :] = value
+
     if last:
-        inner = pl.ds(SUB, nz - 2 * SUB)
-        for j in range(rows):
-            for z in (0, nz - SUB):
+        for group in sorted(late_groups(nz) - {0, nz // SUB - 1}):
+            for j in range(rows):
+                send(j, (pl.ds(1, nx - 2), pl.ds(group * SUB, SUB), slice(None)))
+        for which in range(2):
+            if which < n_x:
+                patch_x(which)
+            for j in range(rows):
+                send(j, (near(which, px, nx), pl.ds(SUB, nz - 2 * SUB), slice(None)))
+        for which in range(2):
+            if which < n_z:
+                patch_z(which)
+            z = pl.multiple_of(near(which, pz, nz // SUB) * SUB, SUB)
+            for j in range(rows):
                 send(j, (slice(None), pl.ds(z, SUB), slice(None)))
-            for x in (0, nx - 1):
-                send(j, (x, inner, slice(None)))
         for copy in copies:
             copy.wait()
         return
+    for which in range(n_z):
+        patch_z(which)
+    for which in range(n_x):
+        patch_x(which)
     for which in range(n_z):
         z = near(which, pz, nz)
         for j in range(rows):
@@ -332,19 +372,22 @@
         y_halos = [swap(face, "rows", k, sizes[0]) for k, face in enumerate(y_faces)]
         x_halos = [swap(face, "cols", k, sizes[1]) for k, face in enumerate(x_faces)]
         z_halos = [swap(face, "slabs", k, sizes[2]) for k, face in enumerate(z_faces)]
-        stage_sems = pltpu.SemaphoreType.DMA((nz // SUB,))
         kernel = functools.partial(bulk_kernel, dims, counts, step)
         args = (*state, *y_halos, crowding)
         if step == 0:
-            args = (pltpu.with_memory_space_constraint(tracer, pltpu.HBM), *args[1:])
+            args = (pltpu.with_memory_space_constraint(tracer, pltpu.HBM), *y_faces, *args[1:])
+            fetched = rows - len(face_rows(counts[0], rows))
             state = call(
                 kernel,
                 "bulk0",
                 [state_row] * rows,
                 args,
                 in_specs=[HBM_SPEC] + [VMEM_SPEC] * (len(args) - 1),
-                scratch=[pltpu.VMEM(tracer.shape, f32), stage_sems],
-                vmem=tracer.size * 4 // 2**20 + 1,
+                scratch=[
+                    pltpu.VMEM((fetched, nx, nz, species), f32),
+                    pltpu.SemaphoreType.DMA((nz // SUB, fetched)),
+                ],
+                vmem=tracer.size // rows * fetched * 4 // 2**20 + 1,
             )
         elif last:
             state = call(
@@ -370,7 +413,7 @@
                 in_specs=specs + [VMEM_SPEC] * (len(args) - len(specs)),
                 out_specs=specs,
                 aliases=aliases,
-                scratch=[pltpu.SemaphoreType.DMA((4 * rows,))],
+                scratch=[pltpu.SemaphoreType.DMA(((2 + len(late_groups(nz))) * rows,))],
             )[0]
         out_shape = [state_row] * rows + [x_face] * counts[1] + [z_face] * counts[2]
         patched = call(kernel, f"patch{step}", out_shape, args, aliases=aliases)

time: 58.7 us -> 57.6 us (0.981)
  Pallas kernels: 28.2 us -> 27.1 us
    pallas_call x9, Pallas kernels: 28.2 us -> 27.1 us  [call(): pl.pallas_call(kernel, name=name, out_shape=out_shape, in_specs=in_specs...]
  transfers between devices with their start and end apart: 20 -> 20, of which waited for: 2 -> 2; matrix products, arithmetic and copies ran while one was open for 0% -> 0% of each run, Pallas kernels for 39% -> 38%
where the time goes in v3:
time: 57.6 us; the launch traced here: 57.3 us
  starting transfers between devices  28.7 us (50%)
  Pallas kernels  27.1 us (47%)
  waiting for transfers between devices  1.19 us (2%)
    ppermute x20, starting transfers between devices, swap(): return lax.ppermute(face, axis, matchings(count)[which])  28.7 us
    pallas_call x9, Pallas kernels, call(): pl.pallas_call(kernel, name=name, out_shape=out_shape, in_specs=in_specs...  27.1 us
    ppermute x20, waiting for transfers between devices, swap(): return lax.ppermute(face, axis, matchings(count)[which])  1.19 us
  transfers between devices with their start and end apart: 20, of which 2 were waited for; matrix products, arithmetic and copies ran while one was open for 0% of the time, Pallas kernels for 38%

profile of v3, /device:TPU:13, one launch (start us, length us, event | category | flops | bytes accessed | tf_op | source)
XLA Modules:
  0.0 57.3 jit_solution(7827886502137586254)
XLA Ops:
  0.0 3.0 %pack.1 = (f32[64,96,128]{2,1,0:T(8,128)S(1)}, f32[4,96,128]{2,1,0:T(8,128)S(1)}, f32[4,96,128]{2,1,0:T(8,128)S(1)}, f32[4,64,128]{2,1,0:T(8,128)S(1)}, f32[4,64,128]{2,1,0:T(8,128)S(1)}) custom-call(f32[4,64,96,128]{3,2,1,0:T(8,128)} %refs_0_.1), custom_call_target="tpu_custom_call" | custom-call | tf_op jit(solution)/shard_map/pack/pallas_call | solution.py:330
  3.0 0.7 %collective-permute-start = (f32[64,96,128]{2,1,0:T(8,128)S(1)}, f32[64,96,128]{2,1,0:T(8,128)S(1)}, u32[]{:S(2)}, u32[]{:S(2)}) collective-permute-start(f32[64,96,128]{2,1,0:T(8,128)S(1)} %get-tuple-element.52.refs_1_), channel_id=1, source_target_pairs={{0,16},{16,0},{1,17},{17,1},{2,18},{18,2},{3,19},{19,3},{4,20},{20... | collective-permute-start | bytes 9437192 | tf_op jit(solution)/shard_map/swap_rows_0/ppermute | solution.py:27
  3.7 1.2 %collective-permute-start.1 = (f32[4,96,128]{2,1,0:T(8,128)S(1)}, f32[4,96,128]{2,1,0:T(8,128)S(1)}, u32[]{:S(2)}, u32[]{:S(2)}) collective-permute-start(f32[4,96,128]{2,1,0:T(8,128)S(1)} %get-tuple-element.57), channel_id=1, source_target_pairs={{0,4},{8,12},{4,0},{12,8},{1,5},{9,13},{5,1},{13,9},{2,6},{10,14},... | collective-permute-start | bytes 589832 | tf_op jit(solution)/shard_map/swap_cols_0/ppermute | solution.py:27
  4.9 2.4 %collective-permute-start.2 = (f32[4,96,128]{2,1,0:T(8,128)S(1)}, f32[4,96,128]{2,1,0:T(8,128)S(1)}, u32[]{:S(2)}, u32[]{:S(2)}) collective-permute-start(f32[4,96,128]{2,1,0:T(8,128)S(1)} %get-tuple-element.58), channel_id=1, source_target_pairs={{4,8},{8,4},{5,9},{9,5},{6,10},{10,6},{7,11},{11,7},{20,24},{24,20... | collective-permute-start | bytes 589832 | tf_op jit(solution)/shard_map/swap_cols_1/ppermute | solution.py:27
  7.3 0.1 collective-permute-start.3
  7.4 4.5 %collective-permute-start.4 = (f32[4,64,128]{2,1,0:T(8,128)S(1)}, f32[4,64,128]{2,1,0:T(8,128)S(1)}, u32[]{:S(2)}, u32[]{:S(2)}) collective-permute-start(f32[4,64,128]{2,1,0:T(8,128)S(1)} %get-tuple-element.60), channel_id=1, source_target_pairs={{1,2},{2,1},{5,6},{6,5},{9,10},{10,9},{13,14},{14,13},{17,18},{18,... | collective-permute-start | bytes 393224 | tf_op jit(solution)/shard_map/swap_slabs_1/ppermute | solution.py:27
  11.9 6.5 %bulk0.1 = (f32[6240,128]{1,0:T(8,128)S(1)}, f32[6240,128]{1,0:T(8,128)S(1)}, f32[6240,128]{1,0:T(8,128)S(1)}, f32[6240,128]{1,0:T(8,128)S(1)}) custom-call(f32[4,64,96,128]{3,2,1,0:T(8,128)} %refs_0_.1, f32[64,96,128]{2,1,0:T(8,128)S(1)} %get-tuple-element.52.refs_1_, f32[64,96,128]{2,1,0:T(8,128)S(1)} %collective-permute-done.refs_2_, ...), custom_call_target="tpu_custom_call" | custom-call | tf_op jit(solution)/shard_map/bulk0/pallas_call | solution.py:330
  18.4 0.0 collective-permute-done.3.refs_6_
  18.4 0.0 collective-permute-done.1.refs_4_
  18.4 0.0 collective-permute-done.2.refs_5_
  18.4 0.1 patch0.1
  18.5 1.3 %collective-permute-start.5 = (f32[6240,128]{1,0:T(8,128)S(1)}, f32[6240,128]{1,0:T(8,128)S(1)}, u32[]{:S(2)}, u32[]{:S(2)}) collective-permute-start(f32[6240,128]{1,0:T(8,128)S(1)} %get-tuple-element.64.refs_3_), channel_id=1, source_target_pairs={{0,16},{16,0},{1,17},{17,1},{2,18},{18,2},{3,19},{19,3},{4,20},{20... | collective-permute-start | bytes 9584648 | tf_op jit(solution)/shard_map/swap_rows_0/ppermute | solution.py:27
  19.8 0.0 collective-permute-start.6
  19.8 3.9 %collective-permute-start.7 = (f32[4,96,128]{2,1,0:T(8,128)S(1)}, f32[4,96,128]{2,1,0:T(8,128)S(1)}, u32[]{:S(2)}, u32[]{:S(2)}) collective-permute-start(f32[4,96,128]{2,1,0:T(8,128)S(1)} %get-tuple-element.70), channel_id=1, source_target_pairs={{4,8},{8,4},{5,9},{9,5},{6,10},{10,6},{7,11},{11,7},{20,24},{24,20... | collective-permute-start | bytes 589832 | tf_op jit(solution)/shard_map/swap_cols_1/ppermute | solution.py:27
  23.7 0.1 collective-permute-start.8
  23.8 1.9 %collective-permute-start.9 = (f32[4,64,128]{2,1,0:T(8,128)S(1)}, f32[4,64,128]{2,1,0:T(8,128)S(1)}, u32[]{:S(2)}, u32[]{:S(2)}) collective-permute-start(f32[4,64,128]{2,1,0:T(8,128)S(1)} %get-tuple-element.72), channel_id=1, source_target_pairs={{1,2},{2,1},{5,6},{6,5},{9,10},{10,9},{13,14},{14,13},{17,18},{18,... | collective-permute-start | bytes 393224 | tf_op jit(solution)/shard_map/swap_slabs_1/ppermute | solution.py:27
  25.8 4.7 %bulk1.1 = (f32[6240,128]{1,0:T(8,128)S(1)}, f32[6240,128]{1,0:T(8,128)S(1)}, f32[6240,128]{1,0:T(8,128)S(1)}, f32[6240,128]{1,0:T(8,128)S(1)}) custom-call(f32[6240,128]{1,0:T(8,128)S(1)} %get-tuple-element.61.refs_0_, f32[6240,128]{1,0:T(8,128)S(1)} %get-tuple-element.62.refs_1_, f32[6240,128]{1,0:T(8,128)S(1)} %get-tuple-element.63.refs_2_, ...), custom_call_target="tpu_custom_call" | custom-call | tf_op jit(solution)/shard_map/bulk1/pallas_call | solution.py:330
  30.5 0.8 %collective-permute-done.7.refs_5_ = f32[4,96,128]{2,1,0:T(8,128)S(1)} collective-permute-done((f32[4,96,128]{2,1,0:T(8,128)S(1)}, f32[4,96,128]{2,1,0:T(8,128)S(1)}, u32[]{:S(2)}, u32[]{:S(2)}) %collective-permute-start.7) | collective-permute-done | bytes 196640 | tf_op jit(solution)/shard_map/swap_cols_1/ppermute | solution.py:27
  31.2 0.1 patch1.1
  31.4 0.7 %collective-permute-start.10 = (f32[6240,128]{1,0:T(8,128)S(1)}, f32[6240,128]{1,0:T(8,128)S(1)}, u32[]{:S(2)}, u32[]{:S(2)}) collective-permute-start(f32[6240,128]{1,0:T(8,128)S(1)} %get-tuple-element.76.refs_3_), channel_id=1, source_target_pairs={{0,16},{16,0},{1,17},{17,1},{2,18},{18,2},{3,19},{19,3},{4,20},{20... | collective-permute-start | bytes 9584648 | tf_op jit(solution)/shard_map/swap_rows_0/ppermute | solution.py:27
  32.1 2.3 %collective-permute-start.12 = (f32[4,96,128]{2,1,0:T(8,128)S(1)}, f32[4,96,128]{2,1,0:T(8,128)S(1)}, u32[]{:S(2)}, u32[]{:S(2)}) collective-permute-start(f32[4,96,128]{2,1,0:T(8,128)S(1)} %get-tuple-element.82), channel_id=1, source_target_pairs={{4,8},{8,4},{5,9},{9,5},{6,10},{10,6},{7,11},{11,7},{20,24},{24,20... | collective-permute-start | bytes 589832 | tf_op jit(solution)/shard_map/swap_cols_1/ppermute | solution.py:27
  34.4 0.1 collective-permute-start.13
  34.5 2.6 %collective-permute-start.14 = (f32[4,64,128]{2,1,0:T(8,128)S(1)}, f32[4,64,128]{2,1,0:T(8,128)S(1)}, u32[]{:S(2)}, u32[]{:S(2)}) collective-permute-start(f32[4,64,128]{2,1,0:T(8,128)S(1)} %get-tuple-element.84), channel_id=1, source_target_pairs={{1,2},{2,1},{5,6},{6,5},{9,10},{10,9},{13,14},{14,13},{17,18},{18,... | collective-permute-start | bytes 393224 | tf_op jit(solution)/shard_map/swap_slabs_1/ppermute | solution.py:27
  37.0 0.4 collective-permute-done.10.refs_4_
  37.4 4.7 %bulk2.1 = (f32[6240,128]{1,0:T(8,128)S(1)}, f32[6240,128]{1,0:T(8,128)S(1)}, f32[6240,128]{1,0:T(8,128)S(1)}, f32[6240,128]{1,0:T(8,128)S(1)}) custom-call(f32[6240,128]{1,0:T(8,128)S(1)} %get-tuple-element.73.refs_0_, f32[6240,128]{1,0:T(8,128)S(1)} %get-tuple-element.74.refs_1_, f32[6240,128]{1,0:T(8,128)S(1)} %get-tuple-element.75.refs_2_, ...), custom_call_target="tpu_custom_call" | custom-call | tf_op jit(solution)/shard_map/bulk2/pallas_call | solution.py:330
  42.2 0.1 patch2.1
  42.3 0.5 collective-permute-start.15
  42.8 3.8 %collective-permute-start.17 = (f32[4,96,128]{2,1,0:T(8,128)S(1)}, f32[4,96,128]{2,1,0:T(8,128)S(1)}, u32[]{:S(2)}, u32[]{:S(2)}) collective-permute-start(f32[4,96,128]{2,1,0:T(8,128)S(1)} %get-tuple-element.95), channel_id=1, source_target_pairs={{4,8},{8,4},{5,9},{9,5},{6,10},{10,6},{7,11},{11,7},{20,24},{24,20... | collective-permute-start | bytes 589832 | tf_op jit(solution)/shard_map/swap_cols_1/ppermute | solution.py:27
  46.6 0.1 collective-permute-start.18
  46.7 2.6 %collective-permute-start.19 = (f32[4,64,128]{2,1,0:T(8,128)S(1)}, f32[4,64,128]{2,1,0:T(8,128)S(1)}, u32[]{:S(2)}, u32[]{:S(2)}) collective-permute-start(f32[4,64,128]{2,1,0:T(8,128)S(1)} %get-tuple-element.97), channel_id=1, source_target_pairs={{1,2},{2,1},{5,6},{6,5},{9,10},{10,9},{13,14},{14,13},{17,18},{18,... | collective-permute-start | bytes 393224 | tf_op jit(solution)/shard_map/swap_slabs_1/ppermute | solution.py:27
  49.3 6.0 %bulk_last.1 = (f32[4,64,96,128]{3,2,1,0:T(8,128)}, f32[64,96,128]{2,1,0:T(8,128)S(1)}, f32[64,96,128]{2,1,0:T(8,128)S(1)}, f32[64,96,128]{2,1,0:T(8,128)S(1)}, f32[64,96,128]{2,1,0:T(8,128)S(1)}) custom-call(f32[6240,128]{1,0:T(8,128)S(1)} %get-tuple-element.85.refs_0_, f32[6240,128]{1,0:T(8,128)S(1)} %get-tuple-element.86.refs_1_, ...), custom_call_target="tpu_custom_call" | custom-call | tf_op jit(solution)/shard_map/bulk_last/pallas_call | solution.py:330
  55.4 1.9 %patch_last.1 = (f32[4,64,96,128]{3,2,1,0:T(8,128)}, f32[64,96,128]{2,1,0:T(8,128)S(1)}, f32[64,96,128]{2,1,0:T(8,128)S(1)}, f32[64,96,128]{2,1,0:T(8,128)S(1)}, f32[64,96,128]{2,1,0:T(8,128)S(1)}) custom-call(f32[4,64,96,128]{3,2,1,0:T(8,128)} %get-tuple-element.89.refs_0_, ...), custom_call_target="tpu_custom_call", output_to_operand_aliasing={{0}: (0, {}), {1}: (1, {}), {2}: (2, {}), {3}: (3, {}), {4}... | custom-call | tf_op jit(solution)/shard_map/patch_last/pallas_call | solution.py:330
  (19 shorter events, 0.0 us)
Async XLA Ops:
  0.0 11.9 %copy-start = (f32[4,64,96,128]{3,2,1,0:T(8,128)S(1)}, f32[4,64,96,128]{3,2,1,0:T(8,128)}, u32[]{:S(2)}) copy-start(f32[4,64,96,128]{3,2,1,0:T(8,128)} %refs_5_.5) | copy-start | bytes 37748740
  3.0 8.9 %collective-permute-start = (f32[64,96,128]{2,1,0:T(8,128)S(1)}, f32[64,96,128]{2,1,0:T(8,128)S(1)}, u32[]{:S(2)}, u32[]{:S(2)}) collective-permute-start(f32[64,96,128]{2,1,0:T(8,128)S(1)} %get-tuple-element.52.refs_1_), channel_id=1, source_target_pairs={{0,16},{16,0},{1,17},{17,1},{2,18},{18,2},{3,19},{19,3},{4,20},{20... | collective-permute-start | bytes 9437192 | tf_op jit(solution)/shard_map/swap_rows_0/ppermute | solution.py:27
  3.7 14.7 %collective-permute-start.1 = (f32[4,96,128]{2,1,0:T(8,128)S(1)}, f32[4,96,128]{2,1,0:T(8,128)S(1)}, u32[]{:S(2)}, u32[]{:S(2)}) collective-permute-start(f32[4,96,128]{2,1,0:T(8,128)S(1)} %get-tuple-element.57), channel_id=1, source_target_pairs={{0,4},{8,12},{4,0},{12,8},{1,5},{9,13},{5,1},{13,9},{2,6},{10,14},... | collective-permute-start | bytes 589832 | tf_op jit(solution)/shard_map/swap_cols_0/ppermute | solution.py:27
  4.9 13.5 %collective-permute-start.2 = (f32[4,96,128]{2,1,0:T(8,128)S(1)}, f32[4,96,128]{2,1,0:T(8,128)S(1)}, u32[]{:S(2)}, u32[]{:S(2)}) collective-permute-start(f32[4,96,128]{2,1,0:T(8,128)S(1)} %get-tuple-element.58), channel_id=1, source_target_pairs={{4,8},{8,4},{5,9},{9,5},{6,10},{10,6},{7,11},{11,7},{20,24},{24,20... | collective-permute-start | bytes 589832 | tf_op jit(solution)/shard_map/swap_cols_1/ppermute | solution.py:27
  7.3 11.1 %collective-permute-start.3 = (f32[4,64,128]{2,1,0:T(8,128)S(1)}, f32[4,64,128]{2,1,0:T(8,128)S(1)}, u32[]{:S(2)}, u32[]{:S(2)}) collective-permute-start(f32[4,64,128]{2,1,0:T(8,128)S(1)} %get-tuple-element.59), channel_id=1, source_target_pairs={{0,1},{2,3},{1,0},{3,2},{4,5},{6,7},{5,4},{7,6},{8,9},{10,11},{9,8... | collective-permute-start | bytes 393224 | tf_op jit(solution)/shard_map/swap_slabs_0/ppermute | solution.py:27
  7.4 11.0 %collective-permute-start.4 = (f32[4,64,128]{2,1,0:T(8,128)S(1)}, f32[4,64,128]{2,1,0:T(8,128)S(1)}, u32[]{:S(2)}, u32[]{:S(2)}) collective-permute-start(f32[4,64,128]{2,1,0:T(8,128)S(1)} %get-tuple-element.60), channel_id=1, source_target_pairs={{1,2},{2,1},{5,6},{6,5},{9,10},{10,9},{13,14},{14,13},{17,18},{18,... | collective-permute-start | bytes 393224 | tf_op jit(solution)/shard_map/swap_slabs_1/ppermute | solution.py:27
  18.5 7.2 %collective-permute-start.5 = (f32[6240,128]{1,0:T(8,128)S(1)}, f32[6240,128]{1,0:T(8,128)S(1)}, u32[]{:S(2)}, u32[]{:S(2)}) collective-permute-start(f32[6240,128]{1,0:T(8,128)S(1)} %get-tuple-element.64.refs_3_), channel_id=1, source_target_pairs={{0,16},{16,0},{1,17},{17,1},{2,18},{18,2},{3,19},{19,3},{4,20},{20... | collective-permute-start | bytes 9584648 | tf_op jit(solution)/shard_map/swap_rows_0/ppermute | solution.py:27
  19.8 10.7 %collective-permute-start.6 = (f32[4,96,128]{2,1,0:T(8,128)S(1)}, f32[4,96,128]{2,1,0:T(8,128)S(1)}, u32[]{:S(2)}, u32[]{:S(2)}) collective-permute-start(f32[4,96,128]{2,1,0:T(8,128)S(1)} %get-tuple-element.69), channel_id=1, source_target_pairs={{0,4},{8,12},{4,0},{12,8},{1,5},{9,13},{5,1},{13,9},{2,6},{10,14},... | collective-permute-start | bytes 589832 | tf_op jit(solution)/shard_map/swap_cols_0/ppermute | solution.py:27
  19.8 11.4 %collective-permute-start.7 = (f32[4,96,128]{2,1,0:T(8,128)S(1)}, f32[4,96,128]{2,1,0:T(8,128)S(1)}, u32[]{:S(2)}, u32[]{:S(2)}) collective-permute-start(f32[4,96,128]{2,1,0:T(8,128)S(1)} %get-tuple-element.70), channel_id=1, source_target_pairs={{4,8},{8,4},{5,9},{9,5},{6,10},{10,6},{7,11},{11,7},{20,24},{24,20... | collective-permute-start | bytes 589832 | tf_op jit(solution)/shard_map/swap_cols_1/ppermute | solution.py:27
  23.7 6.7 %collective-permute-start.8 = (f32[4,64,128]{2,1,0:T(8,128)S(1)}, f32[4,64,128]{2,1,0:T(8,128)S(1)}, u32[]{:S(2)}, u32[]{:S(2)}) collective-permute-start(f32[4,64,128]{2,1,0:T(8,128)S(1)} %get-tuple-element.71), channel_id=1, source_target_pairs={{0,1},{2,3},{1,0},{3,2},{4,5},{6,7},{5,4},{7,6},{8,9},{10,11},{9,8... | collective-permute-start | bytes 393224 | tf_op jit(solution)/shard_map/swap_slabs_0/ppermute | solution.py:27
  23.8 6.7 %collective-permute-start.9 = (f32[4,64,128]{2,1,0:T(8,128)S(1)}, f32[4,64,128]{2,1,0:T(8,128)S(1)}, u32[]{:S(2)}, u32[]{:S(2)}) collective-permute-start(f32[4,64,128]{2,1,0:T(8,128)S(1)} %get-tuple-element.72), channel_id=1, source_target_pairs={{1,2},{2,1},{5,6},{6,5},{9,10},{10,9},{13,14},{14,13},{17,18},{18,... | collective-permute-start | bytes 393224 | tf_op jit(solution)/shard_map/swap_slabs_1/ppermute | solution.py:27
  31.4 6.1 %collective-permute-start.10 = (f32[6240,128]{1,0:T(8,128)S(1)}, f32[6240,128]{1,0:T(8,128)S(1)}, u32[]{:S(2)}, u32[]{:S(2)}) collective-permute-start(f32[6240,128]{1,0:T(8,128)S(1)} %get-tuple-element.76.refs_3_), channel_id=1, source_target_pairs={{0,16},{16,0},{1,17},{17,1},{2,18},{18,2},{3,19},{19,3},{4,20},{20... | collective-permute-start | bytes 9584648 | tf_op jit(solution)/shard_map/swap_rows_0/ppermute | solution.py:27
  32.1 10.1 %collective-permute-start.11 = (f32[4,96,128]{2,1,0:T(8,128)S(1)}, f32[4,96,128]{2,1,0:T(8,128)S(1)}, u32[]{:S(2)}, u32[]{:S(2)}) collective-permute-start(f32[4,96,128]{2,1,0:T(8,128)S(1)} %get-tuple-element.81), channel_id=1, source_target_pairs={{0,4},{8,12},{4,0},{12,8},{1,5},{9,13},{5,1},{13,9},{2,6},{10,14},... | collective-permute-start | bytes 589832 | tf_op jit(solution)/shard_map/swap_cols_0/ppermute | solution.py:27
  32.1 10.1 %collective-permute-start.12 = (f32[4,96,128]{2,1,0:T(8,128)S(1)}, f32[4,96,128]{2,1,0:T(8,128)S(1)}, u32[]{:S(2)}, u32[]{:S(2)}) collective-permute-start(f32[4,96,128]{2,1,0:T(8,128)S(1)} %get-tuple-element.82), channel_id=1, source_target_pairs={{4,8},{8,4},{5,9},{9,5},{6,10},{10,6},{7,11},{11,7},{20,24},{24,20... | collective-permute-start | bytes 589832 | tf_op jit(solution)/shard_map/swap_cols_1/ppermute | solution.py:27
  34.4 7.7 %collective-permute-start.13 = (f32[4,64,128]{2,1,0:T(8,128)S(1)}, f32[4,64,128]{2,1,0:T(8,128)S(1)}, u32[]{:S(2)}, u32[]{:S(2)}) collective-permute-start(f32[4,64,128]{2,1,0:T(8,128)S(1)} %get-tuple-element.83), channel_id=1, source_target_pairs={{0,1},{2,3},{1,0},{3,2},{4,5},{6,7},{5,4},{7,6},{8,9},{10,11},{9,8... | collective-permute-start | bytes 393224 | tf_op jit(solution)/shard_map/swap_slabs_0/ppermute | solution.py:27
  34.5 7.7 %collective-permute-start.14 = (f32[4,64,128]{2,1,0:T(8,128)S(1)}, f32[4,64,128]{2,1,0:T(8,128)S(1)}, u32[]{:S(2)}, u32[]{:S(2)}) collective-permute-start(f32[4,64,128]{2,1,0:T(8,128)S(1)} %get-tuple-element.84), channel_id=1, source_target_pairs={{1,2},{2,1},{5,6},{6,5},{9,10},{10,9},{13,14},{14,13},{17,18},{18,... | collective-permute-start | bytes 393224 | tf_op jit(solution)/shard_map/swap_slabs_1/ppermute | solution.py:27
  42.3 7.0 %collective-permute-start.15 = (f32[6240,128]{1,0:T(8,128)S(1)}, f32[6240,128]{1,0:T(8,128)S(1)}, u32[]{:S(2)}, u32[]{:S(2)}) collective-permute-start(f32[6240,128]{1,0:T(8,128)S(1)} %get-tuple-element.88.refs_3_), channel_id=1, source_target_pairs={{0,16},{16,0},{1,17},{17,1},{2,18},{18,2},{3,19},{19,3},{4,20},{20... | collective-permute-start | bytes 9584648 | tf_op jit(solution)/shard_map/swap_rows_0/ppermute | solution.py:27
  42.8 12.6 %collective-permute-start.16 = (f32[4,96,128]{2,1,0:T(8,128)S(1)}, f32[4,96,128]{2,1,0:T(8,128)S(1)}, u32[]{:S(2)}, u32[]{:S(2)}) collective-permute-start(f32[4,96,128]{2,1,0:T(8,128)S(1)} %get-tuple-element.94), channel_id=1, source_target_pairs={{0,4},{8,12},{4,0},{12,8},{1,5},{9,13},{5,1},{13,9},{2,6},{10,14},... | collective-permute-start | bytes 589832 | tf_op jit(solution)/shard_map/swap_cols_0/ppermute | solution.py:27
  42.8 12.6 %collective-permute-start.17 = (f32[4,96,128]{2,1,0:T(8,128)S(1)}, f32[4,96,128]{2,1,0:T(8,128)S(1)}, u32[]{:S(2)}, u32[]{:S(2)}) collective-permute-start(f32[4,96,128]{2,1,0:T(8,128)S(1)} %get-tuple-element.95), channel_id=1, source_target_pairs={{4,8},{8,4},{5,9},{9,5},{6,10},{10,6},{7,11},{11,7},{20,24},{24,20... | collective-permute-start | bytes 589832 | tf_op jit(solution)/shard_map/swap_cols_1/ppermute | solution.py:27
  46.6 8.8 %collective-permute-start.18 = (f32[4,64,128]{2,1,0:T(8,128)S(1)}, f32[4,64,128]{2,1,0:T(8,128)S(1)}, u32[]{:S(2)}, u32[]{:S(2)}) collective-permute-start(f32[4,64,128]{2,1,0:T(8,128)S(1)} %get-tuple-element.96), channel_id=1, source_target_pairs={{0,1},{2,3},{1,0},{3,2},{4,5},{6,7},{5,4},{7,6},{8,9},{10,11},{9,8... | collective-permute-start | bytes 393224 | tf_op jit(solution)/shard_map/swap_slabs_0/ppermute | solution.py:27
  46.7 8.7 %collective-permute-start.19 = (f32[4,64,128]{2,1,0:T(8,128)S(1)}, f32[4,64,128]{2,1,0:T(8,128)S(1)}, u32[]{:S(2)}, u32[]{:S(2)}) collective-permute-start(f32[4,64,128]{2,1,0:T(8,128)S(1)} %get-tuple-element.97), channel_id=1, source_target_pairs={{1,2},{2,1},{5,6},{6,5},{9,10},{10,9},{13,14},{14,13},{17,18},{18,... | collective-permute-start | bytes 393224 | tf_op jit(solution)/shard_map/swap_slabs_1/ppermute | solution.py:27

commit v4 on v3

--- a/solution.py
+++ b/solution.py
@@ -43,37 +43,27 @@
 def pack_kernel(dims, counts, tracer, *refs):
     rows, nx, nz = dims
     n_y, n_x, n_z = counts
-    faces, (groups, sems) = refs[: sum(counts)], refs[sum(counts) :]
+    faces, sems = refs[: sum(counts)], refs[sum(counts)]
     y_faces, x_faces, z_faces = faces[:n_y], faces[n_y : n_y + n_x], faces[n_y + n_x :]
     py = lax.rem(lax.axis_index("rows"), 2)
     px = lax.rem(lax.axis_index("cols"), 2)
     pz = lax.rem(lax.axis_index("slabs"), 2)
     order = [mirrored(j, py, rows) for j in range(rows)]
-    z_copies, copies = [], []
-    for which in range(n_z):
-        z = pl.multiple_of(near(which, pz, nz // SUB) * SUB, SUB)
-        for j in range(rows):
-            z_copies.append((tracer.at[order[j], :, pl.ds(z, SUB), :], groups.at[which, j]))
+    copies = []
     for which in range(n_x):
         for j in range(rows):
             copies.append((tracer.at[order[j], near(which, px, nx)], x_faces[which].at[j]))
+    for which in range(n_z):
+        for j in range(rows):
+            copies.append((tracer.at[order[j], :, near(which, pz, nz)], z_faces[which].at[j]))
     for which in range(n_y):
         copies.append((tracer.at[order[rows - 1 if which == 0 else 0]], y_faces[which]))
     started = []
-    for k, (src, dst) in enumerate(z_copies + copies):
+    for k, (src, dst) in enumerate(copies):
         copy = pltpu.make_async_copy(src, dst, sems.at[k])
         copy.start()
         started.append(copy)
-    for copy in started[: len(z_copies)]:
-        copy.wait()
-    for which in range(n_z):
-        z = near(which, pz, SUB)
-        for j in range(rows):
-            cells = groups.at[which, j].reshape(nx * SUB, 128)
-            for x in range(0, nx, SUB):
-                face = cells[pl.ds(x * SUB + z, SUB, stride=SUB), :]
-                z_faces[which][j, pl.ds(x, SUB), :] = face
-    for copy in started[len(z_copies) :]:
+    for copy in started:
         copy.wait()
 
 
@@ -185,7 +175,7 @@
 
         planes, above, below = plane(0)
         carry = ([planes[k][1:] + [above[k]] for k in range(together)], planes, below)
-        unroll = max(k for k in range(1, 10) if (nx - 1) % k == 0)
+        unroll = max(k for k in range(1, 22) if (nx - 1) % k == 0)
 
         def body(i, carry):
             for k in range(unroll):
@@ -351,19 +341,17 @@
     x_face = pltpu.VMEM((rows, nz, species), f32)
     z_face = pltpu.VMEM((rows, nx, species), f32)
 
-    out_shape = [full_row] * counts[0] + [x_face] * counts[1] + [z_face] * counts[2]
+    thin = [(nx, nz, 1, species)] * counts[0] + [(rows, nz, 1, species)] * counts[1]
+    thin += [(rows, nx, 1, species)] * counts[2]
     packed = call(
         functools.partial(pack_kernel, dims, counts),
         "pack",
-        out_shape,
-        (pltpu.with_memory_space_constraint(tracer, pltpu.HBM),),
+        [pltpu.VMEM(shape, f32) for shape in thin],
+        (pltpu.with_memory_space_constraint(tracer.reshape(rows, nx, nz, 1, species), pltpu.HBM),),
         in_specs=[HBM_SPEC],
-        scratch=[
-            pltpu.VMEM((counts[2], rows, nx, SUB, species), f32),
-            pltpu.SemaphoreType.DMA((counts[0] + rows * (counts[1] + counts[2]),)),
-        ],
-        vmem=4,
+        scratch=[pltpu.SemaphoreType.DMA((counts[0] + rows * (counts[1] + counts[2]),))],
     )
+    packed = [face.reshape(face.shape[0], face.shape[1], species) for face in packed]
     y_faces, packed = packed[: counts[0]], packed[counts[0] :]
     x_faces, z_faces = packed[: counts[1]], packed[counts[1] :]
     state = [tracer]

time: 57.6 us -> 56.5 us (0.981)
  Pallas kernels: 27.1 us -> 25.9 us
    pallas_call x9, Pallas kernels: 27.1 us -> 25.9 us  [call(): pl.pallas_call(kernel, name=name, out_shape=out_shape, in_specs=in_specs...]
  transfers between devices with their start and end apart: 20 -> 20, of which waited for: 2 -> 3; matrix products, arithmetic and copies ran while one was open for 0% -> 0% of each run, Pallas kernels for 38% -> 37%
where the time goes in v4:
time: 56.5 us; the launch traced here: 56.3 us
  starting transfers between devices  28.5 us (50%)
  Pallas kernels  25.9 us (46%)
  waiting for transfers between devices  1.58 us (3%)
    ppermute x20, starting transfers between devices, swap(): return lax.ppermute(face, axis, matchings(count)[which])  28.5 us
    pallas_call x9, Pallas kernels, call(): pl.pallas_call(kernel, name=name, out_shape=out_shape, in_specs=in_specs...  25.9 us
    ppermute x20, waiting for transfers between devices, swap(): return lax.ppermute(face, axis, matchings(count)[which])  1.58 us
  transfers between devices with their start and end apart: 20, of which 3 were waited for; matrix products, arithmetic and copies ran while one was open for 0% of the time, Pallas kernels for 37%

profile of v4, /device:TPU:13, one launch (start us, length us, event | category | flops | bytes accessed | tf_op | source)
XLA Modules:
  0.0 56.3 jit_solution(17944688657251828039)
XLA Ops:
  0.0 2.5 %pack.1 = (f32[64,96,1,128]{3,2,1,0:T(1,128)S(1)}, f32[4,96,1,128]{3,2,1,0:T(1,128)S(1)}, f32[4,96,1,128]{3,2,1,0:T(1,128)S(1)}, f32[4,64,1,128]{3,2,1,0:T(1,128)S(1)}, f32[4,64,1,128]{3,2,1,0:T(1,128)S(1)}) custom-call(f32[4,64,96,1,128]{4,3,2,1,0:T(1,128)} %bitcast.12), custom_call_target="tpu_custom_call" | custom-call | tf_op jit(solution)/shard_map/pack/pallas_call | solution.py:320
  2.5 0.7 %collective-permute-start = (f32[64,96,128]{2,1,0:T(8,128)S(1)}, f32[64,96,128]{2,1,0:T(8,128)S(1)}, u32[]{:S(2)}, u32[]{:S(2)}) collective-permute-start(f32[64,96,128]{2,1,0:T(8,128)S(1)} %bitcast.6), channel_id=1, source_target_pairs={{0,16},{16,0},{1,17},{17,1},{2,18},{18,2},{3,19},{19,3},{4,20},{20... | collective-permute-start | bytes 9437192 | tf_op jit(solution)/shard_map/swap_rows_0/ppermute | solution.py:27
  3.3 1.2 %collective-permute-start.1 = (f32[4,96,128]{2,1,0:T(8,128)S(1)}, f32[4,96,128]{2,1,0:T(8,128)S(1)}, u32[]{:S(2)}, u32[]{:S(2)}) collective-permute-start(f32[4,96,128]{2,1,0:T(8,128)S(1)} %bitcast.9), channel_id=1, source_target_pairs={{0,4},{8,12},{4,0},{12,8},{1,5},{9,13},{5,1},{13,9},{2,6},{10,14},... | collective-permute-start | bytes 589832 | tf_op jit(solution)/shard_map/swap_cols_0/ppermute | solution.py:27
  4.5 2.4 %collective-permute-start.2 = (f32[4,96,128]{2,1,0:T(8,128)S(1)}, f32[4,96,128]{2,1,0:T(8,128)S(1)}, u32[]{:S(2)}, u32[]{:S(2)}) collective-permute-start(f32[4,96,128]{2,1,0:T(8,128)S(1)} %bitcast.8), channel_id=1, source_target_pairs={{4,8},{8,4},{5,9},{9,5},{6,10},{10,6},{7,11},{11,7},{20,24},{24,20... | collective-permute-start | bytes 589832 | tf_op jit(solution)/shard_map/swap_cols_1/ppermute | solution.py:27
  6.8 0.1 collective-permute-start.3
  6.9 4.5 %collective-permute-start.4 = (f32[4,64,128]{2,1,0:T(8,128)S(1)}, f32[4,64,128]{2,1,0:T(8,128)S(1)}, u32[]{:S(2)}, u32[]{:S(2)}) collective-permute-start(f32[4,64,128]{2,1,0:T(8,128)S(1)} %bitcast.10), channel_id=1, source_target_pairs={{1,2},{2,1},{5,6},{6,5},{9,10},{10,9},{13,14},{14,13},{17,18},{18,... | collective-permute-start | bytes 393224 | tf_op jit(solution)/shard_map/swap_slabs_1/ppermute | solution.py:27
  11.4 6.2 %bulk0.1 = (f32[6240,128]{1,0:T(8,128)S(1)}, f32[6240,128]{1,0:T(8,128)S(1)}, f32[6240,128]{1,0:T(8,128)S(1)}, f32[6240,128]{1,0:T(8,128)S(1)}) custom-call(f32[4,64,96,128]{3,2,1,0:T(8,128)} %refs_0_.1, f32[64,96,128]{2,1,0:T(8,128)S(1)} %bitcast.7, f32[64,96,128]{2,1,0:T(8,128)S(1)} %collective-permute-done.refs_2_, f32[4,64,96,128]{3,2,1,0:T(8,128)S(1)} %copy-done), custom_call_target="tpu_custom_call" | custom-call | tf_op jit(solution)/shard_map/bulk0/pallas_call | solution.py:320
  17.7 0.0 collective-permute-done.4.refs_7_
  17.7 0.0 collective-permute-done.1.refs_4_
  17.7 0.1 patch0.1
  17.8 1.3 %collective-permute-start.5 = (f32[6240,128]{1,0:T(8,128)S(1)}, f32[6240,128]{1,0:T(8,128)S(1)}, u32[]{:S(2)}, u32[]{:S(2)}) collective-permute-start(f32[6240,128]{1,0:T(8,128)S(1)} %get-tuple-element.64.refs_3_), channel_id=1, source_target_pairs={{0,16},{16,0},{1,17},{17,1},{2,18},{18,2},{3,19},{19,3},{4,20},{20... | collective-permute-start | bytes 9584648 | tf_op jit(solution)/shard_map/swap_rows_0/ppermute | solution.py:27
  19.1 3.9 %collective-permute-start.7 = (f32[4,96,128]{2,1,0:T(8,128)S(1)}, f32[4,96,128]{2,1,0:T(8,128)S(1)}, u32[]{:S(2)}, u32[]{:S(2)}) collective-permute-start(f32[4,96,128]{2,1,0:T(8,128)S(1)} %get-tuple-element.70), channel_id=1, source_target_pairs={{4,8},{8,4},{5,9},{9,5},{6,10},{10,6},{7,11},{11,7},{20,24},{24,20... | collective-permute-start | bytes 589832 | tf_op jit(solution)/shard_map/swap_cols_1/ppermute | solution.py:27
  23.0 0.1 collective-permute-start.8
  23.1 1.9 %collective-permute-start.9 = (f32[4,64,128]{2,1,0:T(8,128)S(1)}, f32[4,64,128]{2,1,0:T(8,128)S(1)}, u32[]{:S(2)}, u32[]{:S(2)}) collective-permute-start(f32[4,64,128]{2,1,0:T(8,128)S(1)} %get-tuple-element.72), channel_id=1, source_target_pairs={{1,2},{2,1},{5,6},{6,5},{9,10},{10,9},{13,14},{14,13},{17,18},{18,... | collective-permute-start | bytes 393224 | tf_op jit(solution)/shard_map/swap_slabs_1/ppermute | solution.py:27
  25.0 0.0 collective-permute-done.5.refs_4_
  25.0 4.5 %bulk1.1 = (f32[6240,128]{1,0:T(8,128)S(1)}, f32[6240,128]{1,0:T(8,128)S(1)}, f32[6240,128]{1,0:T(8,128)S(1)}, f32[6240,128]{1,0:T(8,128)S(1)}) custom-call(f32[6240,128]{1,0:T(8,128)S(1)} %get-tuple-element.61.refs_0_, f32[6240,128]{1,0:T(8,128)S(1)} %get-tuple-element.62.refs_1_, f32[6240,128]{1,0:T(8,128)S(1)} %get-tuple-element.63.refs_2_, ...), custom_call_target="tpu_custom_call" | custom-call | tf_op jit(solution)/shard_map/bulk1/pallas_call | solution.py:320
  29.6 0.1 collective-permute-done.9.refs_7_
  29.7 0.9 %collective-permute-done.7.refs_5_ = f32[4,96,128]{2,1,0:T(8,128)S(1)} collective-permute-done((f32[4,96,128]{2,1,0:T(8,128)S(1)}, f32[4,96,128]{2,1,0:T(8,128)S(1)}, u32[]{:S(2)}, u32[]{:S(2)}) %collective-permute-start.7) | collective-permute-done | bytes 196640 | tf_op jit(solution)/shard_map/swap_cols_1/ppermute | solution.py:27
  30.5 0.1 patch1.1
  30.6 0.7 %collective-permute-start.10 = (f32[6240,128]{1,0:T(8,128)S(1)}, f32[6240,128]{1,0:T(8,128)S(1)}, u32[]{:S(2)}, u32[]{:S(2)}) collective-permute-start(f32[6240,128]{1,0:T(8,128)S(1)} %get-tuple-element.76.refs_3_), channel_id=1, source_target_pairs={{0,16},{16,0},{1,17},{17,1},{2,18},{18,2},{3,19},{19,3},{4,20},{20... | collective-permute-start | bytes 9584648 | tf_op jit(solution)/shard_map/swap_rows_0/ppermute | solution.py:27
  31.4 2.2 %collective-permute-start.12 = (f32[4,96,128]{2,1,0:T(8,128)S(1)}, f32[4,96,128]{2,1,0:T(8,128)S(1)}, u32[]{:S(2)}, u32[]{:S(2)}) collective-permute-start(f32[4,96,128]{2,1,0:T(8,128)S(1)} %get-tuple-element.82), channel_id=1, source_target_pairs={{4,8},{8,4},{5,9},{9,5},{6,10},{10,6},{7,11},{11,7},{20,24},{24,20... | collective-permute-start | bytes 589832 | tf_op jit(solution)/shard_map/swap_cols_1/ppermute | solution.py:27
  33.6 0.1 collective-permute-start.13
  33.7 2.5 %collective-permute-start.14 = (f32[4,64,128]{2,1,0:T(8,128)S(1)}, f32[4,64,128]{2,1,0:T(8,128)S(1)}, u32[]{:S(2)}, u32[]{:S(2)}) collective-permute-start(f32[4,64,128]{2,1,0:T(8,128)S(1)} %get-tuple-element.84), channel_id=1, source_target_pairs={{1,2},{2,1},{5,6},{6,5},{9,10},{10,9},{13,14},{14,13},{17,18},{18,... | collective-permute-start | bytes 393224 | tf_op jit(solution)/shard_map/swap_slabs_1/ppermute | solution.py:27
  36.1 0.6 %collective-permute-done.10.refs_4_ = f32[6240,128]{1,0:T(8,128)S(1)} collective-permute-done((f32[6240,128]{1,0:T(8,128)S(1)}, f32[6240,128]{1,0:T(8,128)S(1)}, u32[]{:S(2)}, u32[]{:S(2)}) %collective-permute-start.10) | collective-permute-done | bytes 3194912 | tf_op jit(solution)/shard_map/swap_rows_0/ppermute | solution.py:27
  36.7 4.5 %bulk2.1 = (f32[6240,128]{1,0:T(8,128)S(1)}, f32[6240,128]{1,0:T(8,128)S(1)}, f32[6240,128]{1,0:T(8,128)S(1)}, f32[6240,128]{1,0:T(8,128)S(1)}) custom-call(f32[6240,128]{1,0:T(8,128)S(1)} %get-tuple-element.73.refs_0_, f32[6240,128]{1,0:T(8,128)S(1)} %get-tuple-element.74.refs_1_, f32[6240,128]{1,0:T(8,128)S(1)} %get-tuple-element.75.refs_2_, ...), custom_call_target="tpu_custom_call" | custom-call | tf_op jit(solution)/shard_map/bulk2/pallas_call | solution.py:320
  41.3 0.1 patch2.1
  41.4 0.5 collective-permute-start.15
  41.9 3.9 %collective-permute-start.17 = (f32[4,96,128]{2,1,0:T(8,128)S(1)}, f32[4,96,128]{2,1,0:T(8,128)S(1)}, u32[]{:S(2)}, u32[]{:S(2)}) collective-permute-start(f32[4,96,128]{2,1,0:T(8,128)S(1)} %get-tuple-element.95), channel_id=1, source_target_pairs={{4,8},{8,4},{5,9},{9,5},{6,10},{10,6},{7,11},{11,7},{20,24},{24,20... | collective-permute-start | bytes 589832 | tf_op jit(solution)/shard_map/swap_cols_1/ppermute | solution.py:27
  45.9 0.1 collective-permute-start.18
  45.9 2.5 %collective-permute-start.19 = (f32[4,64,128]{2,1,0:T(8,128)S(1)}, f32[4,64,128]{2,1,0:T(8,128)S(1)}, u32[]{:S(2)}, u32[]{:S(2)}) collective-permute-start(f32[4,64,128]{2,1,0:T(8,128)S(1)} %get-tuple-element.97), channel_id=1, source_target_pairs={{1,2},{2,1},{5,6},{6,5},{9,10},{10,9},{13,14},{14,13},{17,18},{18,... | collective-permute-start | bytes 393224 | tf_op jit(solution)/shard_map/swap_slabs_1/ppermute | solution.py:27
  48.4 5.9 %bulk_last.1 = (f32[4,64,96,128]{3,2,1,0:T(8,128)}, f32[64,96,128]{2,1,0:T(8,128)S(1)}, f32[64,96,128]{2,1,0:T(8,128)S(1)}, f32[64,96,128]{2,1,0:T(8,128)S(1)}, f32[64,96,128]{2,1,0:T(8,128)S(1)}) custom-call(f32[6240,128]{1,0:T(8,128)S(1)} %get-tuple-element.85.refs_0_, f32[6240,128]{1,0:T(8,128)S(1)} %get-tuple-element.86.refs_1_, ...), custom_call_target="tpu_custom_call" | custom-call | tf_op jit(solution)/shard_map/bulk_last/pallas_call | solution.py:320
  54.3 1.9 %patch_last.1 = (f32[4,64,96,128]{3,2,1,0:T(8,128)}, f32[64,96,128]{2,1,0:T(8,128)S(1)}, f32[64,96,128]{2,1,0:T(8,128)S(1)}, f32[64,96,128]{2,1,0:T(8,128)S(1)}, f32[64,96,128]{2,1,0:T(8,128)S(1)}) custom-call(f32[4,64,96,128]{3,2,1,0:T(8,128)} %get-tuple-element.89.refs_0_, ...), custom_call_target="tpu_custom_call", output_to_operand_aliasing={{0}: (0, {}), {1}: (1, {}), {2}: (2, {}), {3}: (3, {}), {4}... | custom-call | tf_op jit(solution)/shard_map/patch_last/pallas_call | solution.py:320
  (19 shorter events, 0.0 us)
Async XLA Ops:
  0.0 11.4 %copy-start = (f32[4,64,96,128]{3,2,1,0:T(8,128)S(1)}, f32[4,64,96,128]{3,2,1,0:T(8,128)}, u32[]{:S(2)}) copy-start(f32[4,64,96,128]{3,2,1,0:T(8,128)} %refs_5_.5) | copy-start | bytes 37748740
  2.5 8.9 %collective-permute-start = (f32[64,96,128]{2,1,0:T(8,128)S(1)}, f32[64,96,128]{2,1,0:T(8,128)S(1)}, u32[]{:S(2)}, u32[]{:S(2)}) collective-permute-start(f32[64,96,128]{2,1,0:T(8,128)S(1)} %bitcast.6), channel_id=1, source_target_pairs={{0,16},{16,0},{1,17},{17,1},{2,18},{18,2},{3,19},{19,3},{4,20},{20... | collective-permute-start | bytes 9437192 | tf_op jit(solution)/shard_map/swap_rows_0/ppermute | solution.py:27
  3.3 14.4 %collective-permute-start.1 = (f32[4,96,128]{2,1,0:T(8,128)S(1)}, f32[4,96,128]{2,1,0:T(8,128)S(1)}, u32[]{:S(2)}, u32[]{:S(2)}) collective-permute-start(f32[4,96,128]{2,1,0:T(8,128)S(1)} %bitcast.9), channel_id=1, source_target_pairs={{0,4},{8,12},{4,0},{12,8},{1,5},{9,13},{5,1},{13,9},{2,6},{10,14},... | collective-permute-start | bytes 589832 | tf_op jit(solution)/shard_map/swap_cols_0/ppermute | solution.py:27
  4.5 13.2 %collective-permute-start.2 = (f32[4,96,128]{2,1,0:T(8,128)S(1)}, f32[4,96,128]{2,1,0:T(8,128)S(1)}, u32[]{:S(2)}, u32[]{:S(2)}) collective-permute-start(f32[4,96,128]{2,1,0:T(8,128)S(1)} %bitcast.8), channel_id=1, source_target_pairs={{4,8},{8,4},{5,9},{9,5},{6,10},{10,6},{7,11},{11,7},{20,24},{24,20... | collective-permute-start | bytes 589832 | tf_op jit(solution)/shard_map/swap_cols_1/ppermute | solution.py:27
  6.8 10.8 %collective-permute-start.3 = (f32[4,64,128]{2,1,0:T(8,128)S(1)}, f32[4,64,128]{2,1,0:T(8,128)S(1)}, u32[]{:S(2)}, u32[]{:S(2)}) collective-permute-start(f32[4,64,128]{2,1,0:T(8,128)S(1)} %bitcast.11), channel_id=1, source_target_pairs={{0,1},{2,3},{1,0},{3,2},{4,5},{6,7},{5,4},{7,6},{8,9},{10,11},{9,8... | collective-permute-start | bytes 393224 | tf_op jit(solution)/shard_map/swap_slabs_0/ppermute | solution.py:27
  6.9 10.7 %collective-permute-start.4 = (f32[4,64,128]{2,1,0:T(8,128)S(1)}, f32[4,64,128]{2,1,0:T(8,128)S(1)}, u32[]{:S(2)}, u32[]{:S(2)}) collective-permute-start(f32[4,64,128]{2,1,0:T(8,128)S(1)} %bitcast.10), channel_id=1, source_target_pairs={{1,2},{2,1},{5,6},{6,5},{9,10},{10,9},{13,14},{14,13},{17,18},{18,... | collective-permute-start | bytes 393224 | tf_op jit(solution)/shard_map/swap_slabs_1/ppermute | solution.py:27
  17.8 7.2 %collective-permute-start.5 = (f32[6240,128]{1,0:T(8,128)S(1)}, f32[6240,128]{1,0:T(8,128)S(1)}, u32[]{:S(2)}, u32[]{:S(2)}) collective-permute-start(f32[6240,128]{1,0:T(8,128)S(1)} %get-tuple-element.64.refs_3_), channel_id=1, source_target_pairs={{0,16},{16,0},{1,17},{17,1},{2,18},{18,2},{3,19},{19,3},{4,20},{20... | collective-permute-start | bytes 9584648 | tf_op jit(solution)/shard_map/swap_rows_0/ppermute | solution.py:27
  19.1 10.6 %collective-permute-start.6 = (f32[4,96,128]{2,1,0:T(8,128)S(1)}, f32[4,96,128]{2,1,0:T(8,128)S(1)}, u32[]{:S(2)}, u32[]{:S(2)}) collective-permute-start(f32[4,96,128]{2,1,0:T(8,128)S(1)} %get-tuple-element.69), channel_id=1, source_target_pairs={{0,4},{8,12},{4,0},{12,8},{1,5},{9,13},{5,1},{13,9},{2,6},{10,14},... | collective-permute-start | bytes 589832 | tf_op jit(solution)/shard_map/swap_cols_0/ppermute | solution.py:27
  19.1 11.4 %collective-permute-start.7 = (f32[4,96,128]{2,1,0:T(8,128)S(1)}, f32[4,96,128]{2,1,0:T(8,128)S(1)}, u32[]{:S(2)}, u32[]{:S(2)}) collective-permute-start(f32[4,96,128]{2,1,0:T(8,128)S(1)} %get-tuple-element.70), channel_id=1, source_target_pairs={{4,8},{8,4},{5,9},{9,5},{6,10},{10,6},{7,11},{11,7},{20,24},{24,20... | collective-permute-start | bytes 589832 | tf_op jit(solution)/shard_map/swap_cols_1/ppermute | solution.py:27
  23.0 6.5 %collective-permute-start.8 = (f32[4,64,128]{2,1,0:T(8,128)S(1)}, f32[4,64,128]{2,1,0:T(8,128)S(1)}, u32[]{:S(2)}, u32[]{:S(2)}) collective-permute-start(f32[4,64,128]{2,1,0:T(8,128)S(1)} %get-tuple-element.71), channel_id=1, source_target_pairs={{0,1},{2,3},{1,0},{3,2},{4,5},{6,7},{5,4},{7,6},{8,9},{10,11},{9,8... | collective-permute-start | bytes 393224 | tf_op jit(solution)/shard_map/swap_slabs_0/ppermute | solution.py:27
  23.1 6.6 %collective-permute-start.9 = (f32[4,64,128]{2,1,0:T(8,128)S(1)}, f32[4,64,128]{2,1,0:T(8,128)S(1)}, u32[]{:S(2)}, u32[]{:S(2)}) collective-permute-start(f32[4,64,128]{2,1,0:T(8,128)S(1)} %get-tuple-element.72), channel_id=1, source_target_pairs={{1,2},{2,1},{5,6},{6,5},{9,10},{10,9},{13,14},{14,13},{17,18},{18,... | collective-permute-start | bytes 393224 | tf_op jit(solution)/shard_map/swap_slabs_1/ppermute | solution.py:27
  30.6 6.1 %collective-permute-start.10 = (f32[6240,128]{1,0:T(8,128)S(1)}, f32[6240,128]{1,0:T(8,128)S(1)}, u32[]{:S(2)}, u32[]{:S(2)}) collective-permute-start(f32[6240,128]{1,0:T(8,128)S(1)} %get-tuple-element.76.refs_3_), channel_id=1, source_target_pairs={{0,16},{16,0},{1,17},{17,1},{2,18},{18,2},{3,19},{19,3},{4,20},{20... | collective-permute-start | bytes 9584648 | tf_op jit(solution)/shard_map/swap_rows_0/ppermute | solution.py:27
  31.4 9.9 %collective-permute-start.11 = (f32[4,96,128]{2,1,0:T(8,128)S(1)}, f32[4,96,128]{2,1,0:T(8,128)S(1)}, u32[]{:S(2)}, u32[]{:S(2)}) collective-permute-start(f32[4,96,128]{2,1,0:T(8,128)S(1)} %get-tuple-element.81), channel_id=1, source_target_pairs={{0,4},{8,12},{4,0},{12,8},{1,5},{9,13},{5,1},{13,9},{2,6},{10,14},... | collective-permute-start | bytes 589832 | tf_op jit(solution)/shard_map/swap_cols_0/ppermute | solution.py:27
  31.4 9.9 %collective-permute-start.12 = (f32[4,96,128]{2,1,0:T(8,128)S(1)}, f32[4,96,128]{2,1,0:T(8,128)S(1)}, u32[]{:S(2)}, u32[]{:S(2)}) collective-permute-start(f32[4,96,128]{2,1,0:T(8,128)S(1)} %get-tuple-element.82), channel_id=1, source_target_pairs={{4,8},{8,4},{5,9},{9,5},{6,10},{10,6},{7,11},{11,7},{20,24},{24,20... | collective-permute-start | bytes 589832 | tf_op jit(solution)/shard_map/swap_cols_1/ppermute | solution.py:27
  33.6 7.6 %collective-permute-start.13 = (f32[4,64,128]{2,1,0:T(8,128)S(1)}, f32[4,64,128]{2,1,0:T(8,128)S(1)}, u32[]{:S(2)}, u32[]{:S(2)}) collective-permute-start(f32[4,64,128]{2,1,0:T(8,128)S(1)} %get-tuple-element.83), channel_id=1, source_target_pairs={{0,1},{2,3},{1,0},{3,2},{4,5},{6,7},{5,4},{7,6},{8,9},{10,11},{9,8... | collective-permute-start | bytes 393224 | tf_op jit(solution)/shard_map/swap_slabs_0/ppermute | solution.py:27
  33.7 7.6 %collective-permute-start.14 = (f32[4,64,128]{2,1,0:T(8,128)S(1)}, f32[4,64,128]{2,1,0:T(8,128)S(1)}, u32[]{:S(2)}, u32[]{:S(2)}) collective-permute-start(f32[4,64,128]{2,1,0:T(8,128)S(1)} %get-tuple-element.84), channel_id=1, source_target_pairs={{1,2},{2,1},{5,6},{6,5},{9,10},{10,9},{13,14},{14,13},{17,18},{18,... | collective-permute-start | bytes 393224 | tf_op jit(solution)/shard_map/swap_slabs_1/ppermute | solution.py:27
  41.4 7.0 %collective-permute-start.15 = (f32[6240,128]{1,0:T(8,128)S(1)}, f32[6240,128]{1,0:T(8,128)S(1)}, u32[]{:S(2)}, u32[]{:S(2)}) collective-permute-start(f32[6240,128]{1,0:T(8,128)S(1)} %get-tuple-element.88.refs_3_), channel_id=1, source_target_pairs={{0,16},{16,0},{1,17},{17,1},{2,18},{18,2},{3,19},{19,3},{4,20},{20... | collective-permute-start | bytes 9584648 | tf_op jit(solution)/shard_map/swap_rows_0/ppermute | solution.py:27
  41.9 12.4 %collective-permute-start.16 = (f32[4,96,128]{2,1,0:T(8,128)S(1)}, f32[4,96,128]{2,1,0:T(8,128)S(1)}, u32[]{:S(2)}, u32[]{:S(2)}) collective-permute-start(f32[4,96,128]{2,1,0:T(8,128)S(1)} %get-tuple-element.94), channel_id=1, source_target_pairs={{0,4},{8,12},{4,0},{12,8},{1,5},{9,13},{5,1},{13,9},{2,6},{10,14},... | collective-permute-start | bytes 589832 | tf_op jit(solution)/shard_map/swap_cols_0/ppermute | solution.py:27
  41.9 12.4 %collective-permute-start.17 = (f32[4,96,128]{2,1,0:T(8,128)S(1)}, f32[4,96,128]{2,1,0:T(8,128)S(1)}, u32[]{:S(2)}, u32[]{:S(2)}) collective-permute-start(f32[4,96,128]{2,1,0:T(8,128)S(1)} %get-tuple-element.95), channel_id=1, source_target_pairs={{4,8},{8,4},{5,9},{9,5},{6,10},{10,6},{7,11},{11,7},{20,24},{24,20... | collective-permute-start | bytes 589832 | tf_op jit(solution)/shard_map/swap_cols_1/ppermute | solution.py:27
  45.9 8.4 %collective-permute-start.18 = (f32[4,64,128]{2,1,0:T(8,128)S(1)}, f32[4,64,128]{2,1,0:T(8,128)S(1)}, u32[]{:S(2)}, u32[]{:S(2)}) collective-permute-start(f32[4,64,128]{2,1,0:T(8,128)S(1)} %get-tuple-element.96), channel_id=1, source_target_pairs={{0,1},{2,3},{1,0},{3,2},{4,5},{6,7},{5,4},{7,6},{8,9},{10,11},{9,8... | collective-permute-start | bytes 393224 | tf_op jit(solution)/shard_map/swap_slabs_0/ppermute | solution.py:27
  45.9 8.4 %collective-permute-start.19 = (f32[4,64,128]{2,1,0:T(8,128)S(1)}, f32[4,64,128]{2,1,0:T(8,128)S(1)}, u32[]{:S(2)}, u32[]{:S(2)}) collective-permute-start(f32[4,64,128]{2,1,0:T(8,128)S(1)} %get-tuple-element.97), channel_id=1, source_target_pairs={{1,2},{2,1},{5,6},{6,5},{9,10},{10,9},{13,14},{14,13},{17,18},{18,... | collective-permute-start | bytes 393224 | tf_op jit(solution)/shard_map/swap_slabs_1/ppermute | solution.py:27

commit v5 on v4

--- a/solution.py
+++ b/solution.py
@@ -40,10 +40,18 @@
     return {rows - 1 if which == 0 else 0: which for which in range(n_y)}
 
 
+def fetched_rows(n_y, rows):
+    return [j for j in range(rows) if j not in face_rows(n_y, rows)]
+
+
+def preloaded(nz):
+    return min(together_of(nz) * 2 * SUB, nz)
+
+
 def pack_kernel(dims, counts, tracer, *refs):
     rows, nx, nz = dims
     n_y, n_x, n_z = counts
-    faces, sems = refs[: sum(counts)], refs[sum(counts)]
+    faces, (cells, sems) = refs[: sum(counts)], refs[sum(counts) :]
     y_faces, x_faces, z_faces = faces[:n_y], faces[n_y : n_y + n_x], faces[n_y + n_x :]
     py = lax.rem(lax.axis_index("rows"), 2)
     px = lax.rem(lax.axis_index("cols"), 2)
@@ -58,6 +66,9 @@
             copies.append((tracer.at[order[j], :, near(which, pz, nz)], z_faces[which].at[j]))
     for which in range(n_y):
         copies.append((tracer.at[order[rows - 1 if which == 0 else 0]], y_faces[which]))
+    ahead = pl.ds(0, preloaded(nz))
+    for n, j in enumerate(fetched_rows(n_y, rows)):
+        copies.append((tracer.at[order[j], :, ahead], cells.at[n, :, ahead]))
     started = []
     for k, (src, dst) in enumerate(copies):
         copy = pltpu.make_async_copy(src, dst, sems.at[k])
@@ -76,13 +87,17 @@
     return {0, *range(groups - 1 - together * (together - 1), groups, together)}
 
 
+def padded(nz):
+    return nz + SUB if nz % 16 == 0 else nz
+
+
 def bulk_kernel(dims, counts, step, *refs):
     rows, nx, nz = dims
     first, last = step == 0, step == STEPS - 1
     n_src = 1 + counts[0] if first else rows
     src, refs = refs[:n_src], refs[n_src:]
     halos, refs = refs[: counts[0]], refs[counts[0] :]
-    crowding, refs = refs[0], refs[1:]
+    crowding, refs = refs[0], refs[1 + first :]
     py = lax.rem(lax.axis_index("rows"), 2)
     order = [mirrored(j, py, rows) for j in range(rows)]
     pitch = nz + 1
@@ -94,10 +109,11 @@
     copies = []
     if first:
         outs, (cells, sems) = refs[:rows], refs[rows:]
+        landed = preloaded(nz) // piece
         held = face_rows(counts[0], rows)
-        fetched = [j for j in range(rows) if j not in held]
+        fetched = fetched_rows(counts[0], rows)
         planes_of = [src[1 + held[j]] if j in held else cells.at[fetched.index(j)] for j in range(rows)]
-        for k in range(nz // piece):
+        for k in range(landed, nz // piece):
             for n, j in enumerate(fetched):
                 at = (slice(None), pl.ds(k * piece, piece), slice(None))
                 dst = cells.at[n].at[at]
@@ -190,7 +206,7 @@
 
     parts = [(k, part) for k in range(blocks) for part in range(together)]
     if first:
-        landed = 0
+        early = landed
         for k, part in parts:
             base = k * span + part * SUB
             top = base + (together - 1) * piece + SUB
@@ -201,7 +217,7 @@
                 edges[-1] = 1
             while landed * piece < min(top + 1, nz):
                 for n in range(len(fetched)):
-                    copies[landed * len(fetched) + n].wait()
+                    copies[(landed - early) * len(fetched) + n].wait()
                 landed += 1
             block(k * span, part, edges)
     elif last:
@@ -250,12 +266,12 @@
     py = lax.rem(lax.axis_index("rows"), 2)
     px = lax.rem(lax.axis_index("cols"), 2)
     pz = lax.rem(lax.axis_index("slabs"), 2)
-    pitch = nz if last else nz + 1
+    pitch = padded(nz) if last else nz + 1
     offset = 0 if last else 1
 
     if last:
         order = [mirrored(j, py, rows) for j in range(rows)]
-        views = [cells[j].reshape(nx * nz, 128) for j in range(rows)]
+        views = [cells[j].reshape(nx * pitch, 128) for j in range(rows)]
     else:
         views = state
 
@@ -336,22 +352,25 @@
     counts = [len(matchings(size)) for size in sizes]
     pitch_rows = -(-(nx * (nz + 1) + SUB) // 32) * 32
     f32 = jnp.float32
-    full_row = pltpu.VMEM((nx, nz, species), f32)
+    padded_row = pltpu.VMEM((nx, padded(nz), species), f32)
     state_row = pltpu.VMEM((pitch_rows, species), f32)
     x_face = pltpu.VMEM((rows, nz, species), f32)
     z_face = pltpu.VMEM((rows, nx, species), f32)
 
     thin = [(nx, nz, 1, species)] * counts[0] + [(rows, nz, 1, species)] * counts[1]
     thin += [(rows, nx, 1, species)] * counts[2]
+    fetched = len(fetched_rows(counts[0], rows))
+    thin += [(fetched, nx, nz, 1, species)]
     packed = call(
         functools.partial(pack_kernel, dims, counts),
         "pack",
         [pltpu.VMEM(shape, f32) for shape in thin],
         (pltpu.with_memory_space_constraint(tracer.reshape(rows, nx, nz, 1, species), pltpu.HBM),),
         in_specs=[HBM_SPEC],
-        scratch=[pltpu.SemaphoreType.DMA((counts[0] + rows * (counts[1] + counts[2]),))],
+        scratch=[pltpu.SemaphoreType.DMA((rows * (1 + counts[1] + counts[2]),))],
     )
-    packed = [face.reshape(face.shape[0], face.shape[1], species) for face in packed]
+    packed = [face.reshape(*face.shape[:-2], species) for face in packed]
+    *packed, cells = packed
     y_faces, packed = packed[: counts[0]], packed[counts[0] :]
     x_faces, z_faces = packed[: counts[1]], packed[counts[1] :]
     state = [tracer]
@@ -363,25 +382,21 @@
         kernel = functools.partial(bulk_kernel, dims, counts, step)
         args = (*state, *y_halos, crowding)
         if step == 0:
-            args = (pltpu.with_memory_space_constraint(tracer, pltpu.HBM), *y_faces, *args[1:])
-            fetched = rows - len(face_rows(counts[0], rows))
+            args = (pltpu.with_memory_space_constraint(tracer, pltpu.HBM), *y_faces, *args[1:], cells)
             state = call(
                 kernel,
                 "bulk0",
-                [state_row] * rows,
+                [state_row] * rows + [pltpu.VMEM(cells.shape, f32)],
                 args,
                 in_specs=[HBM_SPEC] + [VMEM_SPEC] * (len(args) - 1),
-                scratch=[
-                    pltpu.VMEM((fetched, nx, nz, species), f32),
-                    pltpu.SemaphoreType.DMA((nz // SUB, fetched)),
-                ],
-                vmem=tracer.size // rows * fetched * 4 // 2**20 + 1,
-            )
+                aliases={len(args) - 1: rows},
+                scratch=[pltpu.SemaphoreType.DMA((nz // SUB, fetched))],
+            )[:rows]
         elif last:
             state = call(
                 kernel,
                 "bulk_last",
-                [pltpu.HBM(tracer.shape, f32)] + [full_row] * rows,
+                [pltpu.HBM(tracer.shape, f32)] + [padded_row] * rows,
                 args,
                 out_specs=[HBM_SPEC] + [VMEM_SPEC] * rows,
                 scratch=[pltpu.SemaphoreType.DMA((nz // SUB, rows))],
@@ -396,7 +411,7 @@
             return call(
                 kernel,
                 "patch_last",
-                [pltpu.HBM(tracer.shape, f32)] + [full_row] * rows,
+                [pltpu.HBM(tracer.shape, f32)] + [padded_row] * rows,
                 args,
                 in_specs=specs + [VMEM_SPEC] * (len(args) - len(specs)),
                 out_specs=specs,

time: 56.5 us -> 56.2 us (level)
  transfers between devices with their start and end apart: 20 -> 20, of which waited for: 3 -> 3; matrix products, arithmetic and copies ran while one was open for 0% -> 0% of each run, Pallas kernels for 37% -> 35%
where the time goes in v5:
time: 56.2 us; the launch traced here: 56 us
  starting transfers between devices  28.5 us (51%)
  Pallas kernels  25.6 us (46%)
  waiting for transfers between devices  1.58 us (3%)
    ppermute x20, starting transfers between devices, swap(): return lax.ppermute(face, axis, matchings(count)[which])  28.5 us
    pallas_call x9, Pallas kernels, call(): pl.pallas_call(kernel, name=name, out_shape=out_shape, in_specs=in_specs...  25.6 us
    ppermute x20, waiting for transfers between devices, swap(): return lax.ppermute(face, axis, matchings(count)[which])  1.58 us
  transfers between devices with their start and end apart: 20, of which 3 were waited for; matrix products, arithmetic and copies ran while one was open for 0% of the time, Pallas kernels for 35%

profile of v5, /device:TPU:13, one launch (start us, length us, event | category | flops | bytes accessed | tf_op | source)
XLA Modules:
  0.0 56.0 jit_solution(7100035221952287248)
XLA Ops:
  0.0 3.5 %pack.1 = (f32[64,96,1,128]{3,2,1,0:T(1,128)S(1)}, f32[4,96,1,128]{3,2,1,0:T(1,128)S(1)}, f32[4,96,1,128]{3,2,1,0:T(1,128)S(1)}, f32[4,64,1,128]{3,2,1,0:T(1,128...) custom-call(f32[4,64,96,1,128]{4,3,2,1,0:T(1,128)} %bitcast.14), custom_call_target="tpu_custom_call" | custom-call | tf_op jit(solution)/shard_map/pack/pallas_call | solution.py:336
  3.5 0.7 %collective-permute-start = (f32[64,96,128]{2,1,0:T(8,128)S(1)}, f32[64,96,128]{2,1,0:T(8,128)S(1)}, u32[]{:S(2)}, u32[]{:S(2)}) collective-permute-start(f32[64,96,128]{2,1,0:T(8,128)S(1)} %bitcast.8), channel_id=1, source_target_pairs={{0,16},{16,0},{1,17},{17,1},{2,18},{18,2},{3,19},{19,3},{4,20},{20... | collective-permute-start | bytes 9437192 | tf_op jit(solution)/shard_map/swap_rows_0/ppermute | solution.py:27
  4.2 1.2 %collective-permute-start.1 = (f32[4,96,128]{2,1,0:T(8,128)S(1)}, f32[4,96,128]{2,1,0:T(8,128)S(1)}, u32[]{:S(2)}, u32[]{:S(2)}) collective-permute-start(f32[4,96,128]{2,1,0:T(8,128)S(1)} %bitcast.11), channel_id=1, source_target_pairs={{0,4},{8,12},{4,0},{12,8},{1,5},{9,13},{5,1},{13,9},{2,6},{10,14},... | collective-permute-start | bytes 589832 | tf_op jit(solution)/shard_map/swap_cols_0/ppermute | solution.py:27
  5.4 2.4 %collective-permute-start.2 = (f32[4,96,128]{2,1,0:T(8,128)S(1)}, f32[4,96,128]{2,1,0:T(8,128)S(1)}, u32[]{:S(2)}, u32[]{:S(2)}) collective-permute-start(f32[4,96,128]{2,1,0:T(8,128)S(1)} %bitcast.10), channel_id=1, source_target_pairs={{4,8},{8,4},{5,9},{9,5},{6,10},{10,6},{7,11},{11,7},{20,24},{24,20... | collective-permute-start | bytes 589832 | tf_op jit(solution)/shard_map/swap_cols_1/ppermute | solution.py:27
  7.8 0.1 collective-permute-start.3
  7.9 4.5 %collective-permute-start.4 = (f32[4,64,128]{2,1,0:T(8,128)S(1)}, f32[4,64,128]{2,1,0:T(8,128)S(1)}, u32[]{:S(2)}, u32[]{:S(2)}) collective-permute-start(f32[4,64,128]{2,1,0:T(8,128)S(1)} %bitcast.12), channel_id=1, source_target_pairs={{1,2},{2,1},{5,6},{6,5},{9,10},{10,9},{13,14},{14,13},{17,18},{18,... | collective-permute-start | bytes 393224 | tf_op jit(solution)/shard_map/swap_slabs_1/ppermute | solution.py:27
  12.3 0.0 collective-permute-done.refs_2_
  12.4 5.0 %bulk0.1 = (f32[6240,128]{1,0:T(8,128)S(1)}, f32[6240,128]{1,0:T(8,128)S(1)}, f32[6240,128]{1,0:T(8,128)S(1)}, f32[6240,128]{1,0:T(8,128)S(1)}, f32[3,64,96,128]{3,2,1,0:T(8,128)S(1)}) custom-call(f32[4,64,96,128]{3,2,1,0:T(8,128)} %refs_0_.1, f32[64,96,128]{2,1,0:T(8,128)S(1)} %bitcast.9, ...), custom_call_target="tpu_custom_call", output_to_operand_aliasing={{4}: (4, {})} | custom-call | tf_op jit(solution)/shard_map/bulk0/pallas_call | solution.py:336
  17.4 0.0 collective-permute-done.3.refs_6_
  17.4 0.0 collective-permute-done.4.refs_7_
  17.4 0.1 patch0.1
  17.6 1.3 %collective-permute-start.5 = (f32[6240,128]{1,0:T(8,128)S(1)}, f32[6240,128]{1,0:T(8,128)S(1)}, u32[]{:S(2)}, u32[]{:S(2)}) collective-permute-start(f32[6240,128]{1,0:T(8,128)S(1)} %get-tuple-element.66.refs_3_), channel_id=1, source_target_pairs={{0,16},{16,0},{1,17},{17,1},{2,18},{18,2},{3,19},{19,3},{4,20},{20... | collective-permute-start | bytes 9584648 | tf_op jit(solution)/shard_map/swap_rows_0/ppermute | solution.py:27
  18.8 3.9 %collective-permute-start.7 = (f32[4,96,128]{2,1,0:T(8,128)S(1)}, f32[4,96,128]{2,1,0:T(8,128)S(1)}, u32[]{:S(2)}, u32[]{:S(2)}) collective-permute-start(f32[4,96,128]{2,1,0:T(8,128)S(1)} %get-tuple-element.72), channel_id=1, source_target_pairs={{4,8},{8,4},{5,9},{9,5},{6,10},{10,6},{7,11},{11,7},{20,24},{24,20... | collective-permute-start | bytes 589832 | tf_op jit(solution)/shard_map/swap_cols_1/ppermute | solution.py:27
  22.8 0.1 collective-permute-start.8
  22.9 1.9 %collective-permute-start.9 = (f32[4,64,128]{2,1,0:T(8,128)S(1)}, f32[4,64,128]{2,1,0:T(8,128)S(1)}, u32[]{:S(2)}, u32[]{:S(2)}) collective-permute-start(f32[4,64,128]{2,1,0:T(8,128)S(1)} %get-tuple-element.74), channel_id=1, source_target_pairs={{1,2},{2,1},{5,6},{6,5},{9,10},{10,9},{13,14},{14,13},{17,18},{18,... | collective-permute-start | bytes 393224 | tf_op jit(solution)/shard_map/swap_slabs_1/ppermute | solution.py:27
  24.8 4.5 %bulk1.1 = (f32[6240,128]{1,0:T(8,128)S(1)}, f32[6240,128]{1,0:T(8,128)S(1)}, f32[6240,128]{1,0:T(8,128)S(1)}, f32[6240,128]{1,0:T(8,128)S(1)}) custom-call(f32[6240,128]{1,0:T(8,128)S(1)} %get-tuple-element.63.refs_0_, f32[6240,128]{1,0:T(8,128)S(1)} %get-tuple-element.64.refs_1_, f32[6240,128]{1,0:T(8,128)S(1)} %get-tuple-element.65.refs_2_, ...), custom_call_target="tpu_custom_call" | custom-call | tf_op jit(solution)/shard_map/bulk1/pallas_call | solution.py:336
  29.3 0.1 collective-permute-done.9.refs_7_
  29.4 0.9 %collective-permute-done.7.refs_5_ = f32[4,96,128]{2,1,0:T(8,128)S(1)} collective-permute-done((f32[4,96,128]{2,1,0:T(8,128)S(1)}, f32[4,96,128]{2,1,0:T(8,128)S(1)}, u32[]{:S(2)}, u32[]{:S(2)}) %collective-permute-start.7) | collective-permute-done | bytes 196640 | tf_op jit(solution)/shard_map/swap_cols_1/ppermute | solution.py:27
  30.3 0.1 patch1.1
  30.4 0.7 %collective-permute-start.10 = (f32[6240,128]{1,0:T(8,128)S(1)}, f32[6240,128]{1,0:T(8,128)S(1)}, u32[]{:S(2)}, u32[]{:S(2)}) collective-permute-start(f32[6240,128]{1,0:T(8,128)S(1)} %get-tuple-element.78.refs_3_), channel_id=1, source_target_pairs={{0,16},{16,0},{1,17},{17,1},{2,18},{18,2},{3,19},{19,3},{4,20},{20... | collective-permute-start | bytes 9584648 | tf_op jit(solution)/shard_map/swap_rows_0/ppermute | solution.py:27
  31.1 2.2 %collective-permute-start.12 = (f32[4,96,128]{2,1,0:T(8,128)S(1)}, f32[4,96,128]{2,1,0:T(8,128)S(1)}, u32[]{:S(2)}, u32[]{:S(2)}) collective-permute-start(f32[4,96,128]{2,1,0:T(8,128)S(1)} %get-tuple-element.84), channel_id=1, source_target_pairs={{4,8},{8,4},{5,9},{9,5},{6,10},{10,6},{7,11},{11,7},{20,24},{24,20... | collective-permute-start | bytes 589832 | tf_op jit(solution)/shard_map/swap_cols_1/ppermute | solution.py:27
  33.3 0.1 collective-permute-start.13
  33.4 2.5 %collective-permute-start.14 = (f32[4,64,128]{2,1,0:T(8,128)S(1)}, f32[4,64,128]{2,1,0:T(8,128)S(1)}, u32[]{:S(2)}, u32[]{:S(2)}) collective-permute-start(f32[4,64,128]{2,1,0:T(8,128)S(1)} %get-tuple-element.86), channel_id=1, source_target_pairs={{1,2},{2,1},{5,6},{6,5},{9,10},{10,9},{13,14},{14,13},{17,18},{18,... | collective-permute-start | bytes 393224 | tf_op jit(solution)/shard_map/swap_slabs_1/ppermute | solution.py:27
  35.9 0.6 %collective-permute-done.10.refs_4_ = f32[6240,128]{1,0:T(8,128)S(1)} collective-permute-done((f32[6240,128]{1,0:T(8,128)S(1)}, f32[6240,128]{1,0:T(8,128)S(1)}, u32[]{:S(2)}, u32[]{:S(2)}) %collective-permute-start.10) | collective-permute-done | bytes 3194912 | tf_op jit(solution)/shard_map/swap_rows_0/ppermute | solution.py:27
  36.5 4.5 %bulk2.1 = (f32[6240,128]{1,0:T(8,128)S(1)}, f32[6240,128]{1,0:T(8,128)S(1)}, f32[6240,128]{1,0:T(8,128)S(1)}, f32[6240,128]{1,0:T(8,128)S(1)}) custom-call(f32[6240,128]{1,0:T(8,128)S(1)} %get-tuple-element.75.refs_0_, f32[6240,128]{1,0:T(8,128)S(1)} %get-tuple-element.76.refs_1_, f32[6240,128]{1,0:T(8,128)S(1)} %get-tuple-element.77.refs_2_, ...), custom_call_target="tpu_custom_call" | custom-call | tf_op jit(solution)/shard_map/bulk2/pallas_call | solution.py:336
  41.0 0.1 patch2.1
  41.1 0.5 collective-permute-start.15
  41.7 3.9 %collective-permute-start.17 = (f32[4,96,128]{2,1,0:T(8,128)S(1)}, f32[4,96,128]{2,1,0:T(8,128)S(1)}, u32[]{:S(2)}, u32[]{:S(2)}) collective-permute-start(f32[4,96,128]{2,1,0:T(8,128)S(1)} %get-tuple-element.97), channel_id=1, source_target_pairs={{4,8},{8,4},{5,9},{9,5},{6,10},{10,6},{7,11},{11,7},{20,24},{24,20... | collective-permute-start | bytes 589832 | tf_op jit(solution)/shard_map/swap_cols_1/ppermute | solution.py:27
  45.6 0.1 collective-permute-start.18
  45.7 2.5 %collective-permute-start.19 = (f32[4,64,128]{2,1,0:T(8,128)S(1)}, f32[4,64,128]{2,1,0:T(8,128)S(1)}, u32[]{:S(2)}, u32[]{:S(2)}) collective-permute-start(f32[4,64,128]{2,1,0:T(8,128)S(1)} %get-tuple-element.99), channel_id=1, source_target_pairs={{1,2},{2,1},{5,6},{6,5},{9,10},{10,9},{13,14},{14,13},{17,18},{18,... | collective-permute-start | bytes 393224 | tf_op jit(solution)/shard_map/swap_slabs_1/ppermute | solution.py:27
  48.2 5.8 %bulk_last.1 = (f32[4,64,96,128]{3,2,1,0:T(8,128)}, f32[64,104,128]{2,1,0:T(8,128)S(1)}, f32[64,104,128]{2,1,0:T(8,128)S(1)}, f32[64,104,128]{2,1,0:T(8,128)S(1)}, f32[64,104,128]{2,1,0:T(8,128)S(1)}) custom-call(f32[6240,128]{1,0:T(8,128)S(1)} %get-tuple-element.87.refs_0_, f32[6240,128]{1,0:T(8,128)S(1)} %get-tuple-element.88.refs_1_, ...), custom_call_target="tpu_custom_call" | custom-call | tf_op jit(solution)/shard_map/bulk_last/pallas_call | solution.py:336
  54.0 1.9 %patch_last.1 = (f32[4,64,96,128]{3,2,1,0:T(8,128)}, f32[64,104,128]{2,1,0:T(8,128)S(1)}, f32[64,104,128]{2,1,0:T(8,128)S(1)}, f32[64,104,128]{2,1,0:T(8,128)S(1)}, f32[64,104,128]{2,1,0:T(8,128)S(1)}) custom-call(f32[4,64,96,128]{3,2,1,0:T(8,128)} %get-tuple-element.91.refs_0_, ...), custom_call_target="tpu_custom_call", output_to_operand_aliasing={{0}: (0, {}), {1}: (1, {}), {2}: (2, {}), {3}: (3, {}), {4}... | custom-call | tf_op jit(solution)/shard_map/patch_last/pallas_call | solution.py:336
  (19 shorter events, 0.0 us)
Async XLA Ops:
  0.0 12.4 %copy-start = (f32[4,64,96,128]{3,2,1,0:T(8,128)S(1)}, f32[4,64,96,128]{3,2,1,0:T(8,128)}, u32[]{:S(2)}) copy-start(f32[4,64,96,128]{3,2,1,0:T(8,128)} %refs_5_.5) | copy-start | bytes 37748740
  3.5 8.9 %collective-permute-start = (f32[64,96,128]{2,1,0:T(8,128)S(1)}, f32[64,96,128]{2,1,0:T(8,128)S(1)}, u32[]{:S(2)}, u32[]{:S(2)}) collective-permute-start(f32[64,96,128]{2,1,0:T(8,128)S(1)} %bitcast.8), channel_id=1, source_target_pairs={{0,16},{16,0},{1,17},{17,1},{2,18},{18,2},{3,19},{19,3},{4,20},{20... | collective-permute-start | bytes 9437192 | tf_op jit(solution)/shard_map/swap_rows_0/ppermute | solution.py:27
  4.2 13.2 %collective-permute-start.1 = (f32[4,96,128]{2,1,0:T(8,128)S(1)}, f32[4,96,128]{2,1,0:T(8,128)S(1)}, u32[]{:S(2)}, u32[]{:S(2)}) collective-permute-start(f32[4,96,128]{2,1,0:T(8,128)S(1)} %bitcast.11), channel_id=1, source_target_pairs={{0,4},{8,12},{4,0},{12,8},{1,5},{9,13},{5,1},{13,9},{2,6},{10,14},... | collective-permute-start | bytes 589832 | tf_op jit(solution)/shard_map/swap_cols_0/ppermute | solution.py:27
  5.4 12.0 %collective-permute-start.2 = (f32[4,96,128]{2,1,0:T(8,128)S(1)}, f32[4,96,128]{2,1,0:T(8,128)S(1)}, u32[]{:S(2)}, u32[]{:S(2)}) collective-permute-start(f32[4,96,128]{2,1,0:T(8,128)S(1)} %bitcast.10), channel_id=1, source_target_pairs={{4,8},{8,4},{5,9},{9,5},{6,10},{10,6},{7,11},{11,7},{20,24},{24,20... | collective-permute-start | bytes 589832 | tf_op jit(solution)/shard_map/swap_cols_1/ppermute | solution.py:27
  7.8 9.6 %collective-permute-start.3 = (f32[4,64,128]{2,1,0:T(8,128)S(1)}, f32[4,64,128]{2,1,0:T(8,128)S(1)}, u32[]{:S(2)}, u32[]{:S(2)}) collective-permute-start(f32[4,64,128]{2,1,0:T(8,128)S(1)} %bitcast.13), channel_id=1, source_target_pairs={{0,1},{2,3},{1,0},{3,2},{4,5},{6,7},{5,4},{7,6},{8,9},{10,11},{9,8... | collective-permute-start | bytes 393224 | tf_op jit(solution)/shard_map/swap_slabs_0/ppermute | solution.py:27
  7.9 9.6 %collective-permute-start.4 = (f32[4,64,128]{2,1,0:T(8,128)S(1)}, f32[4,64,128]{2,1,0:T(8,128)S(1)}, u32[]{:S(2)}, u32[]{:S(2)}) collective-permute-start(f32[4,64,128]{2,1,0:T(8,128)S(1)} %bitcast.12), channel_id=1, source_target_pairs={{1,2},{2,1},{5,6},{6,5},{9,10},{10,9},{13,14},{14,13},{17,18},{18,... | collective-permute-start | bytes 393224 | tf_op jit(solution)/shard_map/swap_slabs_1/ppermute | solution.py:27
  17.6 7.2 %collective-permute-start.5 = (f32[6240,128]{1,0:T(8,128)S(1)}, f32[6240,128]{1,0:T(8,128)S(1)}, u32[]{:S(2)}, u32[]{:S(2)}) collective-permute-start(f32[6240,128]{1,0:T(8,128)S(1)} %get-tuple-element.66.refs_3_), channel_id=1, source_target_pairs={{0,16},{16,0},{1,17},{17,1},{2,18},{18,2},{3,19},{19,3},{4,20},{20... | collective-permute-start | bytes 9584648 | tf_op jit(solution)/shard_map/swap_rows_0/ppermute | solution.py:27
  18.8 10.6 %collective-permute-start.6 = (f32[4,96,128]{2,1,0:T(8,128)S(1)}, f32[4,96,128]{2,1,0:T(8,128)S(1)}, u32[]{:S(2)}, u32[]{:S(2)}) collective-permute-start(f32[4,96,128]{2,1,0:T(8,128)S(1)} %get-tuple-element.71), channel_id=1, source_target_pairs={{0,4},{8,12},{4,0},{12,8},{1,5},{9,13},{5,1},{13,9},{2,6},{10,14},... | collective-permute-start | bytes 589832 | tf_op jit(solution)/shard_map/swap_cols_0/ppermute | solution.py:27
  18.8 11.4 %collective-permute-start.7 = (f32[4,96,128]{2,1,0:T(8,128)S(1)}, f32[4,96,128]{2,1,0:T(8,128)S(1)}, u32[]{:S(2)}, u32[]{:S(2)}) collective-permute-start(f32[4,96,128]{2,1,0:T(8,128)S(1)} %get-tuple-element.72), channel_id=1, source_target_pairs={{4,8},{8,4},{5,9},{9,5},{6,10},{10,6},{7,11},{11,7},{20,24},{24,20... | collective-permute-start | bytes 589832 | tf_op jit(solution)/shard_map/swap_cols_1/ppermute | solution.py:27
  22.8 6.5 %collective-permute-start.8 = (f32[4,64,128]{2,1,0:T(8,128)S(1)}, f32[4,64,128]{2,1,0:T(8,128)S(1)}, u32[]{:S(2)}, u32[]{:S(2)}) collective-permute-start(f32[4,64,128]{2,1,0:T(8,128)S(1)} %get-tuple-element.73), channel_id=1, source_target_pairs={{0,1},{2,3},{1,0},{3,2},{4,5},{6,7},{5,4},{7,6},{8,9},{10,11},{9,8... | collective-permute-start | bytes 393224 | tf_op jit(solution)/shard_map/swap_slabs_0/ppermute | solution.py:27
  22.9 6.6 %collective-permute-start.9 = (f32[4,64,128]{2,1,0:T(8,128)S(1)}, f32[4,64,128]{2,1,0:T(8,128)S(1)}, u32[]{:S(2)}, u32[]{:S(2)}) collective-permute-start(f32[4,64,128]{2,1,0:T(8,128)S(1)} %get-tuple-element.74), channel_id=1, source_target_pairs={{1,2},{2,1},{5,6},{6,5},{9,10},{10,9},{13,14},{14,13},{17,18},{18,... | collective-permute-start | bytes 393224 | tf_op jit(solution)/shard_map/swap_slabs_1/ppermute | solution.py:27
  30.4 6.1 %collective-permute-start.10 = (f32[6240,128]{1,0:T(8,128)S(1)}, f32[6240,128]{1,0:T(8,128)S(1)}, u32[]{:S(2)}, u32[]{:S(2)}) collective-permute-start(f32[6240,128]{1,0:T(8,128)S(1)} %get-tuple-element.78.refs_3_), channel_id=1, source_target_pairs={{0,16},{16,0},{1,17},{17,1},{2,18},{18,2},{3,19},{19,3},{4,20},{20... | collective-permute-start | bytes 9584648 | tf_op jit(solution)/shard_map/swap_rows_0/ppermute | solution.py:27
  31.1 9.9 %collective-permute-start.11 = (f32[4,96,128]{2,1,0:T(8,128)S(1)}, f32[4,96,128]{2,1,0:T(8,128)S(1)}, u32[]{:S(2)}, u32[]{:S(2)}) collective-permute-start(f32[4,96,128]{2,1,0:T(8,128)S(1)} %get-tuple-element.83), channel_id=1, source_target_pairs={{0,4},{8,12},{4,0},{12,8},{1,5},{9,13},{5,1},{13,9},{2,6},{10,14},... | collective-permute-start | bytes 589832 | tf_op jit(solution)/shard_map/swap_cols_0/ppermute | solution.py:27
  31.1 9.9 %collective-permute-start.12 = (f32[4,96,128]{2,1,0:T(8,128)S(1)}, f32[4,96,128]{2,1,0:T(8,128)S(1)}, u32[]{:S(2)}, u32[]{:S(2)}) collective-permute-start(f32[4,96,128]{2,1,0:T(8,128)S(1)} %get-tuple-element.84), channel_id=1, source_target_pairs={{4,8},{8,4},{5,9},{9,5},{6,10},{10,6},{7,11},{11,7},{20,24},{24,20... | collective-permute-start | bytes 589832 | tf_op jit(solution)/shard_map/swap_cols_1/ppermute | solution.py:27
  33.3 7.6 %collective-permute-start.13 = (f32[4,64,128]{2,1,0:T(8,128)S(1)}, f32[4,64,128]{2,1,0:T(8,128)S(1)}, u32[]{:S(2)}, u32[]{:S(2)}) collective-permute-start(f32[4,64,128]{2,1,0:T(8,128)S(1)} %get-tuple-element.85), channel_id=1, source_target_pairs={{0,1},{2,3},{1,0},{3,2},{4,5},{6,7},{5,4},{7,6},{8,9},{10,11},{9,8... | collective-permute-start | bytes 393224 | tf_op jit(solution)/shard_map/swap_slabs_0/ppermute | solution.py:27
  33.4 7.6 %collective-permute-start.14 = (f32[4,64,128]{2,1,0:T(8,128)S(1)}, f32[4,64,128]{2,1,0:T(8,128)S(1)}, u32[]{:S(2)}, u32[]{:S(2)}) collective-permute-start(f32[4,64,128]{2,1,0:T(8,128)S(1)} %get-tuple-element.86), channel_id=1, source_target_pairs={{1,2},{2,1},{5,6},{6,5},{9,10},{10,9},{13,14},{14,13},{17,18},{18,... | collective-permute-start | bytes 393224 | tf_op jit(solution)/shard_map/swap_slabs_1/ppermute | solution.py:27
  41.1 7.0 %collective-permute-start.15 = (f32[6240,128]{1,0:T(8,128)S(1)}, f32[6240,128]{1,0:T(8,128)S(1)}, u32[]{:S(2)}, u32[]{:S(2)}) collective-permute-start(f32[6240,128]{1,0:T(8,128)S(1)} %get-tuple-element.90.refs_3_), channel_id=1, source_target_pairs={{0,16},{16,0},{1,17},{17,1},{2,18},{18,2},{3,19},{19,3},{4,20},{20... | collective-permute-start | bytes 9584648 | tf_op jit(solution)/shard_map/swap_rows_0/ppermute | solution.py:27
  41.7 12.3 %collective-permute-start.16 = (f32[4,96,128]{2,1,0:T(8,128)S(1)}, f32[4,96,128]{2,1,0:T(8,128)S(1)}, u32[]{:S(2)}, u32[]{:S(2)}) collective-permute-start(f32[4,96,128]{2,1,0:T(8,128)S(1)} %get-tuple-element.96), channel_id=1, source_target_pairs={{0,4},{8,12},{4,0},{12,8},{1,5},{9,13},{5,1},{13,9},{2,6},{10,14},... | collective-permute-start | bytes 589832 | tf_op jit(solution)/shard_map/swap_cols_0/ppermute | solution.py:27
  41.7 12.3 %collective-permute-start.17 = (f32[4,96,128]{2,1,0:T(8,128)S(1)}, f32[4,96,128]{2,1,0:T(8,128)S(1)}, u32[]{:S(2)}, u32[]{:S(2)}) collective-permute-start(f32[4,96,128]{2,1,0:T(8,128)S(1)} %get-tuple-element.97), channel_id=1, source_target_pairs={{4,8},{8,4},{5,9},{9,5},{6,10},{10,6},{7,11},{11,7},{20,24},{24,20... | collective-permute-start | bytes 589832 | tf_op jit(solution)/shard_map/swap_cols_1/ppermute | solution.py:27
  45.6 8.4 %collective-permute-start.18 = (f32[4,64,128]{2,1,0:T(8,128)S(1)}, f32[4,64,128]{2,1,0:T(8,128)S(1)}, u32[]{:S(2)}, u32[]{:S(2)}) collective-permute-start(f32[4,64,128]{2,1,0:T(8,128)S(1)} %get-tuple-element.98), channel_id=1, source_target_pairs={{0,1},{2,3},{1,0},{3,2},{4,5},{6,7},{5,4},{7,6},{8,9},{10,11},{9,8... | collective-permute-start | bytes 393224 | tf_op jit(solution)/shard_map/swap_slabs_0/ppermute | solution.py:27
  45.7 8.3 %collective-permute-start.19 = (f32[4,64,128]{2,1,0:T(8,128)S(1)}, f32[4,64,128]{2,1,0:T(8,128)S(1)}, u32[]{:S(2)}, u32[]{:S(2)}) collective-permute-start(f32[4,64,128]{2,1,0:T(8,128)S(1)} %get-tuple-element.99), channel_id=1, source_target_pairs={{1,2},{2,1},{5,6},{6,5},{9,10},{10,9},{13,14},{14,13},{17,18},{18,... | collective-permute-start | bytes 393224 | tf_op jit(solution)/shard_map/swap_slabs_1/ppermute | solution.py:27

commit v6 on v5

--- a/solution.py
+++ b/solution.py
@@ -109,13 +109,13 @@
     copies = []
     if first:
         outs, (cells, sems) = refs[:rows], refs[rows:]
-        landed = preloaded(nz) // piece
+        landed = preloaded(nz) // SUB
         held = face_rows(counts[0], rows)
         fetched = fetched_rows(counts[0], rows)
         planes_of = [src[1 + held[j]] if j in held else cells.at[fetched.index(j)] for j in range(rows)]
-        for k in range(landed, nz // piece):
+        for k in range(landed, nz // SUB):
             for n, j in enumerate(fetched):
-                at = (slice(None), pl.ds(k * piece, piece), slice(None))
+                at = (slice(None), pl.ds(k * SUB, SUB), slice(None))
                 dst = cells.at[n].at[at]
                 copies.append(pltpu.make_async_copy(src[0].at[order[j]].at[at], dst, sems.at[k, n]))
                 copies[-1].start()
@@ -215,7 +215,7 @@
                 edges[0] = -1
             if top == nz:
                 edges[-1] = 1
-            while landed * piece < min(top + 1, nz):
+            while landed * SUB < min(top + 1, nz):
                 for n in range(len(fetched)):
                     copies[(landed - early) * len(fetched) + n].wait()
                 landed += 1

time: 56.2 us -> 56.1 us (level)
  no operation moved by 1% of the time
where the time goes in v6:
time: 56.1 us; the launch traced here: 55.8 us
  starting transfers between devices  28.5 us (51%)
  Pallas kernels  25.4 us (45%)
  waiting for transfers between devices  1.58 us (3%)
    ppermute x20, starting transfers between devices, swap(): return lax.ppermute(face, axis, matchings(count)[which])  28.5 us
    pallas_call x9, Pallas kernels, call(): pl.pallas_call(kernel, name=name, out_shape=out_shape, in_specs=in_specs...  25.4 us
    ppermute x20, waiting for transfers between devices, swap(): return lax.ppermute(face, axis, matchings(count)[which])  1.58 us
  transfers between devices with their start and end apart: 20, of which 3 were waited for; matrix products, arithmetic and copies ran while one was open for 0% of the time, Pallas kernels for 35%

profile of v6, /device:TPU:13, one launch (start us, length us, event | category | flops | bytes accessed | tf_op | source)
XLA Modules:
  0.0 55.8 jit_solution(14280630307511552454)
XLA Ops:
  0.0 3.5 %pack.1 = (f32[64,96,1,128]{3,2,1,0:T(1,128)S(1)}, f32[4,96,1,128]{3,2,1,0:T(1,128)S(1)}, f32[4,96,1,128]{3,2,1,0:T(1,128)S(1)}, f32[4,64,1,128]{3,2,1,0:T(1,128...) custom-call(f32[4,64,96,1,128]{4,3,2,1,0:T(1,128)} %bitcast.14), custom_call_target="tpu_custom_call" | custom-call | tf_op jit(solution)/shard_map/pack/pallas_call | solution.py:336
  3.5 0.7 %collective-permute-start = (f32[64,96,128]{2,1,0:T(8,128)S(1)}, f32[64,96,128]{2,1,0:T(8,128)S(1)}, u32[]{:S(2)}, u32[]{:S(2)}) collective-permute-start(f32[64,96,128]{2,1,0:T(8,128)S(1)} %bitcast.8), channel_id=1, source_target_pairs={{0,16},{16,0},{1,17},{17,1},{2,18},{18,2},{3,19},{19,3},{4,20},{20... | collective-permute-start | bytes 9437192 | tf_op jit(solution)/shard_map/swap_rows_0/ppermute | solution.py:27
  4.2 1.2 %collective-permute-start.1 = (f32[4,96,128]{2,1,0:T(8,128)S(1)}, f32[4,96,128]{2,1,0:T(8,128)S(1)}, u32[]{:S(2)}, u32[]{:S(2)}) collective-permute-start(f32[4,96,128]{2,1,0:T(8,128)S(1)} %bitcast.11), channel_id=1, source_target_pairs={{0,4},{8,12},{4,0},{12,8},{1,5},{9,13},{5,1},{13,9},{2,6},{10,14},... | collective-permute-start | bytes 589832 | tf_op jit(solution)/shard_map/swap_cols_0/ppermute | solution.py:27
  5.4 2.4 %collective-permute-start.2 = (f32[4,96,128]{2,1,0:T(8,128)S(1)}, f32[4,96,128]{2,1,0:T(8,128)S(1)}, u32[]{:S(2)}, u32[]{:S(2)}) collective-permute-start(f32[4,96,128]{2,1,0:T(8,128)S(1)} %bitcast.10), channel_id=1, source_target_pairs={{4,8},{8,4},{5,9},{9,5},{6,10},{10,6},{7,11},{11,7},{20,24},{24,20... | collective-permute-start | bytes 589832 | tf_op jit(solution)/shard_map/swap_cols_1/ppermute | solution.py:27
  7.8 0.1 collective-permute-start.3
  7.9 4.5 %collective-permute-start.4 = (f32[4,64,128]{2,1,0:T(8,128)S(1)}, f32[4,64,128]{2,1,0:T(8,128)S(1)}, u32[]{:S(2)}, u32[]{:S(2)}) collective-permute-start(f32[4,64,128]{2,1,0:T(8,128)S(1)} %bitcast.12), channel_id=1, source_target_pairs={{1,2},{2,1},{5,6},{6,5},{9,10},{10,9},{13,14},{14,13},{17,18},{18,... | collective-permute-start | bytes 393224 | tf_op jit(solution)/shard_map/swap_slabs_1/ppermute | solution.py:27
  12.3 0.0 collective-permute-done.refs_2_
  12.4 4.8 %bulk0.1 = (f32[6240,128]{1,0:T(8,128)S(1)}, f32[6240,128]{1,0:T(8,128)S(1)}, f32[6240,128]{1,0:T(8,128)S(1)}, f32[6240,128]{1,0:T(8,128)S(1)}, f32[3,64,96,128]{3,2,1,0:T(8,128)S(1)}) custom-call(f32[4,64,96,128]{3,2,1,0:T(8,128)} %refs_0_.1, f32[64,96,128]{2,1,0:T(8,128)S(1)} %bitcast.9, ...), custom_call_target="tpu_custom_call", output_to_operand_aliasing={{4}: (4, {})} | custom-call | tf_op jit(solution)/shard_map/bulk0/pallas_call | solution.py:336
  17.2 0.0 collective-permute-done.3.refs_6_
  17.2 0.0 collective-permute-done.4.refs_7_
  17.3 0.1 patch0.1
  17.4 1.3 %collective-permute-start.5 = (f32[6240,128]{1,0:T(8,128)S(1)}, f32[6240,128]{1,0:T(8,128)S(1)}, u32[]{:S(2)}, u32[]{:S(2)}) collective-permute-start(f32[6240,128]{1,0:T(8,128)S(1)} %get-tuple-element.66.refs_3_), channel_id=1, source_target_pairs={{0,16},{16,0},{1,17},{17,1},{2,18},{18,2},{3,19},{19,3},{4,20},{20... | collective-permute-start | bytes 9584648 | tf_op jit(solution)/shard_map/swap_rows_0/ppermute | solution.py:27
  18.7 3.9 %collective-permute-start.7 = (f32[4,96,128]{2,1,0:T(8,128)S(1)}, f32[4,96,128]{2,1,0:T(8,128)S(1)}, u32[]{:S(2)}, u32[]{:S(2)}) collective-permute-start(f32[4,96,128]{2,1,0:T(8,128)S(1)} %get-tuple-element.72), channel_id=1, source_target_pairs={{4,8},{8,4},{5,9},{9,5},{6,10},{10,6},{7,11},{11,7},{20,24},{24,20... | collective-permute-start | bytes 589832 | tf_op jit(solution)/shard_map/swap_cols_1/ppermute | solution.py:27
  22.6 0.1 collective-permute-start.8
  22.7 1.9 %collective-permute-start.9 = (f32[4,64,128]{2,1,0:T(8,128)S(1)}, f32[4,64,128]{2,1,0:T(8,128)S(1)}, u32[]{:S(2)}, u32[]{:S(2)}) collective-permute-start(f32[4,64,128]{2,1,0:T(8,128)S(1)} %get-tuple-element.74), channel_id=1, source_target_pairs={{1,2},{2,1},{5,6},{6,5},{9,10},{10,9},{13,14},{14,13},{17,18},{18,... | collective-permute-start | bytes 393224 | tf_op jit(solution)/shard_map/swap_slabs_1/ppermute | solution.py:27
  24.6 4.5 %bulk1.1 = (f32[6240,128]{1,0:T(8,128)S(1)}, f32[6240,128]{1,0:T(8,128)S(1)}, f32[6240,128]{1,0:T(8,128)S(1)}, f32[6240,128]{1,0:T(8,128)S(1)}) custom-call(f32[6240,128]{1,0:T(8,128)S(1)} %get-tuple-element.63.refs_0_, f32[6240,128]{1,0:T(8,128)S(1)} %get-tuple-element.64.refs_1_, f32[6240,128]{1,0:T(8,128)S(1)} %get-tuple-element.65.refs_2_, ...), custom_call_target="tpu_custom_call" | custom-call | tf_op jit(solution)/shard_map/bulk1/pallas_call | solution.py:336
  29.1 0.1 collective-permute-done.9.refs_7_
  29.3 0.9 %collective-permute-done.7.refs_5_ = f32[4,96,128]{2,1,0:T(8,128)S(1)} collective-permute-done((f32[4,96,128]{2,1,0:T(8,128)S(1)}, f32[4,96,128]{2,1,0:T(8,128)S(1)}, u32[]{:S(2)}, u32[]{:S(2)}) %collective-permute-start.7) | collective-permute-done | bytes 196640 | tf_op jit(solution)/shard_map/swap_cols_1/ppermute | solution.py:27
  30.1 0.1 patch1.1
  30.2 0.7 %collective-permute-start.10 = (f32[6240,128]{1,0:T(8,128)S(1)}, f32[6240,128]{1,0:T(8,128)S(1)}, u32[]{:S(2)}, u32[]{:S(2)}) collective-permute-start(f32[6240,128]{1,0:T(8,128)S(1)} %get-tuple-element.78.refs_3_), channel_id=1, source_target_pairs={{0,16},{16,0},{1,17},{17,1},{2,18},{18,2},{3,19},{19,3},{4,20},{20... | collective-permute-start | bytes 9584648 | tf_op jit(solution)/shard_map/swap_rows_0/ppermute | solution.py:27
  30.9 2.2 %collective-permute-start.12 = (f32[4,96,128]{2,1,0:T(8,128)S(1)}, f32[4,96,128]{2,1,0:T(8,128)S(1)}, u32[]{:S(2)}, u32[]{:S(2)}) collective-permute-start(f32[4,96,128]{2,1,0:T(8,128)S(1)} %get-tuple-element.84), channel_id=1, source_target_pairs={{4,8},{8,4},{5,9},{9,5},{6,10},{10,6},{7,11},{11,7},{20,24},{24,20... | collective-permute-start | bytes 589832 | tf_op jit(solution)/shard_map/swap_cols_1/ppermute | solution.py:27
  33.2 0.1 collective-permute-start.13
  33.3 2.5 %collective-permute-start.14 = (f32[4,64,128]{2,1,0:T(8,128)S(1)}, f32[4,64,128]{2,1,0:T(8,128)S(1)}, u32[]{:S(2)}, u32[]{:S(2)}) collective-permute-start(f32[4,64,128]{2,1,0:T(8,128)S(1)} %get-tuple-element.86), channel_id=1, source_target_pairs={{1,2},{2,1},{5,6},{6,5},{9,10},{10,9},{13,14},{14,13},{17,18},{18,... | collective-permute-start | bytes 393224 | tf_op jit(solution)/shard_map/swap_slabs_1/ppermute | solution.py:27
  35.7 0.6 %collective-permute-done.10.refs_4_ = f32[6240,128]{1,0:T(8,128)S(1)} collective-permute-done((f32[6240,128]{1,0:T(8,128)S(1)}, f32[6240,128]{1,0:T(8,128)S(1)}, u32[]{:S(2)}, u32[]{:S(2)}) %collective-permute-start.10) | collective-permute-done | bytes 3194912 | tf_op jit(solution)/shard_map/swap_rows_0/ppermute | solution.py:27
  36.3 4.5 %bulk2.1 = (f32[6240,128]{1,0:T(8,128)S(1)}, f32[6240,128]{1,0:T(8,128)S(1)}, f32[6240,128]{1,0:T(8,128)S(1)}, f32[6240,128]{1,0:T(8,128)S(1)}) custom-call(f32[6240,128]{1,0:T(8,128)S(1)} %get-tuple-element.75.refs_0_, f32[6240,128]{1,0:T(8,128)S(1)} %get-tuple-element.76.refs_1_, f32[6240,128]{1,0:T(8,128)S(1)} %get-tuple-element.77.refs_2_, ...), custom_call_target="tpu_custom_call" | custom-call | tf_op jit(solution)/shard_map/bulk2/pallas_call | solution.py:336
  40.8 0.1 patch2.1
  41.0 0.5 collective-permute-start.15
  41.5 3.9 %collective-permute-start.17 = (f32[4,96,128]{2,1,0:T(8,128)S(1)}, f32[4,96,128]{2,1,0:T(8,128)S(1)}, u32[]{:S(2)}, u32[]{:S(2)}) collective-permute-start(f32[4,96,128]{2,1,0:T(8,128)S(1)} %get-tuple-element.97), channel_id=1, source_target_pairs={{4,8},{8,4},{5,9},{9,5},{6,10},{10,6},{7,11},{11,7},{20,24},{24,20... | collective-permute-start | bytes 589832 | tf_op jit(solution)/shard_map/swap_cols_1/ppermute | solution.py:27
  45.5 0.1 collective-permute-start.18
  45.5 2.5 %collective-permute-start.19 = (f32[4,64,128]{2,1,0:T(8,128)S(1)}, f32[4,64,128]{2,1,0:T(8,128)S(1)}, u32[]{:S(2)}, u32[]{:S(2)}) collective-permute-start(f32[4,64,128]{2,1,0:T(8,128)S(1)} %get-tuple-element.99), channel_id=1, source_target_pairs={{1,2},{2,1},{5,6},{6,5},{9,10},{10,9},{13,14},{14,13},{17,18},{18,... | collective-permute-start | bytes 393224 | tf_op jit(solution)/shard_map/swap_slabs_1/ppermute | solution.py:27
  48.0 5.8 %bulk_last.1 = (f32[4,64,96,128]{3,2,1,0:T(8,128)}, f32[64,104,128]{2,1,0:T(8,128)S(1)}, f32[64,104,128]{2,1,0:T(8,128)S(1)}, f32[64,104,128]{2,1,0:T(8,128)S(1)}, f32[64,104,128]{2,1,0:T(8,128)S(1)}) custom-call(f32[6240,128]{1,0:T(8,128)S(1)} %get-tuple-element.87.refs_0_, f32[6240,128]{1,0:T(8,128)S(1)} %get-tuple-element.88.refs_1_, ...), custom_call_target="tpu_custom_call" | custom-call | tf_op jit(solution)/shard_map/bulk_last/pallas_call | solution.py:336
  53.9 1.9 %patch_last.1 = (f32[4,64,96,128]{3,2,1,0:T(8,128)}, f32[64,104,128]{2,1,0:T(8,128)S(1)}, f32[64,104,128]{2,1,0:T(8,128)S(1)}, f32[64,104,128]{2,1,0:T(8,128)S(1)}, f32[64,104,128]{2,1,0:T(8,128)S(1)}) custom-call(f32[4,64,96,128]{3,2,1,0:T(8,128)} %get-tuple-element.91.refs_0_, ...), custom_call_target="tpu_custom_call", output_to_operand_aliasing={{0}: (0, {}), {1}: (1, {}), {2}: (2, {}), {3}: (3, {}), {4}... | custom-call | tf_op jit(solution)/shard_map/patch_last/pallas_call | solution.py:336
  (19 shorter events, 0.0 us)
Async XLA Ops:
  0.0 12.4 %copy-start = (f32[4,64,96,128]{3,2,1,0:T(8,128)S(1)}, f32[4,64,96,128]{3,2,1,0:T(8,128)}, u32[]{:S(2)}) copy-start(f32[4,64,96,128]{3,2,1,0:T(8,128)} %refs_5_.5) | copy-start | bytes 37748740
  3.5 8.9 %collective-permute-start = (f32[64,96,128]{2,1,0:T(8,128)S(1)}, f32[64,96,128]{2,1,0:T(8,128)S(1)}, u32[]{:S(2)}, u32[]{:S(2)}) collective-permute-start(f32[64,96,128]{2,1,0:T(8,128)S(1)} %bitcast.8), channel_id=1, source_target_pairs={{0,16},{16,0},{1,17},{17,1},{2,18},{18,2},{3,19},{19,3},{4,20},{20... | collective-permute-start | bytes 9437192 | tf_op jit(solution)/shard_map/swap_rows_0/ppermute | solution.py:27
  4.2 13.0 %collective-permute-start.1 = (f32[4,96,128]{2,1,0:T(8,128)S(1)}, f32[4,96,128]{2,1,0:T(8,128)S(1)}, u32[]{:S(2)}, u32[]{:S(2)}) collective-permute-start(f32[4,96,128]{2,1,0:T(8,128)S(1)} %bitcast.11), channel_id=1, source_target_pairs={{0,4},{8,12},{4,0},{12,8},{1,5},{9,13},{5,1},{13,9},{2,6},{10,14},... | collective-permute-start | bytes 589832 | tf_op jit(solution)/shard_map/swap_cols_0/ppermute | solution.py:27
  5.4 11.8 %collective-permute-start.2 = (f32[4,96,128]{2,1,0:T(8,128)S(1)}, f32[4,96,128]{2,1,0:T(8,128)S(1)}, u32[]{:S(2)}, u32[]{:S(2)}) collective-permute-start(f32[4,96,128]{2,1,0:T(8,128)S(1)} %bitcast.10), channel_id=1, source_target_pairs={{4,8},{8,4},{5,9},{9,5},{6,10},{10,6},{7,11},{11,7},{20,24},{24,20... | collective-permute-start | bytes 589832 | tf_op jit(solution)/shard_map/swap_cols_1/ppermute | solution.py:27
  7.8 9.4 %collective-permute-start.3 = (f32[4,64,128]{2,1,0:T(8,128)S(1)}, f32[4,64,128]{2,1,0:T(8,128)S(1)}, u32[]{:S(2)}, u32[]{:S(2)}) collective-permute-start(f32[4,64,128]{2,1,0:T(8,128)S(1)} %bitcast.13), channel_id=1, source_target_pairs={{0,1},{2,3},{1,0},{3,2},{4,5},{6,7},{5,4},{7,6},{8,9},{10,11},{9,8... | collective-permute-start | bytes 393224 | tf_op jit(solution)/shard_map/swap_slabs_0/ppermute | solution.py:27
  7.9 9.4 %collective-permute-start.4 = (f32[4,64,128]{2,1,0:T(8,128)S(1)}, f32[4,64,128]{2,1,0:T(8,128)S(1)}, u32[]{:S(2)}, u32[]{:S(2)}) collective-permute-start(f32[4,64,128]{2,1,0:T(8,128)S(1)} %bitcast.12), channel_id=1, source_target_pairs={{1,2},{2,1},{5,6},{6,5},{9,10},{10,9},{13,14},{14,13},{17,18},{18,... | collective-permute-start | bytes 393224 | tf_op jit(solution)/shard_map/swap_slabs_1/ppermute | solution.py:27
  17.4 7.2 %collective-permute-start.5 = (f32[6240,128]{1,0:T(8,128)S(1)}, f32[6240,128]{1,0:T(8,128)S(1)}, u32[]{:S(2)}, u32[]{:S(2)}) collective-permute-start(f32[6240,128]{1,0:T(8,128)S(1)} %get-tuple-element.66.refs_3_), channel_id=1, source_target_pairs={{0,16},{16,0},{1,17},{17,1},{2,18},{18,2},{3,19},{19,3},{4,20},{20... | collective-permute-start | bytes 9584648 | tf_op jit(solution)/shard_map/swap_rows_0/ppermute | solution.py:27
  18.7 10.6 %collective-permute-start.6 = (f32[4,96,128]{2,1,0:T(8,128)S(1)}, f32[4,96,128]{2,1,0:T(8,128)S(1)}, u32[]{:S(2)}, u32[]{:S(2)}) collective-permute-start(f32[4,96,128]{2,1,0:T(8,128)S(1)} %get-tuple-element.71), channel_id=1, source_target_pairs={{0,4},{8,12},{4,0},{12,8},{1,5},{9,13},{5,1},{13,9},{2,6},{10,14},... | collective-permute-start | bytes 589832 | tf_op jit(solution)/shard_map/swap_cols_0/ppermute | solution.py:27
  18.7 11.4 %collective-permute-start.7 = (f32[4,96,128]{2,1,0:T(8,128)S(1)}, f32[4,96,128]{2,1,0:T(8,128)S(1)}, u32[]{:S(2)}, u32[]{:S(2)}) collective-permute-start(f32[4,96,128]{2,1,0:T(8,128)S(1)} %get-tuple-element.72), channel_id=1, source_target_pairs={{4,8},{8,4},{5,9},{9,5},{6,10},{10,6},{7,11},{11,7},{20,24},{24,20... | collective-permute-start | bytes 589832 | tf_op jit(solution)/shard_map/swap_cols_1/ppermute | solution.py:27
  22.6 6.5 %collective-permute-start.8 = (f32[4,64,128]{2,1,0:T(8,128)S(1)}, f32[4,64,128]{2,1,0:T(8,128)S(1)}, u32[]{:S(2)}, u32[]{:S(2)}) collective-permute-start(f32[4,64,128]{2,1,0:T(8,128)S(1)} %get-tuple-element.73), channel_id=1, source_target_pairs={{0,1},{2,3},{1,0},{3,2},{4,5},{6,7},{5,4},{7,6},{8,9},{10,11},{9,8... | collective-permute-start | bytes 393224 | tf_op jit(solution)/shard_map/swap_slabs_0/ppermute | solution.py:27
  22.7 6.6 %collective-permute-start.9 = (f32[4,64,128]{2,1,0:T(8,128)S(1)}, f32[4,64,128]{2,1,0:T(8,128)S(1)}, u32[]{:S(2)}, u32[]{:S(2)}) collective-permute-start(f32[4,64,128]{2,1,0:T(8,128)S(1)} %get-tuple-element.74), channel_id=1, source_target_pairs={{1,2},{2,1},{5,6},{6,5},{9,10},{10,9},{13,14},{14,13},{17,18},{18,... | collective-permute-start | bytes 393224 | tf_op jit(solution)/shard_map/swap_slabs_1/ppermute | solution.py:27
  30.2 6.1 %collective-permute-start.10 = (f32[6240,128]{1,0:T(8,128)S(1)}, f32[6240,128]{1,0:T(8,128)S(1)}, u32[]{:S(2)}, u32[]{:S(2)}) collective-permute-start(f32[6240,128]{1,0:T(8,128)S(1)} %get-tuple-element.78.refs_3_), channel_id=1, source_target_pairs={{0,16},{16,0},{1,17},{17,1},{2,18},{18,2},{3,19},{19,3},{4,20},{20... | collective-permute-start | bytes 9584648 | tf_op jit(solution)/shard_map/swap_rows_0/ppermute | solution.py:27
  30.9 9.9 %collective-permute-start.11 = (f32[4,96,128]{2,1,0:T(8,128)S(1)}, f32[4,96,128]{2,1,0:T(8,128)S(1)}, u32[]{:S(2)}, u32[]{:S(2)}) collective-permute-start(f32[4,96,128]{2,1,0:T(8,128)S(1)} %get-tuple-element.83), channel_id=1, source_target_pairs={{0,4},{8,12},{4,0},{12,8},{1,5},{9,13},{5,1},{13,9},{2,6},{10,14},... | collective-permute-start | bytes 589832 | tf_op jit(solution)/shard_map/swap_cols_0/ppermute | solution.py:27
  30.9 9.9 %collective-permute-start.12 = (f32[4,96,128]{2,1,0:T(8,128)S(1)}, f32[4,96,128]{2,1,0:T(8,128)S(1)}, u32[]{:S(2)}, u32[]{:S(2)}) collective-permute-start(f32[4,96,128]{2,1,0:T(8,128)S(1)} %get-tuple-element.84), channel_id=1, source_target_pairs={{4,8},{8,4},{5,9},{9,5},{6,10},{10,6},{7,11},{11,7},{20,24},{24,20... | collective-permute-start | bytes 589832 | tf_op jit(solution)/shard_map/swap_cols_1/ppermute | solution.py:27
  33.2 7.6 %collective-permute-start.13 = (f32[4,64,128]{2,1,0:T(8,128)S(1)}, f32[4,64,128]{2,1,0:T(8,128)S(1)}, u32[]{:S(2)}, u32[]{:S(2)}) collective-permute-start(f32[4,64,128]{2,1,0:T(8,128)S(1)} %get-tuple-element.85), channel_id=1, source_target_pairs={{0,1},{2,3},{1,0},{3,2},{4,5},{6,7},{5,4},{7,6},{8,9},{10,11},{9,8... | collective-permute-start | bytes 393224 | tf_op jit(solution)/shard_map/swap_slabs_0/ppermute | solution.py:27
  33.3 7.6 %collective-permute-start.14 = (f32[4,64,128]{2,1,0:T(8,128)S(1)}, f32[4,64,128]{2,1,0:T(8,128)S(1)}, u32[]{:S(2)}, u32[]{:S(2)}) collective-permute-start(f32[4,64,128]{2,1,0:T(8,128)S(1)} %get-tuple-element.86), channel_id=1, source_target_pairs={{1,2},{2,1},{5,6},{6,5},{9,10},{10,9},{13,14},{14,13},{17,18},{18,... | collective-permute-start | bytes 393224 | tf_op jit(solution)/shard_map/swap_slabs_1/ppermute | solution.py:27
  41.0 7.0 %collective-permute-start.15 = (f32[6240,128]{1,0:T(8,128)S(1)}, f32[6240,128]{1,0:T(8,128)S(1)}, u32[]{:S(2)}, u32[]{:S(2)}) collective-permute-start(f32[6240,128]{1,0:T(8,128)S(1)} %get-tuple-element.90.refs_3_), channel_id=1, source_target_pairs={{0,16},{16,0},{1,17},{17,1},{2,18},{18,2},{3,19},{19,3},{4,20},{20... | collective-permute-start | bytes 9584648 | tf_op jit(solution)/shard_map/swap_rows_0/ppermute | solution.py:27
  41.5 12.3 %collective-permute-start.16 = (f32[4,96,128]{2,1,0:T(8,128)S(1)}, f32[4,96,128]{2,1,0:T(8,128)S(1)}, u32[]{:S(2)}, u32[]{:S(2)}) collective-permute-start(f32[4,96,128]{2,1,0:T(8,128)S(1)} %get-tuple-element.96), channel_id=1, source_target_pairs={{0,4},{8,12},{4,0},{12,8},{1,5},{9,13},{5,1},{13,9},{2,6},{10,14},... | collective-permute-start | bytes 589832 | tf_op jit(solution)/shard_map/swap_cols_0/ppermute | solution.py:27
  41.5 12.3 %collective-permute-start.17 = (f32[4,96,128]{2,1,0:T(8,128)S(1)}, f32[4,96,128]{2,1,0:T(8,128)S(1)}, u32[]{:S(2)}, u32[]{:S(2)}) collective-permute-start(f32[4,96,128]{2,1,0:T(8,128)S(1)} %get-tuple-element.97), channel_id=1, source_target_pairs={{4,8},{8,4},{5,9},{9,5},{6,10},{10,6},{7,11},{11,7},{20,24},{24,20... | collective-permute-start | bytes 589832 | tf_op jit(solution)/shard_map/swap_cols_1/ppermute | solution.py:27
  45.5 8.4 %collective-permute-start.18 = (f32[4,64,128]{2,1,0:T(8,128)S(1)}, f32[4,64,128]{2,1,0:T(8,128)S(1)}, u32[]{:S(2)}, u32[]{:S(2)}) collective-permute-start(f32[4,64,128]{2,1,0:T(8,128)S(1)} %get-tuple-element.98), channel_id=1, source_target_pairs={{0,1},{2,3},{1,0},{3,2},{4,5},{6,7},{5,4},{7,6},{8,9},{10,11},{9,8... | collective-permute-start | bytes 393224 | tf_op jit(solution)/shard_map/swap_slabs_0/ppermute | solution.py:27
  45.5 8.3 %collective-permute-start.19 = (f32[4,64,128]{2,1,0:T(8,128)S(1)}, f32[4,64,128]{2,1,0:T(8,128)S(1)}, u32[]{:S(2)}, u32[]{:S(2)}) collective-permute-start(f32[4,64,128]{2,1,0:T(8,128)S(1)} %get-tuple-element.99), channel_id=1, source_target_pairs={{1,2},{2,1},{5,6},{6,5},{9,10},{10,9},{13,14},{14,13},{17,18},{18,... | collective-permute-start | bytes 393224 | tf_op jit(solution)/shard_map/swap_slabs_1/ppermute | solution.py:27
